TPU v7x, 32 devices: a whole 2x2x4 slice. The times are simulated.
32 devices in a mesh: terms: 32 (over z, y, x, core).
Axes of the slice: x: 2, y: 2, z: 4, core: 2. Of those that a mesh axis runs over, the one named last changes fastest.
Arguments:
- wavefunction: float32 [512, 16, 512], replicated
- left_env: bfloat16 [64, 512, 512], P('terms')
- pair_ops: bfloat16 [64, 16, 16], P('terms')
- right_env: bfloat16 [64, 512, 512], P('terms')
- full_term: int32 [64], P('terms')
Outputs:
- output 1: float32 [7, 512, 16, 512], P(None, 'terms')
- output 2: float32 [6], replicated
- output 3: float32 [6], replicated
All inputs are finite; a program needn't handle non-finite values.
Results may differ from a plain program's by a relative error of at most 0.0131262.
Values are sent between devices in bfloat16 or wider.
A program may use at most 1 GiB of HBM per device.

v0:
```python
import jax
import jax.numpy as jnp
from jax import lax
from jax.sharding import PartitionSpec as P

LANCZOS_STEPS = 6
AXIS_NAME = 'terms'


def local_sigma(vec_bf, left_loc, pair_loc, right_loc, flag_loc):
    def apply_right(right_env):
        return lax.dot_general(vec_bf, right_env, (((2,), (1,)), ((), ())), preferred_element_type=jnp.float32).astype(jnp.bfloat16)

    def keep_vector(right_env):
        return vec_bf

    def term_body(term_idx, running_sum):
        right_done = lax.cond(flag_loc[term_idx] == 1, apply_right, keep_vector, right_loc[term_idx])
        pair_done = lax.dot_general(pair_loc[term_idx], right_done, (((1,), (1,)), ((), ())), preferred_element_type=jnp.float32).astype(jnp.bfloat16)
        return running_sum + lax.dot_general(left_loc[term_idx], pair_done, (((1,), (1,)), ((), ())), preferred_element_type=jnp.float32)

    start_sum = jnp.zeros(vec_bf.shape, jnp.float32)
    return lax.fori_loop(0, left_loc.shape[0], term_body, start_sum)


def solution(mesh):
    group_size = mesh.shape[AXIS_NAME]

    def device_body(wavefunction, left_loc, pair_loc, right_loc, flag_loc):
        bond_dim = wavefunction.shape[0]
        vec_size = wavefunction.size
        slab_rows = bond_dim // group_size
        row_start = lax.axis_index(AXIS_NAME) * slab_rows
        first_vec = wavefunction / jnp.sqrt(jnp.sum(wavefunction * wavefunction) / vec_size)
        whole_bf = first_vec.astype(jnp.bfloat16)
        current = lax.dynamic_slice_in_dim(first_vec, row_start, slab_rows, axis=0)
        previous = jnp.zeros_like(current)
        beta_prev = jnp.zeros((), jnp.float32)
        slab_list = [current]
        alpha_list = []
        beta_list = []
        for step_num in range(LANCZOS_STEPS):
            part_sigma = local_sigma(whole_bf, left_loc, pair_loc, right_loc, flag_loc)
            sigma_slab = lax.psum_scatter(part_sigma, AXIS_NAME, scatter_dimension=0, tiled=True)
            alpha_now = lax.psum(jnp.sum(sigma_slab * current), AXIS_NAME) / vec_size
            residual = sigma_slab - alpha_now * current - beta_prev * previous
            beta_now = jnp.sqrt(lax.psum(jnp.sum(residual * residual), AXIS_NAME) / vec_size)
            following = residual / beta_now
            slab_list.append(following)
            alpha_list.append(alpha_now)
            beta_list.append(beta_now)
            if step_num + 1 < LANCZOS_STEPS:
                whole_bf = lax.all_gather(following.astype(jnp.bfloat16), AXIS_NAME, axis=0, tiled=True)
            previous, current, beta_prev = current, following, beta_now
        return jnp.stack(slab_list), jnp.stack(alpha_list), jnp.stack(beta_list)

    return jax.shard_map(device_body, mesh=mesh, in_specs=(P(), P(AXIS_NAME), P(AXIS_NAME), P(AXIS_NAME), P(AXIS_NAME)), out_specs=(P(None, AXIS_NAME), P(), P()), check_vma=False)
```

profile of v0, /device:TPU:15, one launch (start us, length us, event | category | flops | bytes accessed | tf_op | source)
XLA Modules:
  0.0 2998.9 jit_solution(4862597470212187909)
XLA Ops:
  18.6 15.9 fusion.65
  46.0 128.5 %while.84 = (s32[]{:T(128)}, f32[512,16,512]{2,0,1:T(8,128)}, bf16[2,512,512]{2,1,0:T(8,128)(2,1)S(1)}, bf16[2,16,16]{2,1,0:T(8,128)(2,1)S(1)}, s32[2]{0:T(128)S...) while((s32[]{:T(128)}, f32[512,16,512]{2,0,1:T(8,128)}, ...), condition=%wide.region_4.0_spmd.clone, body=%wide.region_1.0_spmd.clone.sunk | while | flops 8740929536 | bytes 93327544 | solution.py:23
  47.7 25.1 conditional.18
  57.9 14.9 copy.75
  81.7 27.5 select_add_fusion.12
  110.4 25.1 conditional.18
  120.6 14.9 copy.75
  144.4 29.9 select_add_fusion.12
  174.5 17.7 copy.63
  192.3 183.7 %reduce-scatter.7.cloned.1.call-done = f32[16,16,512]{2,1,0:T(8,128)} async-done(((f32[512,16,512]{2,1,0:T(8,128)}), f32[16,16,512]{2,1,0:T(8,128)}) %reduce-scatter.7.cloned.1.call-update) | async-done | bytes 524304 | tf_op jit(solution)/shard_map/reduce_scatter | solution.py:44
  377.9 40.7 %psum.84 = f32[]{:T(128)} all-reduce(f32[]{:T(128)} %multiply_reduce_fusion.12), channel_id=1, replica_groups=mesh['terms'=32] {'terms'}, use_global_device_ids=true, to_apply=%region_7.0 | all-reduce | flops 1 | bytes 8 | tf_op jit(solution)/shard_map/psum | solution.py:45
  421.3 40.3 %psum.85 = f32[]{:T(128)} all-reduce(f32[]{:T(128)} %multiply_reduce_fusion.11), channel_id=1, replica_groups=mesh['terms'=32] {'terms'}, use_global_device_ids=true, to_apply=%region_9.0 | all-reduce | flops 1 | bytes 8 | tf_op jit(solution)/shard_map/psum | solution.py:47
  464.5 78.1 %all-gather.6.cloned.1.call-done = bf16[512,16,512]{2,1,0:T(8,128)(2,1)} async-done(((bf16[16,16,512]{2,1,0:T(8,128)(2,1)}), bf16[512,16,512]{2,1,0:T(8,128)(2,1)}) %all-gather.6.cloned.1.call-update) | async-done | bytes 8388624 | tf_op jit(solution)/shard_map/all_gather | solution.py:53
  553.9 128.4 %while.85 = (s32[]{:T(128)}, f32[512,16,512]{2,0,1:T(8,128)}, bf16[2,512,512]{2,1,0:T(8,128)(2,1)S(1)}, bf16[2,16,16]{2,1,0:T(8,128)(2,1)S(1)}, s32[2]{0:T(128)S...) while((s32[]{:T(128)}, f32[512,16,512]{2,0,1:T(8,128)}, ...), condition=%wide.region_13.0_spmd.clone, body=%wide.region_10.0_spmd.clone.sunk | while | flops 8740929536 | bytes 93327544 | solution.py:23
  555.6 25.1 conditional.19
  589.5 27.5 select_add_fusion.13
  618.3 25.1 conditional.19
  652.3 29.9 select_add_fusion.13
  682.4 18.1 copy.65
  700.5 182.1 %reduce-scatter.9.cloned.1.call-done = f32[16,16,512]{2,1,0:T(8,128)} async-done(((f32[512,16,512]{2,1,0:T(8,128)}), f32[16,16,512]{2,1,0:T(8,128)}) %reduce-scatter.9.cloned.1.call-update) | async-done | bytes 524304 | tf_op jit(solution)/shard_map/reduce_scatter | solution.py:44
  884.4 40.8 %psum.86 = f32[]{:T(128)} all-reduce(f32[]{:T(128)} %multiply_reduce_fusion.10), channel_id=1, replica_groups=mesh['terms'=32] {'terms'}, use_global_device_ids=true, to_apply=%region_16.0 | all-reduce | flops 1 | bytes 8 | tf_op jit(solution)/shard_map/psum | solution.py:45
  927.8 40.3 %psum.87 = f32[]{:T(128)} all-reduce(f32[]{:T(128)} %get-tuple-element.1283), channel_id=1, replica_groups=mesh['terms'=32] {'terms'}, use_global_device_ids=true, to_apply=%region_18.0 | all-reduce | flops 1 | bytes 8 | tf_op jit(solution)/shard_map/psum | solution.py:47
  969.6 78.1 %all-gather.8.cloned.1.call-done = bf16[512,16,512]{2,1,0:T(8,128)(2,1)} async-done(((bf16[16,16,512]{2,1,0:T(8,128)(2,1)}), bf16[512,16,512]{2,1,0:T(8,128)(2,1)}) %all-gather.8.cloned.1.call-update) | async-done | bytes 8388624 | tf_op jit(solution)/shard_map/all_gather | solution.py:53
  1059.0 128.6 %while.86 = (s32[]{:T(128)}, f32[512,16,512]{2,0,1:T(8,128)}, bf16[2,512,512]{2,1,0:T(8,128)(2,1)S(1)}, bf16[2,16,16]{2,1,0:T(8,128)(2,1)S(1)}, s32[2]{0:T(128)S...) while((s32[]{:T(128)}, f32[512,16,512]{2,0,1:T(8,128)}, ...), condition=%wide.region_22.0_spmd.clone, body=%wide.region_19.0_spmd.clone.sunk | while | flops 8740929536 | bytes 93327544 | solution.py:23
  1060.7 25.1 conditional.20
  1094.7 27.5 select_add_fusion.14
  1123.6 25.1 conditional.20
  1157.5 29.9 select_add_fusion.14
  1187.6 17.7 copy.67
  1205.4 182.1 %reduce-scatter.11.cloned.1.call-done = f32[16,16,512]{2,1,0:T(8,128)} async-done(((f32[512,16,512]{2,1,0:T(8,128)}), f32[16,16,512]{2,1,0:T(8,128)}) %reduce-scatter.11.cloned.1.call-update) | async-done | bytes 524304 | tf_op jit(solution)/shard_map/reduce_scatter | solution.py:44
  1389.3 40.8 %psum.88 = f32[]{:T(128)} all-reduce(f32[]{:T(128)} %multiply_reduce_fusion.8), channel_id=1, replica_groups=mesh['terms'=32] {'terms'}, use_global_device_ids=true, to_apply=%region_25.0 | all-reduce | flops 1 | bytes 8 | tf_op jit(solution)/shard_map/psum | solution.py:45
  1432.5 40.3 %psum.89 = f32[]{:T(128)} all-reduce(f32[]{:T(128)} %get-tuple-element.1281), channel_id=1, replica_groups=mesh['terms'=32] {'terms'}, use_global_device_ids=true, to_apply=%region_27.0 | all-reduce | flops 1 | bytes 8 | tf_op jit(solution)/shard_map/psum | solution.py:47
  1474.3 78.1 %all-gather.10.cloned.1.call-done = bf16[512,16,512]{2,1,0:T(8,128)(2,1)} async-done(((bf16[16,16,512]{2,1,0:T(8,128)(2,1)}), bf16[512,16,512]{2,1,0:T(8,128)(2,1)}) %all-gather.10.cloned.1.call-update) | async-done | bytes 8388624 | tf_op jit(solution)/shard_map/all_gather | solution.py:53
  1563.7 130.7 %while.87 = (s32[]{:T(128)}, f32[512,16,512]{2,0,1:T(8,128)}, bf16[2,512,512]{2,1,0:T(8,128)(2,1)S(1)}, bf16[2,16,16]{2,1,0:T(8,128)(2,1)S(1)}, s32[2]{0:T(128)S...) while((s32[]{:T(128)}, f32[512,16,512]{2,0,1:T(8,128)}, ...), condition=%wide.region_31.0_spmd.clone, body=%wide.region_28.0_spmd.clone.sunk | while | flops 8740929536 | bytes 93328056 | solution.py:23
  1565.3 26.3 conditional.21
  1600.4 27.5 select_add_fusion.15
  1629.1 26.3 conditional.21
  1664.3 29.9 select_add_fusion.15
  1694.4 17.7 copy.69
  1712.1 182.1 %reduce-scatter.13.cloned.1.call-done = f32[16,16,512]{2,1,0:T(8,128)} async-done(((f32[512,16,512]{2,1,0:T(8,128)}), f32[16,16,512]{2,1,0:T(8,128)}) %reduce-scatter.13.cloned.1.call-update) | async-done | bytes 524304 | tf_op jit(solution)/shard_map/reduce_scatter | solution.py:44
  1896.0 40.8 %psum.90 = f32[]{:T(128)} all-reduce(f32[]{:T(128)} %multiply_reduce_fusion.6), channel_id=1, replica_groups=mesh['terms'=32] {'terms'}, use_global_device_ids=true, to_apply=%region_34.0 | all-reduce | flops 1 | bytes 8 | tf_op jit(solution)/shard_map/psum | solution.py:45
  1939.2 40.3 %psum.91 = f32[]{:T(128)} all-reduce(f32[]{:T(128)} %get-tuple-element.1279), channel_id=1, replica_groups=mesh['terms'=32] {'terms'}, use_global_device_ids=true, to_apply=%region_36.0 | all-reduce | flops 1 | bytes 8 | tf_op jit(solution)/shard_map/psum | solution.py:47
  1981.0 78.1 %all-gather.12.cloned.1.call-done = bf16[512,16,512]{2,1,0:T(8,128)(2,1)} async-done(((bf16[16,16,512]{2,1,0:T(8,128)(2,1)}), bf16[512,16,512]{2,1,0:T(8,128)(2,1)}) %all-gather.12.cloned.1.call-update) | async-done | bytes 8388624 | tf_op jit(solution)/shard_map/all_gather | solution.py:53
  2070.4 128.4 %while.88 = (s32[]{:T(128)}, f32[512,16,512]{2,0,1:T(8,128)}, bf16[2,512,512]{2,1,0:T(8,128)(2,1)S(1)}, bf16[2,16,16]{2,1,0:T(8,128)(2,1)S(1)}, s32[2]{0:T(128)S...) while((s32[]{:T(128)}, f32[512,16,512]{2,0,1:T(8,128)}, ...), condition=%wide.region_40.0_spmd.clone, body=%wide.region_37.0_spmd.clone.sunk | while | flops 8740929536 | bytes 93327544 | solution.py:23
  2072.1 25.1 conditional.22
  2106.1 27.5 select_add_fusion.16
  2134.8 25.1 conditional.22
  2145.0 14.9 copy.87
  2168.8 29.9 select_add_fusion.16
  2198.9 17.7 copy.71
  2216.7 182.1 %reduce-scatter.15.cloned.1.call-done = f32[16,16,512]{2,1,0:T(8,128)} async-done(((f32[512,16,512]{2,1,0:T(8,128)}), f32[16,16,512]{2,1,0:T(8,128)}) %reduce-scatter.15.cloned.1.call-update) | async-done | bytes 524304 | tf_op jit(solution)/shard_map/reduce_scatter | solution.py:44
  2400.5 40.8 %psum.92 = f32[]{:T(128)} all-reduce(f32[]{:T(128)} %multiply_reduce_fusion.4), channel_id=1, replica_groups=mesh['terms'=32] {'terms'}, use_global_device_ids=true, to_apply=%region_43.0 | all-reduce | flops 1 | bytes 8 | tf_op jit(solution)/shard_map/psum | solution.py:45
  2443.7 40.3 %psum.93 = f32[]{:T(128)} all-reduce(f32[]{:T(128)} %get-tuple-element.1277), channel_id=1, replica_groups=mesh['terms'=32] {'terms'}, use_global_device_ids=true, to_apply=%region_45.0 | all-reduce | flops 1 | bytes 8 | tf_op jit(solution)/shard_map/psum | solution.py:47
  2485.6 78.1 %all-gather.14.cloned.1.call-done = bf16[512,16,512]{2,1,0:T(8,128)(2,1)} async-done(((bf16[16,16,512]{2,1,0:T(8,128)(2,1)}), bf16[512,16,512]{2,1,0:T(8,128)(2,1)}) %all-gather.14.cloned.1.call-update) | async-done | bytes 8388624 | tf_op jit(solution)/shard_map/all_gather | solution.py:53
  2575.0 128.4 %while.89 = (s32[]{:T(128)}, f32[512,16,512]{2,0,1:T(8,128)}, bf16[2,512,512]{2,1,0:T(8,128)(2,1)S(1)}, bf16[2,16,16]{2,1,0:T(8,128)(2,1)S(1)}, s32[2]{0:T(128)S...) while((s32[]{:T(128)}, f32[512,16,512]{2,0,1:T(8,128)}, ...), condition=%wide.region_49.0_spmd.clone, body=%wide.region_46.0_spmd.clone.sunk | while | flops 8740929536 | bytes 93327544 | solution.py:23
  2576.6 25.1 conditional.23
  2586.8 14.9 copy.90
  2610.6 27.5 select_add_fusion.17
  2639.4 25.1 conditional.23
  2673.4 29.9 select_add_fusion.17
  2703.4 17.7 copy.73
  2726.7 176.6 %reduce-scatter.17.cloned.1.call-done = f32[16,16,512]{2,1,0:T(8,128)} async-done(((f32[512,16,512]{2,1,0:T(8,128)}), f32[16,16,512]{2,1,0:T(8,128)}) %reduce-scatter.17.cloned.1.call-update) | async-done | bytes 524304 | tf_op jit(solution)/shard_map/reduce_scatter | solution.py:44
  2905.9 40.8 %psum.94 = f32[]{:T(128)} all-reduce(f32[]{:T(128)} %multiply_reduce_fusion.2), channel_id=1, replica_groups=mesh['terms'=32] {'terms'}, use_global_device_ids=true, to_apply=%region_52.0 | all-reduce | flops 1 | bytes 8 | tf_op jit(solution)/shard_map/psum | solution.py:45
  2949.2 40.3 %psum.95 = f32[]{:T(128)} all-reduce(f32[]{:T(128)} %get-tuple-element.1275), channel_id=1, replica_groups=mesh['terms'=32] {'terms'}, use_global_device_ids=true, to_apply=%region_54.0 | all-reduce | flops 1 | bytes 8 | tf_op jit(solution)/shard_map/psum | solution.py:47
  (153 shorter events, 472.3 us)
Async XLA Ops:
  7.2 368.8 %reduce-scatter.7.cloned.1.call-start = ((), (), s32[]{:S(2)}) async-start(), calls=%async_computation.6 | async-start | bytes 17301504 | tf_op jit(solution)/shard_map/reduce_scatter | solution.py:44
  34.5 11.5 copy-start
  34.5 11.5 copy-start.17
  34.5 11.5 copy-start.18
  34.5 11.5 copy-start.23
  192.2 350.4 %all-gather.6.cloned.1.call-start = ((), (), s32[]{:S(2)}) async-start(), calls=%async_computation.7 | async-start | bytes 8650752 | tf_op jit(solution)/shard_map/all_gather | solution.py:53
  464.5 418.1 %reduce-scatter.9.cloned.1.call-start = ((), (), s32[]{:S(2)}) async-start(), calls=%async_computation.8 | async-start | bytes 17301504 | tf_op jit(solution)/shard_map/reduce_scatter | solution.py:44
  682.3 18.1 copy-start.19
  700.4 182.2 %copy-start.14 = (f32[16,16,512]{2,1,0:T(8,128)S(1)}, f32[16,16,512]{2,1,0:T(8,128)}, u32[]{:S(2)}) copy-start(f32[16,16,512]{2,1,0:T(8,128)} %get-tuple-element.1286) | copy-start | bytes 1572868
  700.5 347.2 %all-gather.8.cloned.1.call-start = ((), (), s32[]{:S(2)}) async-start(), calls=%async_computation.9 | async-start | bytes 8650752 | tf_op jit(solution)/shard_map/all_gather | solution.py:53
  927.8 131.2 %copy-start.4 = (f32[16,16,512]{2,1,0:T(8,128)}, f32[16,16,512]{2,1,0:T(8,128)S(1)}, u32[]{:S(2)}) copy-start(f32[16,16,512]{2,1,0:T(8,128)S(1)} %get-tuple-element.1284) | copy-start | bytes 1572868
  969.5 418.0 %reduce-scatter.11.cloned.1.call-start = ((), (), s32[]{:S(2)}) async-start(), calls=%async_computation.10 | async-start | bytes 17301504 | tf_op jit(solution)/shard_map/reduce_scatter | solution.py:44
  969.5 89.4 %copy-start.20 = (bf16[2,512,512]{2,1,0:T(8,128)(2,1)S(1)}, bf16[2,512,512]{2,1,0:T(8,128)(2,1)}, u32[]{:S(2)}) copy-start(bf16[2,512,512]{2,1,0:T(8,128)(2,1)} %copy-done.19) | copy-start | bytes 3145732
  1205.3 182.1 %copy-start.5 = (f32[16,16,512]{2,1,0:T(8,128)S(1)}, f32[16,16,512]{2,1,0:T(8,128)}, u32[]{:S(2)}) copy-start(f32[16,16,512]{2,1,0:T(8,128)} %copy-done.4) | copy-start | bytes 1572868
  1205.3 225.4 %copy-start.15 = (f32[16,16,512]{2,1,0:T(8,128)S(1)}, f32[16,16,512]{2,1,0:T(8,128)}, u32[]{:S(2)}) copy-start(f32[16,16,512]{2,1,0:T(8,128)} %get-tuple-element.1286) | copy-start | bytes 1572868
  1205.4 347.0 %all-gather.10.cloned.1.call-start = ((), (), s32[]{:S(2)}) async-start(), calls=%async_computation.11 | async-start | bytes 8650752 | tf_op jit(solution)/shard_map/all_gather | solution.py:53
  1432.5 131.2 %copy-start.8 = (f32[16,16,512]{2,1,0:T(8,128)}, f32[16,16,512]{2,1,0:T(8,128)S(1)}, u32[]{:S(2)}) copy-start(f32[16,16,512]{2,1,0:T(8,128)S(1)} %get-tuple-element.1282) | copy-start | bytes 1572868
  1474.2 420.0 %reduce-scatter.13.cloned.1.call-start = ((), (), s32[]{:S(2)}) async-start(), calls=%async_computation.12 | async-start | bytes 17301504 | tf_op jit(solution)/shard_map/reduce_scatter | solution.py:44
  1712.1 182.2 %copy-start.9 = (f32[16,16,512]{2,1,0:T(8,128)S(1)}, f32[16,16,512]{2,1,0:T(8,128)}, u32[]{:S(2)}) copy-start(f32[16,16,512]{2,1,0:T(8,128)} %copy-done.8) | copy-start | bytes 1572868
  1712.1 225.4 %copy-start.6 = (f32[16,16,512]{2,1,0:T(8,128)S(1)}, f32[16,16,512]{2,1,0:T(8,128)}, u32[]{:S(2)}) copy-start(f32[16,16,512]{2,1,0:T(8,128)} %copy-done.4) | copy-start | bytes 1572868
  1712.1 347.0 %all-gather.12.cloned.1.call-start = ((), (), s32[]{:S(2)}) async-start(), calls=%async_computation.13 | async-start | bytes 8650752 | tf_op jit(solution)/shard_map/all_gather | solution.py:53
  1939.2 131.2 %copy-start.1 = (f32[16,16,512]{2,1,0:T(8,128)}, f32[16,16,512]{2,1,0:T(8,128)S(1)}, u32[]{:S(2)}) copy-start(f32[16,16,512]{2,1,0:T(8,128)S(1)} %get-tuple-element.1280) | copy-start | bytes 1572868
  1981.0 417.8 %reduce-scatter.15.cloned.1.call-start = ((), (), s32[]{:S(2)}) async-start(), calls=%async_computation.14 | async-start | bytes 17301504 | tf_op jit(solution)/shard_map/reduce_scatter | solution.py:44
  1981.0 89.4 %copy-start.21 = (bf16[2,512,512]{2,1,0:T(8,128)(2,1)S(1)}, bf16[2,512,512]{2,1,0:T(8,128)(2,1)}, u32[]{:S(2)}) copy-start(bf16[2,512,512]{2,1,0:T(8,128)(2,1)} %get-tuple-element.1808) | copy-start | bytes 3145732
  2216.6 182.1 %copy-start.2 = (f32[16,16,512]{2,1,0:T(8,128)S(1)}, f32[16,16,512]{2,1,0:T(8,128)}, u32[]{:S(2)}) copy-start(f32[16,16,512]{2,1,0:T(8,128)} %copy-done.1) | copy-start | bytes 1572868
  2216.6 225.4 %copy-start.10 = (f32[16,16,512]{2,1,0:T(8,128)S(1)}, f32[16,16,512]{2,1,0:T(8,128)}, u32[]{:S(2)}) copy-start(f32[16,16,512]{2,1,0:T(8,128)} %copy-done.8) | copy-start | bytes 1572868
  2216.6 347.0 %all-gather.14.cloned.1.call-start = ((), (), s32[]{:S(2)}) async-start(), calls=%async_computation.15 | async-start | bytes 8650752 | tf_op jit(solution)/shard_map/all_gather | solution.py:53
  2443.7 131.2 %copy-start.12 = (f32[16,16,512]{2,1,0:T(8,128)}, f32[16,16,512]{2,1,0:T(8,128)S(1)}, u32[]{:S(2)}) copy-start(f32[16,16,512]{2,1,0:T(8,128)S(1)} %get-tuple-element.1278) | copy-start | bytes 1572868
  2485.5 417.8 %reduce-scatter.17.cloned.1.call-start = ((), (), s32[]{:S(2)}) async-start(), calls=%async_computation.16 | async-start | bytes 17301504 | tf_op jit(solution)/shard_map/reduce_scatter | solution.py:44
  2485.5 89.4 %copy-start.22 = (bf16[2,512,512]{2,1,0:T(8,128)(2,1)S(1)}, bf16[2,512,512]{2,1,0:T(8,128)(2,1)}, u32[]{:S(2)}) copy-start(bf16[2,512,512]{2,1,0:T(8,128)(2,1)} %get-tuple-element.1808) | copy-start | bytes 3145732
  2721.1 2.1 copy-start.16
  2721.1 2.9 copy-start.7
  2721.1 3.8 copy-start.11
  2721.1 4.7 copy-start.3
  2721.1 182.1 %copy-start.13 = (f32[16,16,512]{2,1,0:T(8,128)S(1)}, f32[16,16,512]{2,1,0:T(8,128)}, u32[]{:S(2)}) copy-start(f32[16,16,512]{2,1,0:T(8,128)} %copy-done.12) | copy-start | bytes 1572868
Sparse Core Ops, SparseCore 0:
  192.3 183.6 reduce-scatter.6
  464.6 77.9 all-gather.5
  700.6 181.9 reduce-scatter.8
  969.6 77.9 all-gather.7
  1205.5 181.9 reduce-scatter.10
  1474.4 77.9 all-gather.9
  1712.2 181.9 reduce-scatter.12
  1981.1 77.9 all-gather.11
  2216.7 181.9 reduce-scatter.14
  2485.6 77.9 all-gather.13
  2721.3 181.9 reduce-scatter.16
where the time goes:
time: 3010 us; the launch traced here: 3000 us
  waiting for transfers between devices  1480 us (49%)
  matrix products  575 us (19%)
  blocking collectives  486 us (16%)
  local copies, waits for them, and re-layouts  365 us (12%)
  other arithmetic  58.1 us (2%)
    reduce_scatter x6, waiting for transfers between devices, device_body(): lax.psum_scatter(part_sigma, AXIS_NAME, scatter_dimension=0, tiled=True)  1090 us
    all_gather x5, waiting for transfers between devices, device_body(): lax.all_gather(following.astype(jnp.bfloat16), AXIS_NAME, axis=0, tiled=T...  390 us
    dot_general x12, matrix products, term_body(): lax.dot_general(left_loc[term_idx], pair_done, (((1,), (1,)), ((), ())),...  345 us
    psum x6, blocking collectives, device_body(): alpha_now = lax.psum(jnp.sum(sigma_slab * current), AXIS_NAME) / vec_size  245 us
    psum x6, blocking collectives, device_body(): lax.psum(jnp.sum(residual * residual), AXIS_NAME) / vec_size  242 us
    cond x12, local copies, waits for them, and re-layouts, term_body(): lax.cond(flag_loc[term_idx] == 1, apply_right, keep_vector, right_loc[ter...  179 us
    dot_general x12, matrix products, apply_right(): lax.dot_general(vec_bf, right_env, (((2,), (1,)), ((), ())), preferred_el...  124 us
    dot_general x12, matrix products, term_body(): lax.dot_general(pair_loc[term_idx], right_done, (((1,), (1,)), ((), ())),...  107 us
  transfers between devices with their start and end apart: 11, of which 11 were waited for; matrix products, arithmetic and copies ran while one was open for 0% of the time, Pallas kernels for 0%

commit v1 on v0

v1 whole, which is shorter than its diff:
```python
import functools

import jax
import jax.numpy as jnp
from jax import lax
from jax.experimental import pallas as pl
from jax.experimental.pallas import tpu as pltpu
from jax.sharding import PartitionSpec as P

LANCZOS_STEPS = 6
AXIS_NAME = 'terms'
MESH = pl.DeviceIdType.MESH

CHIPS = 16
CORES = 2
DEVS = 32
CHUNKS = 2
GROUPS = 4
TILE_PARTS = 4


class Dims:
    def __init__(self, bond, pair, terms_dev):
        self.bond = bond
        self.pair = pair
        self.terms_dev = terms_dev
        self.slab = bond // CHIPS
        self.sub = self.slab // 2
        self.half = bond // CORES
        self.chunk = self.half // CHUNKS
        self.rows = self.slab * pair
        self.prod = self.sub * pair
        self.out_rows = bond // DEVS
        self.group_terms = 4 * CORES * terms_dev
        self.vec_size = bond * pair * bond
        self.lane = min(bond, 128)
        self.lane_tiles = bond // self.lane


def lanczos_kernel(d, psi, left, right, wexp, out, info, lv, rv, wv, kw, uv, ps, yst, zst, sig, part, vcur, vprev, tbuf, gbuf, scs, scr, nbuf,
                   loc_sem, psi_sem, d2d_sem, d2d_recv, rw_send, rw_recv, fw_send, fw_recv, l_send, l_recv, u_send, u_recv,
                   p_send, p_recv, s_send, s_recv, k_send, k_recv, n_send, n_recv, o_sem):
    me = lax.axis_index(AXIS_NAME)
    core = me % 2
    xpos = (me // 2) % 2
    ypos = (me // 4) % 2
    zpos = me // 8

    def device(z, y, x, c):
        return ((z * 2 + y) * 2 + x) * 2 + c

    def chip_slot(z, y, x):
        return (x * 2 + y) * 4 + z

    partner = device(zpos, ypos, xpos, 1 - core)
    slot = chip_slot(zpos, ypos, xpos)
    zs = (zpos, zpos + 1 - 2 * (zpos % 2), (zpos + 2) % 4, 3 - zpos)
    y_two = ypos + (1 - core) * (1 - 2 * ypos)
    x_two = xpos + core * (1 - 2 * xpos)
    y_three = ypos + core * (1 - 2 * ypos)
    x_three = xpos + (1 - core) * (1 - 2 * xpos)
    two = device(zpos, y_two, x_two, core)
    three = device(zpos, y_three, x_three, core)

    def remote(src, dst, send, recv, dev):
        return pltpu.make_async_remote_copy(src_ref=src, dst_ref=dst, send_sem=send, recv_sem=recv, device_id=(dev,), device_id_type=MESH)

    class Gather:
        def __init__(self, block, send, recv):
            self.block, self.send_sem, self.recv_sem = block, send, recv

        def send(self, which, dev):
            remote(self.block(which), self.block(which), self.send_sem, self.recv_sem(which), dev).start()

        def wait(self, which):
            remote(self.block(which), self.block(which), self.send_sem, self.recv_sem(which), me).wait_recv()

        def own_along(self):
            for i in (1, 2, 3):
                self.send(slot, device(zs[i], ypos, xpos, core))

        def own_across(self):
            self.send(slot, three)
            self.send(slot, two)

        def event(self, n):
            i = (n + 1) // 2
            if n % 2:
                which = chip_slot(zs[i], ypos, xpos)
                self.wait(which)
                self.send(which, three)
                self.send(which, two)
            else:
                which = chip_slot(zs[i], y_two, x_two)
                self.wait(which)
                self.send(which, three)

        def last(self, diagonal):
            for i in range(4):
                self.wait(chip_slot(zs[i], 1 - ypos, 1 - xpos) if diagonal else chip_slot(zs[i], y_three, x_three))

    l_gather = Gather(lambda s: lv.at[:, s], l_send, lambda s: l_recv.at[s])

    def u_block(ch):
        return lambda s: uv.at[ch, :, pl.ds(pl.multiple_of(s * d.slab, d.slab), d.slab), :]

    u_gather = [Gather(u_block(ch), u_send.at[ch], lambda s, ch=ch: u_recv.at[ch, s]) for ch in range(CHUNKS)]

    for ch in range(CHUNKS):
        for h in range(2):
            mine = left.at[:, pl.ds(pl.multiple_of(core * d.half + ch * d.chunk, d.chunk), d.chunk),
                           pl.ds(pl.multiple_of((core + h) % 2 * d.half, d.half), d.half)]
            theirs = left.at[:, pl.ds(pl.multiple_of((1 - core) * d.half + ch * d.chunk, d.chunk), d.chunk),
                             pl.ds(pl.multiple_of((1 - core + h) % 2 * d.half, d.half), d.half)]
            remote(theirs, lv.at[ch, slot, core, :, h], d2d_sem.at[ch, h], d2d_recv.at[ch, h], partner).start()
            pltpu.make_async_copy(mine, lv.at[ch, slot, core, :, h], loc_sem.at[ch, h]).start()

    psi_rows = d.half * d.pair // 8
    psi_copies = [pltpu.make_async_copy(psi.at[pl.ds(pl.multiple_of(core * d.half * d.pair + n * psi_rows, psi_rows), psi_rows),
                                               pl.ds(c * d.lane, d.lane)],
                                        ps.at[c, pl.ds(n * psi_rows, psi_rows), :], psi_sem.at[n, c])
                  for n in range(8) for c in range(d.lane_tiles)]
    for copy in psi_copies:
        copy.start()

    def right_rows(s):
        return right.at[:, pl.ds(pl.multiple_of(s * d.slab, d.slab), d.slab), :]

    own_right = pltpu.make_async_copy(right_rows(slot), rv.at[slot, core], loc_sem.at[2, 0])
    own_pair = pltpu.make_async_copy(wexp, wv.at[slot, core], loc_sem.at[2, 1])
    own_right.start()
    own_pair.start()
    for n in range(1, CHIPS):
        chip = (me // 2 + n) % CHIPS
        to = chip_slot(chip // 4, chip // 2 % 2, chip % 2)
        remote(right_rows(to), rv.at[slot, core], rw_send.at[0], rw_recv.at[0], chip * 2 + core).start()
        remote(wexp, wv.at[slot, core], rw_send.at[1], rw_recv.at[1], chip * 2 + core).start()

    for ch in range(CHUNKS):
        for h in range(2):
            pltpu.make_async_copy(lv.at[ch, slot, core, :, h], lv.at[ch, slot, core, :, h], loc_sem.at[ch, h]).wait()
            back = remote(lv.at[ch, slot, 1 - core, :, h], lv.at[ch, slot, 1 - core, :, h], d2d_sem.at[ch, h], d2d_recv.at[ch, h], partner)
            back.wait_recv()
    l_gather.own_along()
    l_gather.own_across()

    total = jnp.zeros((8, d.lane), jnp.float32)
    for n in range(8):
        for copy in psi_copies[n * d.lane_tiles:(n + 1) * d.lane_tiles]:
            copy.wait()

        def add_rows(i, acc, n=n):
            x = ps[:, pl.ds(pl.multiple_of(n * psi_rows + i * (psi_rows // 8), 8), psi_rows // 8), :]
            return acc + jnp.sum((x * x).reshape(d.lane_tiles * psi_rows // 64, 8, d.lane), axis=0)

        total = lax.fori_loop(0, 8, add_rows, total)
    nbuf[0] = jnp.broadcast_to(jnp.sum(total, keepdims=True), (8, 128))
    to_partner = remote(nbuf.at[0], nbuf.at[1], n_send, n_recv, partner)
    to_partner.start()
    to_partner.wait()
    norm = jnp.sqrt((nbuf[0] + nbuf[1])[0:1, :] / d.vec_size)
    info[2] = jnp.broadcast_to(norm, (8, 128))
    norm_one = norm[:, 0:1]

    def place(q):
        tiles = [(ps[c, pl.ds(q, d.half, stride=d.pair), :] / norm_one).T for c in range(d.lane_tiles)]
        xt = jnp.concatenate(tiles, axis=0)
        vprev[...] = xt
        return xt.astype(jnp.bfloat16)

    def start_vector(qb, carry):
        for q2 in range(2):
            q = qb * 2 + q2
            xb = place(q)
            for ch in range(CHUNKS):
                uv[ch, qb, :, q2 * d.chunk:(q2 + 1) * d.chunk] = xb[:, ch * d.chunk:(ch + 1) * d.chunk]
            for bh in range(2):
                rows = vprev[pl.ds(pl.multiple_of(slot * d.slab + bh * d.sub, d.sub), d.sub), :]
                vcur[pl.ds(pl.multiple_of((bh * d.pair + q) * d.sub, d.sub), d.sub), :] = rows
        return carry

    lax.fori_loop(0, d.pair // 4, start_vector, 0)
    own_right.wait()
    own_pair.wait()
    fifteen = rv.at[pl.ds(0, CHIPS - 1), 0]
    fifteen_w = wv.at[pl.ds(0, CHIPS - 1), 0]
    remote(fifteen, fifteen, rw_send.at[0], rw_recv.at[0], me).wait()
    remote(fifteen_w, fifteen_w, rw_send.at[1], rw_recv.at[1], me).wait()
    fw_right = remote(rv.at[:, core], rv.at[:, core], fw_send.at[0], fw_recv.at[0], partner)
    fw_pair = remote(wv.at[:, core], wv.at[:, core], fw_send.at[1], fw_recv.at[1], partner)
    fw_right.start()
    fw_pair.start()
    l_gather.event(0)
    l_gather.event(1)
    lax.fori_loop(d.pair // 4, d.pair // 2, start_vector, 0)
    l_gather.event(2)
    l_gather.event(3)
    fw_right.wait()
    fw_pair.wait()
    lane = lax.broadcasted_iota(jnp.int32, (d.sub, d.prod), 1)
    row = lax.broadcasted_iota(jnp.int32, (d.sub, d.prod), 0)
    diagonal = lane % d.sub == row

    def spread_pair(s, carry):
        for c in range(2):
            for t in range(d.terms_dev):
                w = wv[s, c, t].astype(jnp.float32)
                for q in range(d.pair):
                    full = jnp.where(diagonal, jnp.broadcast_to(w[q:q + 1, :], (d.sub, d.prod)), 0.0)
                    kw[s, c, t, q * d.sub:(q + 1) * d.sub, :] = full.astype(jnp.bfloat16)
        return carry

    lax.fori_loop(0, CHIPS, spread_pair, 0)
    l_gather.event(4)
    l_gather.event(5)
    l_gather.event(6)
    vprev[...] = jnp.zeros_like(vprev)

    def products(ch, grp, is_last):
        r_all = rv[pl.ds(grp * 4, 4)].reshape(d.group_terms * d.slab, d.bond)
        for qb in range(d.pair // 2):
            y = jnp.dot(r_all, uv[ch, qb], preferred_element_type=jnp.float32).astype(jnp.bfloat16)
            y = y.reshape(d.group_terms, 2, d.sub, 2 * d.chunk)
            for q2 in range(2):
                q = qb * 2 + q2
                for bh in range(2):
                    yst[:, q * d.sub:(q + 1) * d.sub, bh * d.chunk:(bh + 1) * d.chunk] = y[:, bh, :, q2 * d.chunk:(q2 + 1) * d.chunk]
        for k in range(d.group_terms):
            w = kw[grp * 4 + k // 4, k // 2 % 2, k % 2]
            z = jnp.dot(w, yst[k], preferred_element_type=jnp.float32).astype(jnp.bfloat16)
            for bh in range(2):
                zst[bh * d.prod:(bh + 1) * d.prod, k * d.chunk:(k + 1) * d.chunk] = z[:, bh * d.chunk:(bh + 1) * d.chunk]
        for h in (1, 0):
            l_all = lv[ch, pl.ds(grp * 4, 4), :, :, h].reshape(d.group_terms * d.chunk, d.half)
            sig[h] += jnp.dot(zst[...], l_all, preferred_element_type=jnp.float32)
            if h == 1:
                @pl.when(is_last)
                def _():
                    remote(sig.at[1], part, p_send, p_recv, partner).start()

    def step(j, beta_prev):
        later = jnp.minimum(j, 1)

        @pl.when(j > 0)
        def _():
            for n in range(7):
                u_gather[0].event(n)
            u_gather[1].own_across()
            for n in range(4):
                u_gather[1].event(n)
            u_gather[0].last(False)
            u_gather[0].last(True)

        sig[...] = jnp.zeros_like(sig)

        def part_step(it, carry):
            ch = (1 - later) * (it % 2) + later * (it // 4)
            n = (1 - later) * (it // 2) + later * (it % 4)
            own = xpos * 2 + ypos
            arrive = jnp.where(n == 0, own, jnp.where(n == 1, x_two * 2 + y_two, jnp.where(n == 2, x_three * 2 + y_three, 3 - own)))
            grp = (1 - later) * arrive + later * n

            @pl.when((j == 0) & (it == 4))
            def _():
                l_gather.last(False)

            @pl.when((j == 0) & (it == 6))
            def _():
                l_gather.last(True)

            for at in range(3):
                @pl.when((j > 0) & (it == at))
                def _():
                    u_gather[1].event(4 + at)

            @pl.when((j > 0) & (it == 4))
            def _():
                u_gather[1].last(False)
                u_gather[1].last(True)

            products(ch, grp, it == 7)
            return carry

        lax.fori_loop(0, 2 * GROUPS, part_step, 0)

        @pl.when(j > 0)
        def _():
            for ch in range(CHUNKS):
                sent = uv.at[ch, :, pl.ds(0, 15 * d.slab), :]
                remote(sent, sent, u_send.at[ch], u_recv.at[ch, 0], me).wait_send()

        remote(sig.at[1], part, p_send, p_recv, partner).wait()
        s = sig[0] + part[...]
        v = vcur[...]
        w = s - beta_prev * vprev[...]
        sv = jnp.sum(s * v, keepdims=True)
        wv_sum = jnp.sum(w * v, keepdims=True)
        vv = jnp.sum(v * v, keepdims=True)
        guess = jnp.where(vv > 0.0, wv_sum / jnp.where(vv > 0.0, vv, 1.0), 0.0)
        t = w - guess * v
        sig[0] = t
        tt = jnp.sum(t * t, keepdims=True)
        tv = jnp.sum(t * v, keepdims=True)
        tile_row = lax.broadcasted_iota(jnp.int32, (8, 128), 0)
        tile = jnp.zeros((8, 128), jnp.float32)
        for n, value in enumerate((sv, vv, tt, tv, guess)):
            tile = jnp.where(tile_row == n, value, tile)
        scs[...] = tile
        scr[me] = tile

        def tell(n, carry):
            remote(scs, scr.at[me], s_send, s_recv, (me + n) % DEVS).start()
            return carry

        lax.fori_loop(1, DEVS, tell, 0)
        heard = scr.at[pl.ds(0, DEVS - 1)]
        remote(heard, heard, s_send, s_recv, me).wait()
        alpha = jnp.sum(scr[:, 0, :], axis=0, keepdims=True) / d.vec_size
        off = alpha - scr[:, 4, :]
        square = scr[:, 2, :] - 2.0 * off * scr[:, 3, :] + off * off * scr[:, 1, :]
        beta = jnp.sqrt(jnp.sum(square, axis=0, keepdims=True) / d.vec_size)
        info[0, pl.ds(j, 1), :] = alpha
        info[1, pl.ds(j, 1), :] = beta
        vnew = (sig[0] - (alpha[:, 0:1] - guess) * vcur[...]) / beta[:, 0:1]
        vprev[...] = vcur[...]
        vcur[...] = vnew
        vb = vnew.astype(jnp.bfloat16)

        @pl.when(j < LANCZOS_STEPS - 1)
        def _():
            for ch in range(CHUNKS):
                for bh in range(2):
                    at = pl.ds(pl.multiple_of(slot * d.slab + bh * d.sub, d.sub), d.sub)
                    for q in range(d.pair):
                        uv[ch, q // 2, at, q % 2 * d.chunk:(q % 2 + 1) * d.chunk] = \
                            vb[(bh * d.pair + q) * d.sub:(bh * d.pair + q + 1) * d.sub, ch * d.chunk:(ch + 1) * d.chunk]
            u_gather[0].own_along()
            u_gather[0].own_across()
            u_gather[1].own_along()

        wide = TILE_PARTS * d.slab
        for n in range(d.pair // TILE_PARTS):
            rows = [vcur[(bh * d.pair + q) * d.sub:(bh * d.pair + q + 1) * d.sub, :]
                    for q in range(n * TILE_PARTS, (n + 1) * TILE_PARTS) for bh in range(2)]
            tbuf[j, :, n * wide:(n + 1) * wide] = jnp.concatenate(rows, axis=0).T

        def hand_out(n, carry):
            to = core * CHIPS + n
            block = tbuf.at[j, pl.ds(pl.multiple_of(n * d.out_rows, d.out_rows), d.out_rows), :]

            @pl.when(to != me)
            def _():
                remote(block, gbuf.at[j, slot], k_send, k_recv, to).start()

            @pl.when(to == me)
            def _():
                gbuf[j, slot] = block[...]
            return carry

        lax.fori_loop(0, CHIPS, hand_out, 0)
        return beta[:, 0:1]

    lax.fori_loop(0, LANCZOS_STEPS, step, jnp.zeros((1, 1), jnp.float32))

    fourteen = lv.at[:, pl.ds(0, 15)]
    remote(fourteen, fourteen, l_send, l_recv.at[0], me).wait_send()
    for ch in range(CHUNKS):
        for h in range(2):
            theirs = left.at[:, pl.ds(0, d.chunk), pl.ds(0, d.half)]
            remote(theirs, lv.at[ch, slot, core, :, h], d2d_sem.at[ch, h], d2d_recv.at[ch, h], partner).wait_send()

    sends_self = me // CHIPS == core

    @pl.when(sends_self)
    def _():
        some = gbuf.at[:, pl.ds(0, CHIPS - 1)]
        remote(some, some, k_send, k_recv, me).wait()

    @pl.when(jnp.logical_not(sends_self))
    def _():
        remote(gbuf, gbuf, k_send, k_recv, me).wait()

    wide = TILE_PARTS * d.slab
    lanes = lax.broadcasted_iota(jnp.int32, (d.out_rows, wide), 1) // d.slab

    def put_out(j, carry):
        for ct in range(CHIPS // TILE_PARTS):
            for qt in range(d.pair // TILE_PARTS):
                src = [gbuf[j, ct * TILE_PARTS + c, :, qt * wide:(qt + 1) * wide] for c in range(TILE_PARTS)]
                for q in range(TILE_PARTS):
                    tile = jnp.zeros((d.out_rows, wide), jnp.float32)
                    for c in range(TILE_PARTS):
                        shift = (c - q) % TILE_PARTS * d.slab
                        moved = pltpu.roll(src[c], shift, 1) if shift else src[c]
                        tile = jnp.where(lanes == c, moved, tile)
                    at = (qt * TILE_PARTS + q) * d.out_rows
                    tbuf[j, at:at + d.out_rows, ct * wide:(ct + 1) * wide] = tile
        pltpu.make_async_copy(tbuf.at[j], out.at[j], o_sem).start()
        return carry

    lax.fori_loop(0, LANCZOS_STEPS, put_out, 0)
    pltpu.make_async_copy(tbuf, out, o_sem).wait()


def solution(mesh):
    def device_body(wavefunction, left_loc, pair_loc, right_loc, flag_loc):
        bond, pair = wavefunction.shape[0], wavefunction.shape[1]
        d = Dims(bond, pair, left_loc.shape[0])
        eye = jnp.eye(bond, dtype=jnp.bfloat16)
        right_used = jnp.where((flag_loc == 1)[:, None, None], right_loc, eye)
        pair_wide = jnp.repeat(pair_loc, d.sub, axis=2)
        bf16, f32 = jnp.bfloat16, jnp.float32
        dma = pltpu.SemaphoreType.DMA
        any_space = pl.BlockSpec(memory_space=pl.ANY)
        rows_out, info = pl.pallas_call(
            functools.partial(lanczos_kernel, d),
            out_shape=(jax.ShapeDtypeStruct((LANCZOS_STEPS, d.half, bond), f32), jax.ShapeDtypeStruct((3, 8, 128), f32)),
            in_specs=[any_space] * 4,
            out_specs=(any_space, pl.BlockSpec(memory_space=pltpu.VMEM)),
            scratch_shapes=[
                pltpu.VMEM((CHUNKS, CHIPS, CORES, d.terms_dev, 2, d.chunk, d.half), bf16),
                pltpu.VMEM((CHIPS, CORES, d.terms_dev, d.slab, bond), bf16),
                pltpu.VMEM((CHIPS, CORES, d.terms_dev, pair, d.prod), bf16),
                pltpu.VMEM((CHIPS, CORES, d.terms_dev, d.prod, d.prod), bf16),
                pltpu.VMEM((CHUNKS, pair // 2, bond, 2 * d.chunk), bf16),
                pltpu.VMEM((d.lane_tiles, d.half * pair, d.lane), f32),
                pltpu.VMEM((d.group_terms, d.prod, 2 * d.chunk), bf16),
                pltpu.VMEM((d.rows, d.group_terms * d.chunk), bf16),
                pltpu.VMEM((2, d.rows, d.half), f32),
                pltpu.VMEM((d.rows, d.half), f32),
                pltpu.VMEM((d.rows, d.half), f32),
                pltpu.VMEM((d.rows, d.half), f32),
                pltpu.VMEM((LANCZOS_STEPS, d.half, bond), f32),
                pltpu.VMEM((LANCZOS_STEPS, CHIPS, d.out_rows, bond), f32),
                pltpu.VMEM((8, 128), f32),
                pltpu.VMEM((DEVS, 8, 128), f32),
                pltpu.VMEM((2, 8, 128), f32),
                dma((3, 2)), dma((8, d.lane_tiles)), dma((CHUNKS, 2)), dma((CHUNKS, 2)), dma((2,)), dma((2,)), dma((2,)), dma((2,)),
                dma, dma((CHIPS,)), dma((CHUNKS,)), dma((CHUNKS, CHIPS)),
                dma, dma, dma, dma, dma, dma, dma, dma, dma,
            ],
            compiler_params=pltpu.CompilerParams(has_side_effects=True, vmem_limit_bytes=67043328),
            name='lanczos',
        )(wavefunction.reshape(bond * pair, bond), left_loc, right_used, pair_wide)
        row_start = lax.axis_index(AXIS_NAME) * d.out_rows
        first = lax.dynamic_slice_in_dim(wavefunction, row_start, d.out_rows, axis=0) / info[2, 0, 0]
        later = rows_out.reshape(LANCZOS_STEPS, pair, d.out_rows, bond).transpose(0, 2, 1, 3)
        return jnp.concatenate([first[None], later]), info[0, :LANCZOS_STEPS, 0], info[1, :LANCZOS_STEPS, 0]

    return jax.shard_map(device_body, mesh=mesh, in_specs=(P(), P(AXIS_NAME), P(AXIS_NAME), P(AXIS_NAME), P(AXIS_NAME)),
                         out_specs=(P(None, AXIS_NAME), P(), P()), check_vma=False)
```

time: 3010 us -> 641 us (0.21)
  waiting for transfers between devices: 1480 us -> 0 us
  Pallas kernels: 0 us -> 625 us
  matrix products: 575 us -> 0 us
  blocking collectives: 486 us -> 0 us
  local copies, waits for them, and re-layouts: 365 us -> 7.18 us
  other arithmetic: 58.1 us -> 7.07 us
    reduce_scatter x6 -> x0, waiting for transfers between devices: 1090 us -> none  [device_body(): lax.psum_scatter(part_sigma, AXIS_NAME, scatter_dimension=0, tiled=True)]
    pallas_call x0 -> x1, Pallas kernels: none -> 625 us  [device_body(): pl.pallas_call(functools.partial(lanczos_kernel, d), out_shape=(jax.Shape...]
    dot_general x36 -> x0, matrix products: 575 us -> none  [the longest x12 345 us: term_body(): lax.dot_general(left_loc[term_idx], pair_done, (((1,), (1,)), ((), ())),...]
    psum x12 -> x0, blocking collectives: 486 us -> none  [the longest x6 245 us: device_body(): alpha_now = lax.psum(jnp.sum(sigma_slab * current), AXIS_NAME) / vec_size]
    all_gather x5 -> x0, waiting for transfers between devices: 390 us -> none  [device_body(): lax.all_gather(following.astype(jnp.bfloat16), AXIS_NAME, axis=0, tiled=T...]
    cond x12 -> x0, local copies, waits for them, and re-layouts: 179 us -> none  [term_body(): lax.cond(flag_loc[term_idx] == 1, apply_right, keep_vector, right_loc[ter...]
    while x6 -> x0, local copies, waits for them, and re-layouts: 107 us -> none  [local_sigma(): return lax.fori_loop(0, left_loc.shape[0], term_body, start_sum)]
    unnamed x56 -> x2, local copies, waits for them, and re-layouts: 71 us -> 0.01 us
  transfers between devices with their start and end apart: 11 -> 0, of which waited for: 11 -> 0; matrix products, arithmetic and copies ran while one was open for 0% -> 0% of each run, Pallas kernels for 0% -> 0%
where the time goes in v1:
time: 641 us; the launch traced here: 640 us
  Pallas kernels  625 us (98%)
  local copies, waits for them, and re-layouts  7.18 us (1%)
  other arithmetic  7.07 us (1%)
    pallas_call x1, Pallas kernels, device_body(): pl.pallas_call(functools.partial(lanczos_kernel, d), out_shape=(jax.Shape...  625 us

profile of v1, /device:TPU:15, one launch (start us, length us, event | category | flops | bytes accessed | tf_op | source)
XLA Modules:
  0.0 640.3 jit_solution(9312135365759241675)
XLA Ops:
  0.6 0.7 broadcast_compare_fusion
  1.3 0.8 broadcast_in_dim.21
  2.1 0.8 reshape.17.wexp
  2.9 2.4 broadcast_select_fusion.right
  5.3 625.4 %lanczos.1 = (f32[6,256,512]{2,1,0:T(8,128)}, f32[3,8,128]{2,1,0:T(8,128)}) custom-call(f32[8192,512]{1,0:T(8,128)} %bitcast.10, bf16[2,512,512]{2,1,0:T(8,128)(2,1)} %left.1, bf16[2,512,512]{2,1,0:T(8,128)(2,1)} %broadcast_select_fusion.right, bf16[2,16,256]{2,1,0:T(8,128)(2,1)} %reshape.17.wexp), custom_call_target="tpu_custom_call" | custom-call | tf_op jit(solution)/shard_map/lanczos/pallas_call | solution.py:415
  630.7 0.0 copy-start
  630.8 1.3 slice.9
  632.0 3.7 copy.11
  635.7 0.0 copy-done
  635.7 0.7 slice_reduce_fusion
  636.4 1.8 divide_bitcast_fusion
  638.1 2.2 pad_maximum_fusion
  (1 shorter events, 0.0 us)
Async XLA Ops:
  630.7 5.0 copy-start

commit v2 on v1

--- a/solution.py
+++ b/solution.py
@@ -112,8 +112,8 @@
                            pl.ds(pl.multiple_of((core + h) % 2 * d.half, d.half), d.half)]
             theirs = left.at[:, pl.ds(pl.multiple_of((1 - core) * d.half + ch * d.chunk, d.chunk), d.chunk),
                              pl.ds(pl.multiple_of((1 - core + h) % 2 * d.half, d.half), d.half)]
-            remote(theirs, lv.at[ch, slot, core, :, h], d2d_sem.at[ch, h], d2d_recv.at[ch, h], partner).start()
-            pltpu.make_async_copy(mine, lv.at[ch, slot, core, :, h], loc_sem.at[ch, h]).start()
+            remote(theirs, lv.at[ch, slot, core, :, :, pl.ds(h * d.half, d.half)], d2d_sem.at[ch, h], d2d_recv.at[ch, h], partner).start()
+            pltpu.make_async_copy(mine, lv.at[ch, slot, core, :, :, pl.ds(h * d.half, d.half)], loc_sem.at[ch, h]).start()
 
     psi_rows = d.half * d.pair // 8
     psi_copies = [pltpu.make_async_copy(psi.at[pl.ds(pl.multiple_of(core * d.half * d.pair + n * psi_rows, psi_rows), psi_rows),
@@ -138,8 +138,8 @@
 
     for ch in range(CHUNKS):
         for h in range(2):
-            pltpu.make_async_copy(lv.at[ch, slot, core, :, h], lv.at[ch, slot, core, :, h], loc_sem.at[ch, h]).wait()
-            back = remote(lv.at[ch, slot, 1 - core, :, h], lv.at[ch, slot, 1 - core, :, h], d2d_sem.at[ch, h], d2d_recv.at[ch, h], partner)
+            pltpu.make_async_copy(lv.at[ch, slot, core, :, :, pl.ds(h * d.half, d.half)], lv.at[ch, slot, core, :, :, pl.ds(h * d.half, d.half)], loc_sem.at[ch, h]).wait()
+            back = remote(lv.at[ch, slot, 1 - core, :, :, pl.ds(h * d.half, d.half)], lv.at[ch, slot, 1 - core, :, :, pl.ds(h * d.half, d.half)], d2d_sem.at[ch, h], d2d_recv.at[ch, h], partner)
             back.wait_recv()
     l_gather.own_along()
     l_gather.own_across()
@@ -216,7 +216,7 @@
     l_gather.event(6)
     vprev[...] = jnp.zeros_like(vprev)
 
-    def products(ch, grp, is_last):
+    def products(ch, grp):
         r_all = rv[pl.ds(grp * 4, 4)].reshape(d.group_terms * d.slab, d.bond)
         for qb in range(d.pair // 2):
             y = jnp.dot(r_all, uv[ch, qb], preferred_element_type=jnp.float32).astype(jnp.bfloat16)
@@ -230,13 +230,24 @@
             z = jnp.dot(w, yst[k], preferred_element_type=jnp.float32).astype(jnp.bfloat16)
             for bh in range(2):
                 zst[bh * d.prod:(bh + 1) * d.prod, k * d.chunk:(k + 1) * d.chunk] = z[:, bh * d.chunk:(bh + 1) * d.chunk]
-        for h in (1, 0):
-            l_all = lv[ch, pl.ds(grp * 4, 4), :, :, h].reshape(d.group_terms * d.chunk, d.half)
-            sig[h] += jnp.dot(zst[...], l_all, preferred_element_type=jnp.float32)
-            if h == 1:
-                @pl.when(is_last)
-                def _():
-                    remote(sig.at[1], part, p_send, p_recv, partner).start()
+        l_all = lv[ch, pl.ds(grp * 4, 4)].reshape(d.group_terms * d.chunk, d.bond)
+        sig[...] += jnp.dot(zst[...], l_all, preferred_element_type=jnp.float32)
+
+    def hand_out(j):
+        def one(n, carry):
+            to = core * CHIPS + n
+            block = tbuf.at[j, pl.ds(pl.multiple_of(n * d.out_rows, d.out_rows), d.out_rows), :]
+
+            @pl.when(to != me)
+            def _():
+                remote(block, gbuf.at[j, slot], k_send, k_recv, to).start()
+
+            @pl.when(to == me)
+            def _():
+                gbuf[j, slot] = block[...]
+            return carry
+
+        lax.fori_loop(0, CHIPS, one, 0)
 
     def step(j, beta_prev):
         later = jnp.minimum(j, 1)
@@ -277,8 +288,9 @@
             def _():
                 u_gather[1].last(False)
                 u_gather[1].last(True)
-
-            products(ch, grp, it == 7)
+                hand_out(j - 1)
+
+            products(ch, grp)
             return carry
 
         lax.fori_loop(0, 2 * GROUPS, part_step, 0)
@@ -289,8 +301,11 @@
                 sent = uv.at[ch, :, pl.ds(0, 15 * d.slab), :]
                 remote(sent, sent, u_send.at[ch], u_recv.at[ch, 0], me).wait_send()
 
-        remote(sig.at[1], part, p_send, p_recv, partner).wait()
-        s = sig[0] + part[...]
+        other = sig.at[:, pl.ds(d.half, d.half)]
+        to_other = remote(other, part, p_send, p_recv, partner)
+        to_other.start()
+        to_other.wait()
+        s = sig[:, :d.half] + part[...]
         v = vcur[...]
         w = s - beta_prev * vprev[...]
         sv = jnp.sum(s * v, keepdims=True)
@@ -298,7 +313,7 @@
         vv = jnp.sum(v * v, keepdims=True)
         guess = jnp.where(vv > 0.0, wv_sum / jnp.where(vv > 0.0, vv, 1.0), 0.0)
         t = w - guess * v
-        sig[0] = t
+        sig[:, :d.half] = t
         tt = jnp.sum(t * t, keepdims=True)
         tv = jnp.sum(t * v, keepdims=True)
         tile_row = lax.broadcasted_iota(jnp.int32, (8, 128), 0)
@@ -321,7 +336,7 @@
         beta = jnp.sqrt(jnp.sum(square, axis=0, keepdims=True) / d.vec_size)
         info[0, pl.ds(j, 1), :] = alpha
         info[1, pl.ds(j, 1), :] = beta
-        vnew = (sig[0] - (alpha[:, 0:1] - guess) * vcur[...]) / beta[:, 0:1]
+        vnew = (sig[:, :d.half] - (alpha[:, 0:1] - guess) * vcur[...]) / beta[:, 0:1]
         vprev[...] = vcur[...]
         vcur[...] = vnew
         vb = vnew.astype(jnp.bfloat16)
@@ -344,30 +359,17 @@
                     for q in range(n * TILE_PARTS, (n + 1) * TILE_PARTS) for bh in range(2)]
             tbuf[j, :, n * wide:(n + 1) * wide] = jnp.concatenate(rows, axis=0).T
 
-        def hand_out(n, carry):
-            to = core * CHIPS + n
-            block = tbuf.at[j, pl.ds(pl.multiple_of(n * d.out_rows, d.out_rows), d.out_rows), :]
-
-            @pl.when(to != me)
-            def _():
-                remote(block, gbuf.at[j, slot], k_send, k_recv, to).start()
-
-            @pl.when(to == me)
-            def _():
-                gbuf[j, slot] = block[...]
-            return carry
-
-        lax.fori_loop(0, CHIPS, hand_out, 0)
         return beta[:, 0:1]
 
     lax.fori_loop(0, LANCZOS_STEPS, step, jnp.zeros((1, 1), jnp.float32))
 
+    hand_out(LANCZOS_STEPS - 1)
     fourteen = lv.at[:, pl.ds(0, 15)]
     remote(fourteen, fourteen, l_send, l_recv.at[0], me).wait_send()
     for ch in range(CHUNKS):
         for h in range(2):
             theirs = left.at[:, pl.ds(0, d.chunk), pl.ds(0, d.half)]
-            remote(theirs, lv.at[ch, slot, core, :, h], d2d_sem.at[ch, h], d2d_recv.at[ch, h], partner).wait_send()
+            remote(theirs, lv.at[ch, slot, core, :, :, pl.ds(h * d.half, d.half)], d2d_sem.at[ch, h], d2d_recv.at[ch, h], partner).wait_send()
 
     sends_self = me // CHIPS == core
 
@@ -418,7 +420,7 @@
             in_specs=[any_space] * 4,
             out_specs=(any_space, pl.BlockSpec(memory_space=pltpu.VMEM)),
             scratch_shapes=[
-                pltpu.VMEM((CHUNKS, CHIPS, CORES, d.terms_dev, 2, d.chunk, d.half), bf16),
+                pltpu.VMEM((CHUNKS, CHIPS, CORES, d.terms_dev, d.chunk, bond), bf16),
                 pltpu.VMEM((CHIPS, CORES, d.terms_dev, d.slab, bond), bf16),
                 pltpu.VMEM((CHIPS, CORES, d.terms_dev, pair, d.prod), bf16),
                 pltpu.VMEM((CHIPS, CORES, d.terms_dev, d.prod, d.prod), bf16),
@@ -426,7 +428,7 @@
                 pltpu.VMEM((d.lane_tiles, d.half * pair, d.lane), f32),
                 pltpu.VMEM((d.group_terms, d.prod, 2 * d.chunk), bf16),
                 pltpu.VMEM((d.rows, d.group_terms * d.chunk), bf16),
-                pltpu.VMEM((2, d.rows, d.half), f32),
+                pltpu.VMEM((d.rows, bond), f32),
                 pltpu.VMEM((d.rows, d.half), f32),
                 pltpu.VMEM((d.rows, d.half), f32),
                 pltpu.VMEM((d.rows, d.half), f32),

time: 641 us -> 590 us (0.920)
  Pallas kernels: 625 us -> 574 us
    pallas_call x1, Pallas kernels: 625 us -> 574 us  [device_body(): pl.pallas_call(functools.partial(lanczos_kernel, d), out_shape=(jax.Shape...]
where the time goes in v2:
time: 590 us; the launch traced here: 589 us
  Pallas kernels  574 us (97%)
  local copies, waits for them, and re-layouts  7.18 us (1%)
  other arithmetic  7.07 us (1%)
    pallas_call x1, Pallas kernels, device_body(): pl.pallas_call(functools.partial(lanczos_kernel, d), out_shape=(jax.Shape...  574 us

profile of v2, /device:TPU:15, one launch (start us, length us, event | category | flops | bytes accessed | tf_op | source)
XLA Modules:
  0.0 589.2 jit_solution(1988192584515556840)
XLA Ops:
  0.6 0.7 broadcast_compare_fusion
  1.3 0.8 broadcast_in_dim.21
  2.1 0.8 reshape.17.wexp
  2.9 2.4 broadcast_select_fusion.right
  5.3 574.3 %lanczos.1 = (f32[6,256,512]{2,1,0:T(8,128)}, f32[3,8,128]{2,1,0:T(8,128)}) custom-call(f32[8192,512]{1,0:T(8,128)} %bitcast.10, bf16[2,512,512]{2,1,0:T(8,128)(2,1)} %left.1, bf16[2,512,512]{2,1,0:T(8,128)(2,1)} %broadcast_select_fusion.right, bf16[2,16,256]{2,1,0:T(8,128)(2,1)} %reshape.17.wexp), custom_call_target="tpu_custom_call" | custom-call | tf_op jit(solution)/shard_map/lanczos/pallas_call | solution.py:417
  579.6 0.0 copy-start
  579.6 1.3 slice.9
  580.9 3.7 copy.11
  584.6 0.0 copy-done
  584.6 0.7 slice_reduce_fusion
  585.3 1.8 divide_bitcast_fusion
  587.0 2.2 pad_maximum_fusion
  (1 shorter events, 0.0 us)
Async XLA Ops:
  579.6 5.0 copy-start

commit v3 on v2

--- a/solution.py
+++ b/solution.py
@@ -38,7 +38,7 @@
 
 
 def lanczos_kernel(d, psi, left, right, wexp, out, info, lv, rv, wv, kw, uv, ps, yst, zst, sig, part, vcur, vprev, tbuf, gbuf, scs, scr, nbuf,
-                   loc_sem, psi_sem, d2d_sem, d2d_recv, rw_send, rw_recv, fw_send, fw_recv, l_send, l_recv, u_send, u_recv,
+                   loc_sem, psi_sem, d2d_sem, d2d_recv, rw_send, rw_recv, fw_send, fw_recv, l_send, l_recv, f_send, f_recv, u_send, u_recv,
                    p_send, p_recv, s_send, s_recv, k_send, k_recv, n_send, n_recv, o_sem):
     me = lax.axis_index(AXIS_NAME)
     core = me % 2
@@ -99,7 +99,49 @@
             for i in range(4):
                 self.wait(chip_slot(zs[i], 1 - ypos, 1 - xpos) if diagonal else chip_slot(zs[i], y_three, x_three))
 
-    l_gather = Gather(lambda s: lv.at[:, s], l_send, lambda s: l_recv.at[s])
+    edge = d.chunk
+    l_parts = (
+        (lambda s: lv.at[0, s, :, core], 0),
+        (lambda s: lv.at[1, s, :, core, :, pl.ds(edge, d.bond - edge)], 1),
+        (lambda s: lv.at[0, s, :, 1 - core, :, pl.ds(0, d.half)], 2),
+        (lambda s: lv.at[1, s, :, 1 - core, :, pl.ds(edge, d.half - edge)], 3),
+    )
+    l_gathers = [Gather(block, l_send.at[n], lambda s, n=n: l_recv.at[n, s]) for block, n in l_parts]
+
+    def l_swap(s, term):
+        part = lv.at[:, s, :, term, :, pl.ds(d.half, d.half)]
+        return remote(part, part, f_send, f_recv.at[s], partner)
+
+    def l_event(n):
+        i = (n + 1) // 2
+        for g in l_gathers:
+            g.event(n)
+        l_swap(chip_slot(zs[i], ypos, xpos) if n % 2 else chip_slot(zs[i], y_two, x_two), core).start()
+
+    def l_last(diagonal):
+        for i in range(4):
+            which = chip_slot(zs[i], 1 - ypos, 1 - xpos) if diagonal else chip_slot(zs[i], y_three, x_three)
+            for g in l_gathers:
+                g.wait(which)
+            l_swap(which, core).start()
+
+    def l_fill(n, grp):
+        s = grp * 4 + n
+
+        @pl.when(s != slot)
+        def _():
+            l_swap(s, 1 - core).wait_recv()
+            for c in range(CORES):
+                tile = lv[:, s, c, 1 - core, :, d.half:].reshape(d.half, d.half).T
+                lv[:, s, c, 1 - core, :, d.half:] = tile.reshape(CHUNKS, d.chunk, d.half)
+                for t in range(d.terms_dev):
+                    lv[1, s, c, t, :, :edge] = lv[0, s, c, t, :, edge:d.half].T
+        return grp
+
+    def l_along():
+        for i in (1, 2, 3):
+            for g in l_gathers:
+                g.send(slot, device(zs[i], ypos, xpos, core))
 
     def u_block(ch):
         return lambda s: uv.at[ch, :, pl.ds(pl.multiple_of(s * d.slab, d.slab), d.slab), :]
@@ -141,8 +183,9 @@
             pltpu.make_async_copy(lv.at[ch, slot, core, :, :, pl.ds(h * d.half, d.half)], lv.at[ch, slot, core, :, :, pl.ds(h * d.half, d.half)], loc_sem.at[ch, h]).wait()
             back = remote(lv.at[ch, slot, 1 - core, :, :, pl.ds(h * d.half, d.half)], lv.at[ch, slot, 1 - core, :, :, pl.ds(h * d.half, d.half)], d2d_sem.at[ch, h], d2d_recv.at[ch, h], partner)
             back.wait_recv()
-    l_gather.own_along()
-    l_gather.own_across()
+    l_along()
+    for g in l_gathers:
+        g.own_across()
 
     total = jnp.zeros((8, d.lane), jnp.float32)
     for n in range(8):
@@ -190,11 +233,11 @@
     fw_pair = remote(wv.at[:, core], wv.at[:, core], fw_send.at[1], fw_recv.at[1], partner)
     fw_right.start()
     fw_pair.start()
-    l_gather.event(0)
-    l_gather.event(1)
+    l_event(0)
+    l_event(1)
     lax.fori_loop(d.pair // 4, d.pair // 2, start_vector, 0)
-    l_gather.event(2)
-    l_gather.event(3)
+    l_event(2)
+    l_event(3)
     fw_right.wait()
     fw_pair.wait()
     lane = lax.broadcasted_iota(jnp.int32, (d.sub, d.prod), 1)
@@ -211,9 +254,9 @@
         return carry
 
     lax.fori_loop(0, CHIPS, spread_pair, 0)
-    l_gather.event(4)
-    l_gather.event(5)
-    l_gather.event(6)
+    l_event(4)
+    l_event(5)
+    l_event(6)
     vprev[...] = jnp.zeros_like(vprev)
 
     def products(ch, grp):
@@ -271,13 +314,17 @@
             arrive = jnp.where(n == 0, own, jnp.where(n == 1, x_two * 2 + y_two, jnp.where(n == 2, x_three * 2 + y_three, 3 - own)))
             grp = (1 - later) * arrive + later * n
 
-            @pl.when((j == 0) & (it == 4))
+            @pl.when((j == 0) & (it == 2))
             def _():
-                l_gather.last(False)
+                l_last(False)
 
             @pl.when((j == 0) & (it == 6))
             def _():
-                l_gather.last(True)
+                l_last(True)
+
+            @pl.when((j == 0) & (it % 2 == 0))
+            def _():
+                lax.fori_loop(0, 4, l_fill, grp)
 
             for at in range(3):
                 @pl.when((j > 0) & (it == at))
@@ -364,8 +411,11 @@
     lax.fori_loop(0, LANCZOS_STEPS, step, jnp.zeros((1, 1), jnp.float32))
 
     hand_out(LANCZOS_STEPS - 1)
-    fourteen = lv.at[:, pl.ds(0, 15)]
-    remote(fourteen, fourteen, l_send, l_recv.at[0], me).wait_send()
+    for n, part in enumerate((lv.at[0, pl.ds(0, 15), :, 0], lv.at[1, pl.ds(0, 15), :, 0, :, pl.ds(edge, d.bond - edge)],
+                              lv.at[0, pl.ds(0, 15), :, 0, :, pl.ds(0, d.half)], lv.at[1, pl.ds(0, 15), :, 0, :, pl.ds(edge, d.half - edge)])):
+        remote(part, part, l_send.at[n], l_recv.at[n, 0], me).wait_send()
+    swapped = lv.at[:, pl.ds(0, 15), :, 0, :, pl.ds(d.half, d.half)]
+    remote(swapped, swapped, f_send, f_recv.at[0], me).wait_send()
     for ch in range(CHUNKS):
         for h in range(2):
             theirs = left.at[:, pl.ds(0, d.chunk), pl.ds(0, d.half)]
@@ -438,7 +488,7 @@
                 pltpu.VMEM((DEVS, 8, 128), f32),
                 pltpu.VMEM((2, 8, 128), f32),
                 dma((3, 2)), dma((8, d.lane_tiles)), dma((CHUNKS, 2)), dma((CHUNKS, 2)), dma((2,)), dma((2,)), dma((2,)), dma((2,)),
-                dma, dma((CHIPS,)), dma((CHUNKS,)), dma((CHUNKS, CHIPS)),
+                dma((4,)), dma((4, CHIPS)), dma, dma((CHIPS,)), dma((CHUNKS,)), dma((CHUNKS, CHIPS)),
                 dma, dma, dma, dma, dma, dma, dma, dma, dma,
             ],
             compiler_params=pltpu.CompilerParams(has_side_effects=True, vmem_limit_bytes=67043328),

time: 590 us -> 551 us (0.934)
  Pallas kernels: 574 us -> 536 us
    pallas_call x1, Pallas kernels: 574 us -> 536 us  [device_body(): pl.pallas_call(functools.partial(lanczos_kernel, d), out_shape=(jax.Shape...]
where the time goes in v3:
time: 551 us
  Pallas kernels  536 us (97%)
  local copies, waits for them, and re-layouts  7.18 us (1%)
  other arithmetic  7.07 us (1%)
    pallas_call x1, Pallas kernels, device_body(): pl.pallas_call(functools.partial(lanczos_kernel, d), out_shape=(jax.Shape...  536 us

profile of v3, /device:TPU:15, one launch (start us, length us, event | category | flops | bytes accessed | tf_op | source)
XLA Modules:
  0.0 550.8 jit_solution(9987420592181754196)
XLA Ops:
  0.6 0.7 broadcast_compare_fusion
  1.3 0.8 broadcast_in_dim.21
  2.1 0.8 reshape.17.wexp
  2.9 2.4 broadcast_select_fusion.right
  5.3 535.9 %lanczos.1 = (f32[6,256,512]{2,1,0:T(8,128)}, f32[3,8,128]{2,1,0:T(8,128)}) custom-call(f32[8192,512]{1,0:T(8,128)} %bitcast.10, bf16[2,512,512]{2,1,0:T(8,128)(2,1)} %left.1, bf16[2,512,512]{2,1,0:T(8,128)(2,1)} %broadcast_select_fusion.right, bf16[2,16,256]{2,1,0:T(8,128)(2,1)} %reshape.17.wexp), custom_call_target="tpu_custom_call" | custom-call | tf_op jit(solution)/shard_map/lanczos/pallas_call | solution.py:467
  541.2 0.0 copy-start
  541.3 1.3 slice.9
  542.5 3.7 copy.11
  546.2 0.0 copy-done
  546.2 0.7 slice_reduce_fusion
  546.9 1.8 divide_bitcast_fusion
  548.6 2.2 pad_maximum_fusion
  (1 shorter events, 0.0 us)
Async XLA Ops:
  541.2 5.0 copy-start

commit v4 on v3

--- a/solution.py
+++ b/solution.py
@@ -17,6 +17,29 @@
 CHUNKS = 2
 GROUPS = 4
 TILE_PARTS = 4
+QUARTERS = 4
+PIECES = CHUNKS * QUARTERS
+
+ALONG, ACROSS, FROM_COLUMN, FROM_SECOND, THIRD, DIAGONAL, RESULT, RESULT_OUT = range(8)
+RIGHT_SLOTS = (0, 1, 2, 3, 8, 9, 10, 11)
+SLOTS = (
+    ((1, 0, 1), (1, 0, 6), (0, 1, 1), (1, 0, 2), (1, 0, 3), (0, 1, 2), (1, 0, 4), (1, 0, 7), (0, 2, 2), (1, 0, 5), (0, 1, 3), (0, 1, 0), (0, 2, 0), (0, 3, 0), (0, 3, 1), (0, 2, 1), (0, 3, 2), (1, 0, 0), (3, 0, 3), (3, 0, 2), (2, 1, 2), (2, 1, 1), (0, 3, 3), (2, 1, 0), (2, 2, 0), (3, 0, 0), (2, 2, 1), (3, 1, 1), (0, 2, 3), (2, 2, 2), (3, 1, 0), (2, 3, 0), (3, 2, 0), (3, 0, 1), (2, 2, 3), (0, 3, 4), (2, 3, 1), (2, 3, 2), (0, 3, 5), (3, 3, 0), (0, 1, 4), (0, 2, 4), (0, 1, 5), (2, 1, 3), (3, 2, 1), (3, 2, 3), (3, 3, 1), (0, 2, 5), (0, 1, 6), (2, 3, 3), (0, 3, 7), (3, 3, 2), (3, 1, 3), (0, 3, 6), (3, 2, 2), (0, 2, 6), (3, 1, 2), (0, 2, 7), (3, 3, 3), (5, 0, 0), (3, 0, 4), (4, 0, 1), (4, 0, 0), (3, 0, 5),),
+    ((6, 0, 0), (2, 3, 4), (4, 0, 2), (3, 0, 6), (5, 0, 1),),
+    ((2, 2, 4), (2, 1, 4), (2, 1, 5), (5, 0, 2), (2, 2, 5),),
+    ((5, 0, 3), (0, 1, 7), (3, 3, 4), (4, 0, 3), (2, 3, 5), (2, 1, 6), (2, 2, 6),),
+    (),
+    ((4, 0, 4), (2, 3, 6), (3, 1, 4), (2, 2, 7), (3, 2, 4),),
+    ((3, 3, 5), (3, 2, 5), (3, 1, 5), (2, 3, 7), (2, 1, 7),),
+    ((3, 1, 6), (3, 3, 6),),
+    ((4, 0, 5), (3, 2, 6), (3, 0, 7), (4, 0, 6), (5, 0, 4), (3, 3, 7), (3, 2, 7),),
+    ((5, 0, 5), (3, 1, 7),),
+    ((4, 0, 7), (5, 0, 6),),
+    ((5, 0, 7), (7, 0, 0),),
+    (),
+    (),
+    (),
+    (),
+)
 
 
 class Dims:
@@ -55,6 +78,9 @@
     partner = device(zpos, ypos, xpos, 1 - core)
     slot = chip_slot(zpos, ypos, xpos)
     zs = (zpos, zpos + 1 - 2 * (zpos % 2), (zpos + 2) % 4, 3 - zpos)
+    inner = (zpos + 1) // 2 % 2
+    zn = (zpos, (1 - inner) * (zpos + 1 - zpos // 3 * 2) + inner * (zpos - 1), (1 - inner) * ((zpos + 2) % 4) + inner * (zpos + 1),
+          (1 - inner) * (3 - zpos) + inner * ((zpos + 2) % 4))
     y_two = ypos + (1 - core) * (1 - 2 * ypos)
     x_two = xpos + core * (1 - 2 * xpos)
     y_three = ypos + core * (1 - 2 * ypos)
@@ -143,10 +169,34 @@
             for g in l_gathers:
                 g.send(slot, device(zs[i], ypos, xpos, core))
 
-    def u_block(ch):
-        return lambda s: uv.at[ch, :, pl.ds(pl.multiple_of(s * d.slab, d.slab), d.slab), :]
-
-    u_gather = [Gather(u_block(ch), u_send.at[ch], lambda s, ch=ch: u_recv.at[ch, s]) for ch in range(CHUNKS)]
+    def u_block(p):
+        return lambda s: uv.at[p // QUARTERS, pl.ds(p % QUARTERS * 2, 2), pl.ds(pl.multiple_of(s * d.slab, d.slab), d.slab), :]
+
+    u_gathers = [Gather(u_block(p), u_send.at[p], lambda s, p=p: u_recv.at[p, s]) for p in range(PIECES)]
+
+    def act(kind, i, p, j):
+        g = u_gathers[p]
+        if kind == ALONG:
+            g.send(slot, device(zn[i], ypos, xpos, core))
+        elif kind == ACROSS:
+            g.own_across()
+        elif kind == FROM_COLUMN:
+            which = chip_slot(zn[i], ypos, xpos)
+            g.wait(which)
+            g.send(which, three)
+            g.send(which, two)
+        elif kind == FROM_SECOND:
+            which = chip_slot(zn[i], y_two, x_two)
+            g.wait(which)
+            g.send(which, three)
+        elif kind == THIRD:
+            g.last(False)
+        elif kind == DIAGONAL:
+            g.last(True)
+        elif kind == RESULT:
+            turn_result(j - 1)
+        elif kind == RESULT_OUT:
+            hand_out(j - 1)
 
     for ch in range(CHUNKS):
         for h in range(2):
@@ -259,23 +309,40 @@
     l_event(6)
     vprev[...] = jnp.zeros_like(vprev)
 
-    def products(ch, grp):
+    def right_product(grp, ch, qb):
         r_all = rv[pl.ds(grp * 4, 4)].reshape(d.group_terms * d.slab, d.bond)
+        y = jnp.dot(r_all, uv[ch, qb], preferred_element_type=jnp.float32).astype(jnp.bfloat16)
+        y = y.reshape(d.group_terms, 2, d.sub, 2 * d.chunk)
+        for q2 in range(2):
+            for bh in range(2):
+                yst[pl.ds(grp * d.group_terms, d.group_terms), qb * 2 + q2, :, bh * d.chunk:(bh + 1) * d.chunk] = \
+                    y[:, bh, :, q2 * d.chunk:(q2 + 1) * d.chunk]
+
+    def right_of_group(grp, ch):
         for qb in range(d.pair // 2):
-            y = jnp.dot(r_all, uv[ch, qb], preferred_element_type=jnp.float32).astype(jnp.bfloat16)
-            y = y.reshape(d.group_terms, 2, d.sub, 2 * d.chunk)
-            for q2 in range(2):
-                q = qb * 2 + q2
-                for bh in range(2):
-                    yst[:, q * d.sub:(q + 1) * d.sub, bh * d.chunk:(bh + 1) * d.chunk] = y[:, bh, :, q2 * d.chunk:(q2 + 1) * d.chunk]
+            right_product(grp, ch, qb)
+
+    def right_of_piece(ch, part):
+        for qb in range(2):
+            for grp in range(GROUPS):
+                right_product(grp, ch, part * 2 + qb)
+
+    def left_products(ch, grp):
         for k in range(d.group_terms):
             w = kw[grp * 4 + k // 4, k // 2 % 2, k % 2]
-            z = jnp.dot(w, yst[k], preferred_element_type=jnp.float32).astype(jnp.bfloat16)
+            z = jnp.dot(w, yst[grp * d.group_terms + k].reshape(d.prod, 2 * d.chunk), preferred_element_type=jnp.float32).astype(jnp.bfloat16)
             for bh in range(2):
                 zst[bh * d.prod:(bh + 1) * d.prod, k * d.chunk:(k + 1) * d.chunk] = z[:, bh * d.chunk:(bh + 1) * d.chunk]
         l_all = lv[ch, pl.ds(grp * 4, 4)].reshape(d.group_terms * d.chunk, d.bond)
         sig[...] += jnp.dot(zst[...], l_all, preferred_element_type=jnp.float32)
 
+    def turn_result(j):
+        wide = TILE_PARTS * d.slab
+        for n in range(d.pair // TILE_PARTS):
+            rows = [vcur[(bh * d.pair + q) * d.sub:(bh * d.pair + q + 1) * d.sub, :]
+                    for q in range(n * TILE_PARTS, (n + 1) * TILE_PARTS) for bh in range(2)]
+            tbuf[j, :, n * wide:(n + 1) * wide] = jnp.concatenate(rows, axis=0).T
+
     def hand_out(j):
         def one(n, carry):
             to = core * CHIPS + n
@@ -294,59 +361,66 @@
 
     def step(j, beta_prev):
         later = jnp.minimum(j, 1)
+        own = xpos * 2 + ypos
+        sig[...] = jnp.zeros_like(sig)
+
+        def slot_step(t, carry):
+            n = t // 4
+            first_grp = jnp.where(n == 0, own, jnp.where(n == 1, x_two * 2 + y_two, jnp.where(n == 2, x_three * 2 + y_three, 3 - own)))
+            first_ch = t // 2 % 2
+            done_right = sum((t > r).astype(jnp.int32) for r in RIGHT_SLOTS)
+            done_left = t - done_right
+            now_right = sum((t == r).astype(jnp.int32) for r in RIGHT_SLOTS)
+            is_right = (1 - later) * (1 - t % 2) + later * now_right
+
+            @pl.when(j == 0)
+            def _():
+                @pl.when(t == 4)
+                def _():
+                    l_last(False)
+
+                @pl.when(t == 12)
+                def _():
+                    l_last(True)
+
+                @pl.when(t % 4 == 0)
+                def _():
+                    lax.fori_loop(0, 4, l_fill, first_grp)
+
+            @pl.when(j > 0)
+            def _():
+                for four in range(0, len(SLOTS), 4):
+                    @pl.when((t >= four) & (t < four + 4))
+                    def _():
+                        for at in range(four, four + 4):
+                            if not SLOTS[at]:
+                                continue
+
+                            @pl.when(t == at)
+                            def _():
+                                for kind, i, p in SLOTS[at]:
+                                    act(kind, i, p, j)
+
+            @pl.when((is_right == 1) & (j == 0))
+            def _():
+                right_of_group(first_grp, first_ch)
+
+            @pl.when((is_right == 1) & (j > 0))
+            def _():
+                right_of_piece(done_right // QUARTERS, done_right % QUARTERS)
+
+            @pl.when(is_right == 0)
+            def _():
+                left_products((1 - later) * first_ch + later * (done_left // GROUPS), (1 - later) * first_grp + later * (done_left % GROUPS))
+            return carry
+
+        lax.fori_loop(0, len(SLOTS), slot_step, 0)
 
         @pl.when(j > 0)
         def _():
-            for n in range(7):
-                u_gather[0].event(n)
-            u_gather[1].own_across()
-            for n in range(4):
-                u_gather[1].event(n)
-            u_gather[0].last(False)
-            u_gather[0].last(True)
-
-        sig[...] = jnp.zeros_like(sig)
-
-        def part_step(it, carry):
-            ch = (1 - later) * (it % 2) + later * (it // 4)
-            n = (1 - later) * (it // 2) + later * (it % 4)
-            own = xpos * 2 + ypos
-            arrive = jnp.where(n == 0, own, jnp.where(n == 1, x_two * 2 + y_two, jnp.where(n == 2, x_three * 2 + y_three, 3 - own)))
-            grp = (1 - later) * arrive + later * n
-
-            @pl.when((j == 0) & (it == 2))
-            def _():
-                l_last(False)
-
-            @pl.when((j == 0) & (it == 6))
-            def _():
-                l_last(True)
-
-            @pl.when((j == 0) & (it % 2 == 0))
-            def _():
-                lax.fori_loop(0, 4, l_fill, grp)
-
-            for at in range(3):
-                @pl.when((j > 0) & (it == at))
-                def _():
-                    u_gather[1].event(4 + at)
-
-            @pl.when((j > 0) & (it == 4))
-            def _():
-                u_gather[1].last(False)
-                u_gather[1].last(True)
-                hand_out(j - 1)
-
-            products(ch, grp)
-            return carry
-
-        lax.fori_loop(0, 2 * GROUPS, part_step, 0)
-
-        @pl.when(j > 0)
-        def _():
-            for ch in range(CHUNKS):
-                sent = uv.at[ch, :, pl.ds(0, 15 * d.slab), :]
-                remote(sent, sent, u_send.at[ch], u_recv.at[ch, 0], me).wait_send()
+            for p in range(PIECES):
+                sent = uv.at[p // QUARTERS, pl.ds(0, 2), pl.ds(0, 15 * d.slab), :]
+                remote(sent, sent, u_send.at[p], u_recv.at[p, 0], me).wait_send()
 
         other = sig.at[:, pl.ds(d.half, d.half)]
         to_other = remote(other, part, p_send, p_recv, partner)
@@ -396,20 +470,12 @@
                     for q in range(d.pair):
                         uv[ch, q // 2, at, q % 2 * d.chunk:(q % 2 + 1) * d.chunk] = \
                             vb[(bh * d.pair + q) * d.sub:(bh * d.pair + q + 1) * d.sub, ch * d.chunk:(ch + 1) * d.chunk]
-            u_gather[0].own_along()
-            u_gather[0].own_across()
-            u_gather[1].own_along()
-
-        wide = TILE_PARTS * d.slab
-        for n in range(d.pair // TILE_PARTS):
-            rows = [vcur[(bh * d.pair + q) * d.sub:(bh * d.pair + q + 1) * d.sub, :]
-                    for q in range(n * TILE_PARTS, (n + 1) * TILE_PARTS) for bh in range(2)]
-            tbuf[j, :, n * wide:(n + 1) * wide] = jnp.concatenate(rows, axis=0).T
-
         return beta[:, 0:1]
 
+
     lax.fori_loop(0, LANCZOS_STEPS, step, jnp.zeros((1, 1), jnp.float32))
 
+    turn_result(LANCZOS_STEPS - 1)
     hand_out(LANCZOS_STEPS - 1)
     for n, part in enumerate((lv.at[0, pl.ds(0, 15), :, 0], lv.at[1, pl.ds(0, 15), :, 0, :, pl.ds(edge, d.bond - edge)],
                               lv.at[0, pl.ds(0, 15), :, 0, :, pl.ds(0, d.half)], lv.at[1, pl.ds(0, 15), :, 0, :, pl.ds(edge, d.half - edge)])):
@@ -476,7 +542,7 @@
                 pltpu.VMEM((CHIPS, CORES, d.terms_dev, d.prod, d.prod), bf16),
                 pltpu.VMEM((CHUNKS, pair // 2, bond, 2 * d.chunk), bf16),
                 pltpu.VMEM((d.lane_tiles, d.half * pair, d.lane), f32),
-                pltpu.VMEM((d.group_terms, d.prod, 2 * d.chunk), bf16),
+                pltpu.VMEM((CHIPS * CORES * d.terms_dev, pair, d.sub, 2 * d.chunk), bf16),
                 pltpu.VMEM((d.rows, d.group_terms * d.chunk), bf16),
                 pltpu.VMEM((d.rows, bond), f32),
                 pltpu.VMEM((d.rows, d.half), f32),
@@ -488,7 +554,7 @@
                 pltpu.VMEM((DEVS, 8, 128), f32),
                 pltpu.VMEM((2, 8, 128), f32),
                 dma((3, 2)), dma((8, d.lane_tiles)), dma((CHUNKS, 2)), dma((CHUNKS, 2)), dma((2,)), dma((2,)), dma((2,)), dma((2,)),
-                dma((4,)), dma((4, CHIPS)), dma, dma((CHIPS,)), dma((CHUNKS,)), dma((CHUNKS, CHIPS)),
+                dma((4,)), dma((4, CHIPS)), dma, dma((CHIPS,)), dma((PIECES,)), dma((PIECES, CHIPS)),
                 dma, dma, dma, dma, dma, dma, dma, dma, dma,
             ],
             compiler_params=pltpu.CompilerParams(has_side_effects=True, vmem_limit_bytes=67043328),

time: 551 us -> 498 us (0.904)
  Pallas kernels: 536 us -> 482 us
    pallas_call x1, Pallas kernels: 536 us -> 482 us  [device_body(): pl.pallas_call(functools.partial(lanczos_kernel, d), out_shape=(jax.Shape...]
where the time goes in v4:
time: 498 us; the launch traced here: 497 us
  Pallas kernels  482 us (97%)
  local copies, waits for them, and re-layouts  7.18 us (1%)
  other arithmetic  7.07 us (1%)
    pallas_call x1, Pallas kernels, device_body(): pl.pallas_call(functools.partial(lanczos_kernel, d), out_shape=(jax.Shape...  482 us

profile of v4, /device:TPU:15, one launch (start us, length us, event | category | flops | bytes accessed | tf_op | source)
XLA Modules:
  0.0 496.8 jit_solution(8503412116862556024)
XLA Ops:
  0.6 0.7 broadcast_compare_fusion
  1.3 0.8 broadcast_in_dim.21
  2.1 0.8 reshape.17.wexp
  2.9 2.4 broadcast_select_fusion.right
  5.3 481.9 %lanczos.1 = (f32[6,256,512]{2,1,0:T(8,128)}, f32[3,8,128]{2,1,0:T(8,128)}) custom-call(f32[8192,512]{1,0:T(8,128)} %bitcast.10, bf16[2,512,512]{2,1,0:T(8,128)(2,1)} %left.1, bf16[2,512,512]{2,1,0:T(8,128)(2,1)} %broadcast_select_fusion.right, bf16[2,16,256]{2,1,0:T(8,128)(2,1)} %reshape.17.wexp), custom_call_target="tpu_custom_call" | custom-call | tf_op jit(solution)/shard_map/lanczos/pallas_call | solution.py:533
  487.2 0.0 copy-start
  487.2 1.3 slice.9
  488.5 3.7 copy.11
  492.2 0.0 copy-done
  492.2 0.7 slice_reduce_fusion
  492.8 1.8 divide_bitcast_fusion
  494.6 2.2 pad_maximum_fusion
  (1 shorter events, 0.0 us)
Async XLA Ops:
  487.2 5.0 copy-start

commit v5 on v4

--- a/solution.py
+++ b/solution.py
@@ -28,13 +28,13 @@
     ((2, 2, 4), (2, 1, 4), (2, 1, 5), (5, 0, 2), (2, 2, 5),),
     ((5, 0, 3), (0, 1, 7), (3, 3, 4), (4, 0, 3), (2, 3, 5), (2, 1, 6), (2, 2, 6),),
     (),
-    ((4, 0, 4), (2, 3, 6), (3, 1, 4), (2, 2, 7), (3, 2, 4),),
+    ((4, 0, 4), (2, 3, 6), (3, 1, 4), (2, 2, 7), (3, 2, 4), (7, 0, 0),),
     ((3, 3, 5), (3, 2, 5), (3, 1, 5), (2, 3, 7), (2, 1, 7),),
     ((3, 1, 6), (3, 3, 6),),
     ((4, 0, 5), (3, 2, 6), (3, 0, 7), (4, 0, 6), (5, 0, 4), (3, 3, 7), (3, 2, 7),),
     ((5, 0, 5), (3, 1, 7),),
     ((4, 0, 7), (5, 0, 6),),
-    ((5, 0, 7), (7, 0, 0),),
+    ((5, 0, 7), (7, 1, 0),),
     (),
     (),
     (),
@@ -196,7 +196,7 @@
         elif kind == RESULT:
             turn_result(j - 1)
         elif kind == RESULT_OUT:
-            hand_out(j - 1)
+            hand_out(j - 1, ((0,), (3, 1, 2))[i])
 
     for ch in range(CHUNKS):
         for h in range(2):
@@ -343,21 +343,20 @@
                     for q in range(n * TILE_PARTS, (n + 1) * TILE_PARTS) for bh in range(2)]
             tbuf[j, :, n * wide:(n + 1) * wide] = jnp.concatenate(rows, axis=0).T
 
-    def hand_out(j):
-        def one(n, carry):
-            to = core * CHIPS + n
-            block = tbuf.at[j, pl.ds(pl.multiple_of(n * d.out_rows, d.out_rows), d.out_rows), :]
-
-            @pl.when(to != me)
-            def _():
-                remote(block, gbuf.at[j, slot], k_send, k_recv, to).start()
-
-            @pl.when(to == me)
-            def _():
-                gbuf[j, slot] = block[...]
-            return carry
-
-        lax.fori_loop(0, CHIPS, one, 0)
+    def hand_out(j, planes):
+        for plane in planes:
+            y, x = (ypos + plane // 2 * (1 - 2 * ypos), xpos + plane % 2 * (1 - 2 * xpos))
+            for n in range(4):
+                to = device(core * 2 + (zpos + n // 2) % 2, y, x, n % 2)
+                block = tbuf.at[j, pl.ds(pl.multiple_of((to - core * CHIPS) * d.out_rows, d.out_rows), d.out_rows), :]
+
+                @pl.when(to != me)
+                def _():
+                    remote(block, gbuf.at[j, slot], k_send, k_recv, to).start()
+
+                @pl.when(to == me)
+                def _():
+                    gbuf[j, slot] = block[...]
 
     def step(j, beta_prev):
         later = jnp.minimum(j, 1)
@@ -476,7 +475,7 @@
     lax.fori_loop(0, LANCZOS_STEPS, step, jnp.zeros((1, 1), jnp.float32))
 
     turn_result(LANCZOS_STEPS - 1)
-    hand_out(LANCZOS_STEPS - 1)
+    hand_out(LANCZOS_STEPS - 1, (3, 1, 2, 0))
     for n, part in enumerate((lv.at[0, pl.ds(0, 15), :, 0], lv.at[1, pl.ds(0, 15), :, 0, :, pl.ds(edge, d.bond - edge)],
                               lv.at[0, pl.ds(0, 15), :, 0, :, pl.ds(0, d.half)], lv.at[1, pl.ds(0, 15), :, 0, :, pl.ds(edge, d.half - edge)])):
         remote(part, part, l_send.at[n], l_recv.at[n, 0], me).wait_send()

time: 498 us -> 501 us (level)
  no operation moved by 1% of the time
where the time goes in v5:
time: 501 us; the launch traced here: 498 us
  Pallas kernels  483 us (96%)
  local copies, waits for them, and re-layouts  7.18 us (1%)
  other arithmetic  7.07 us (1%)
    pallas_call x1, Pallas kernels, device_body(): pl.pallas_call(functools.partial(lanczos_kernel, d), out_shape=(jax.Shape...  483 us

profile of v5, /device:TPU:15, one launch (start us, length us, event | category | flops | bytes accessed | tf_op | source)
XLA Modules:
  0.0 498.4 jit_solution(17301490946158638110)
XLA Ops:
  0.6 0.7 broadcast_compare_fusion
  1.3 0.8 broadcast_in_dim.21
  2.1 0.8 reshape.17.wexp
  2.9 2.4 broadcast_select_fusion.right
  5.3 483.4 %lanczos.1 = (f32[6,256,512]{2,1,0:T(8,128)}, f32[3,8,128]{2,1,0:T(8,128)}) custom-call(f32[8192,512]{1,0:T(8,128)} %bitcast.10, bf16[2,512,512]{2,1,0:T(8,128)(2,1)} %left.1, bf16[2,512,512]{2,1,0:T(8,128)(2,1)} %broadcast_select_fusion.right, bf16[2,16,256]{2,1,0:T(8,128)(2,1)} %reshape.17.wexp), custom_call_target="tpu_custom_call" | custom-call | tf_op jit(solution)/shard_map/lanczos/pallas_call | solution.py:532
  488.8 0.0 copy-start
  488.8 1.3 slice.9
  490.0 3.7 copy.11
  493.7 0.0 copy-done
  493.7 0.7 slice_reduce_fusion
  494.4 1.8 divide_bitcast_fusion
  496.2 2.2 pad_maximum_fusion
  (1 shorter events, 0.0 us)
Async XLA Ops:
  488.8 5.0 copy-start

commit v6 on v4

--- a/solution.py
+++ b/solution.py
@@ -23,23 +23,24 @@
 ALONG, ACROSS, FROM_COLUMN, FROM_SECOND, THIRD, DIAGONAL, RESULT, RESULT_OUT = range(8)
 RIGHT_SLOTS = (0, 1, 2, 3, 8, 9, 10, 11)
 SLOTS = (
-    ((1, 0, 1), (1, 0, 6), (0, 1, 1), (1, 0, 2), (1, 0, 3), (0, 1, 2), (1, 0, 4), (1, 0, 7), (0, 2, 2), (1, 0, 5), (0, 1, 3), (0, 1, 0), (0, 2, 0), (0, 3, 0), (0, 3, 1), (0, 2, 1), (0, 3, 2), (1, 0, 0), (3, 0, 3), (3, 0, 2), (2, 1, 2), (2, 1, 1), (0, 3, 3), (2, 1, 0), (2, 2, 0), (3, 0, 0), (2, 2, 1), (3, 1, 1), (0, 2, 3), (2, 2, 2), (3, 1, 0), (2, 3, 0), (3, 2, 0), (3, 0, 1), (2, 2, 3), (0, 3, 4), (2, 3, 1), (2, 3, 2), (0, 3, 5), (3, 3, 0), (0, 1, 4), (0, 2, 4), (0, 1, 5), (2, 1, 3), (3, 2, 1), (3, 2, 3), (3, 3, 1), (0, 2, 5), (0, 1, 6), (2, 3, 3), (0, 3, 7), (3, 3, 2), (3, 1, 3), (0, 3, 6), (3, 2, 2), (0, 2, 6), (3, 1, 2), (0, 2, 7), (3, 3, 3), (5, 0, 0), (3, 0, 4), (4, 0, 1), (4, 0, 0), (3, 0, 5),),
-    ((6, 0, 0), (2, 3, 4), (4, 0, 2), (3, 0, 6), (5, 0, 1),),
-    ((2, 2, 4), (2, 1, 4), (2, 1, 5), (5, 0, 2), (2, 2, 5),),
-    ((5, 0, 3), (0, 1, 7), (3, 3, 4), (4, 0, 3), (2, 3, 5), (2, 1, 6), (2, 2, 6),),
-    (),
-    ((4, 0, 4), (2, 3, 6), (3, 1, 4), (2, 2, 7), (3, 2, 4),),
-    ((3, 3, 5), (3, 2, 5), (3, 1, 5), (2, 3, 7), (2, 1, 7),),
-    ((3, 1, 6), (3, 3, 6),),
-    ((4, 0, 5), (3, 2, 6), (3, 0, 7), (4, 0, 6), (5, 0, 4), (3, 3, 7), (3, 2, 7),),
-    ((5, 0, 5), (3, 1, 7),),
-    ((4, 0, 7), (5, 0, 6),),
-    ((5, 0, 7), (7, 0, 0),),
+    ((0, 1, 0), (0, 1, 1), (1, 0, 2), (0, 2, 0), (1, 0, 5), (1, 0, 3), (1, 0, 6), (1, 0, 0), (0, 3, 0), (3, 0, 2), (0, 2, 1), (0, 1, 3), (1, 0, 4), (0, 3, 1), (1, 0, 7), (0, 1, 2), (1, 0, 1), (0, 3, 3), (2, 1, 0), (2, 2, 0), (0, 2, 3), (0, 3, 2), (2, 1, 1), (3, 0, 0), (2, 3, 0), (3, 1, 0), (2, 2, 1), (0, 2, 2), (0, 1, 4), (3, 0, 1), (2, 1, 3), (3, 2, 0), (2, 3, 1), (2, 2, 2), (2, 2, 3), (2, 1, 2), (4, 0, 0), (0, 2, 5), (0, 3, 4), (0, 2, 4), (0, 1, 5), (0, 1, 6), (0, 1, 7), (3, 3, 0), (2, 3, 3), (3, 1, 1), (3, 2, 1), (0, 2, 6), (2, 3, 2), (4, 0, 1), (3, 3, 1), (0, 3, 6), (3, 2, 2), (3, 1, 2), (0, 3, 5), (0, 2, 7), (0, 3, 7), (3, 2, 3), (3, 3, 2), (3, 0, 3), (5, 0, 0), (3, 3, 3), (4, 0, 3), (3, 1, 3), (3, 0, 4),),
+    ((6, 0, 0), (2, 2, 4), (5, 0, 1), (3, 0, 6), (2, 1, 4), (4, 0, 2),),
+    ((2, 2, 6), (5, 0, 2), (2, 1, 6),),
+    ((2, 2, 5), (5, 0, 3), (3, 2, 4), (2, 3, 4),),
+    ((2, 1, 5), (3, 0, 5), (3, 1, 4),),
+    ((2, 3, 5), (3, 2, 5), (2, 3, 6),),
+    ((2, 2, 7), (3, 3, 4), (2, 1, 7), (3, 1, 5),),
+    ((3, 3, 5), (2, 3, 7), (3, 2, 6), (3, 1, 6), (3, 3, 6),),
+    ((3, 0, 7), (3, 1, 7), (3, 2, 7), (4, 0, 5), (5, 0, 4), (4, 0, 4),),
+    ((3, 3, 7), (5, 0, 5),),
+    ((4, 0, 6), (5, 0, 6),),
+    ((4, 0, 7), (5, 0, 7), (7, 0, 0),),
     (),
     (),
     (),
     (),
 )
+RESULT_EARLY = 9
 
 
 class Dims:
@@ -196,7 +197,7 @@
         elif kind == RESULT:
             turn_result(j - 1)
         elif kind == RESULT_OUT:
-            hand_out(j - 1)
+            hand_out(j - 1, 0, RESULT_EARLY)
 
     for ch in range(CHUNKS):
         for h in range(2):
@@ -343,10 +344,10 @@
                     for q in range(n * TILE_PARTS, (n + 1) * TILE_PARTS) for bh in range(2)]
             tbuf[j, :, n * wide:(n + 1) * wide] = jnp.concatenate(rows, axis=0).T
 
-    def hand_out(j):
-        def one(n, carry):
+    def hand_out(j, first, last):
+        for n in range(first, last):
             to = core * CHIPS + n
-            block = tbuf.at[j, pl.ds(pl.multiple_of(n * d.out_rows, d.out_rows), d.out_rows), :]
+            block = tbuf.at[j, n * d.out_rows:(n + 1) * d.out_rows, :]
 
             @pl.when(to != me)
             def _():
@@ -355,9 +356,6 @@
             @pl.when(to == me)
             def _():
                 gbuf[j, slot] = block[...]
-            return carry
-
-        lax.fori_loop(0, CHIPS, one, 0)
 
     def step(j, beta_prev):
         later = jnp.minimum(j, 1)
@@ -375,15 +373,15 @@
 
             @pl.when(j == 0)
             def _():
-                @pl.when(t == 4)
+                @pl.when(t == 5)
                 def _():
                     l_last(False)
 
-                @pl.when(t == 12)
+                @pl.when(t == 13)
                 def _():
                     l_last(True)
 
-                @pl.when(t % 4 == 0)
+                @pl.when(t % 4 == 1)
                 def _():
                     lax.fori_loop(0, 4, l_fill, first_grp)
 
@@ -437,27 +435,33 @@
         sig[:, :d.half] = t
         tt = jnp.sum(t * t, keepdims=True)
         tv = jnp.sum(t * v, keepdims=True)
-        tile_row = lax.broadcasted_iota(jnp.int32, (8, 128), 0)
-        tile = jnp.zeros((8, 128), jnp.float32)
+        at_lane = lax.broadcasted_iota(jnp.int32, (1, 128), 1)
+        line = jnp.zeros((1, 128), jnp.float32)
         for n, value in enumerate((sv, vv, tt, tv, guess)):
-            tile = jnp.where(tile_row == n, value, tile)
-        scs[...] = tile
-        scr[me] = tile
+            line = jnp.where(at_lane == n, value, line)
+        scs[...] = line
+        scr[me] = line
 
         def tell(n, carry):
             remote(scs, scr.at[me], s_send, s_recv, (me + n) % DEVS).start()
             return carry
 
         lax.fori_loop(1, DEVS, tell, 0)
+
+        @pl.when(j > 0)
+        def _():
+            hand_out(j - 1, RESULT_EARLY, CHIPS)
+
         heard = scr.at[pl.ds(0, DEVS - 1)]
         remote(heard, heard, s_send, s_recv, me).wait()
-        alpha = jnp.sum(scr[:, 0, :], axis=0, keepdims=True) / d.vec_size
-        off = alpha - scr[:, 4, :]
-        square = scr[:, 2, :] - 2.0 * off * scr[:, 3, :] + off * off * scr[:, 1, :]
+        told = scr[:, 0, :]
+        alpha = jnp.sum(told[:, 0:1], axis=0, keepdims=True) / d.vec_size
+        off = alpha - told[:, 4:5]
+        square = told[:, 2:3] - 2.0 * off * told[:, 3:4] + off * off * told[:, 1:2]
         beta = jnp.sqrt(jnp.sum(square, axis=0, keepdims=True) / d.vec_size)
-        info[0, pl.ds(j, 1), :] = alpha
-        info[1, pl.ds(j, 1), :] = beta
-        vnew = (sig[:, :d.half] - (alpha[:, 0:1] - guess) * vcur[...]) / beta[:, 0:1]
+        info[0, pl.ds(j, 1), :] = jnp.broadcast_to(alpha, (1, 128))
+        info[1, pl.ds(j, 1), :] = jnp.broadcast_to(beta, (1, 128))
+        vnew = (sig[:, :d.half] - (alpha - guess) * vcur[...]) / beta
         vprev[...] = vcur[...]
         vcur[...] = vnew
         vb = vnew.astype(jnp.bfloat16)
@@ -470,13 +474,13 @@
                     for q in range(d.pair):
                         uv[ch, q // 2, at, q % 2 * d.chunk:(q % 2 + 1) * d.chunk] = \
                             vb[(bh * d.pair + q) * d.sub:(bh * d.pair + q + 1) * d.sub, ch * d.chunk:(ch + 1) * d.chunk]
-        return beta[:, 0:1]
+        return beta
 
 
     lax.fori_loop(0, LANCZOS_STEPS, step, jnp.zeros((1, 1), jnp.float32))
 
     turn_result(LANCZOS_STEPS - 1)
-    hand_out(LANCZOS_STEPS - 1)
+    hand_out(LANCZOS_STEPS - 1, 0, CHIPS)
     for n, part in enumerate((lv.at[0, pl.ds(0, 15), :, 0], lv.at[1, pl.ds(0, 15), :, 0, :, pl.ds(edge, d.bond - edge)],
                               lv.at[0, pl.ds(0, 15), :, 0, :, pl.ds(0, d.half)], lv.at[1, pl.ds(0, 15), :, 0, :, pl.ds(edge, d.half - edge)])):
         remote(part, part, l_send.at[n], l_recv.at[n, 0], me).wait_send()
@@ -550,8 +554,8 @@
                 pltpu.VMEM((d.rows, d.half), f32),
                 pltpu.VMEM((LANCZOS_STEPS, d.half, bond), f32),
                 pltpu.VMEM((LANCZOS_STEPS, CHIPS, d.out_rows, bond), f32),
-                pltpu.VMEM((8, 128), f32),
-                pltpu.VMEM((DEVS, 8, 128), f32),
+                pltpu.VMEM((1, 128), f32),
+                pltpu.VMEM((DEVS, 1, 128), f32),
                 pltpu.VMEM((2, 8, 128), f32),
                 dma((3, 2)), dma((8, d.lane_tiles)), dma((CHUNKS, 2)), dma((CHUNKS, 2)), dma((2,)), dma((2,)), dma((2,)), dma((2,)),
                 dma((4,)), dma((4, CHIPS)), dma, dma((CHIPS,)), dma((PIECES,)), dma((PIECES, CHIPS)),

time: 498 us -> 473 us (0.950)
  Pallas kernels: 482 us -> 458 us
    pallas_call x1, Pallas kernels: 482 us -> 458 us  [device_body(): pl.pallas_call(functools.partial(lanczos_kernel, d), out_shape=(jax.Shape...]
where the time goes in v6:
time: 473 us
  Pallas kernels  458 us (97%)
  local copies, waits for them, and re-layouts  7.18 us (2%)
  other arithmetic  7.07 us (1%)
    pallas_call x1, Pallas kernels, device_body(): pl.pallas_call(functools.partial(lanczos_kernel, d), out_shape=(jax.Shape...  458 us

profile of v6, /device:TPU:15, one launch (start us, length us, event | category | flops | bytes accessed | tf_op | source)
XLA Modules:
  0.0 472.7 jit_solution(1015940322684225005)
XLA Ops:
  0.6 0.7 broadcast_compare_fusion
  1.3 0.8 broadcast_in_dim.21
  2.1 0.8 reshape.17.wexp
  2.9 2.4 broadcast_select_fusion.right
  5.3 457.7 %lanczos.1 = (f32[6,256,512]{2,1,0:T(8,128)}, f32[3,8,128]{2,1,0:T(8,128)}) custom-call(f32[8192,512]{1,0:T(8,128)} %bitcast.10, bf16[2,512,512]{2,1,0:T(8,128)(2,1)} %left.1, bf16[2,512,512]{2,1,0:T(8,128)(2,1)} %broadcast_select_fusion.right, bf16[2,16,256]{2,1,0:T(8,128)(2,1)} %reshape.17.wexp), custom_call_target="tpu_custom_call" | custom-call | tf_op jit(solution)/shard_map/lanczos/pallas_call | solution.py:537
  463.1 0.0 copy-start
  463.1 1.3 slice.9
  464.3 3.7 copy.11
  468.0 0.0 copy-done
  468.0 0.7 slice_reduce_fusion
  468.7 1.8 divide_bitcast_fusion
  470.5 2.2 pad_maximum_fusion
  (1 shorter events, 0.0 us)
Async XLA Ops:
  463.1 5.0 %copy-start = (f32[3,8,128]{2,1,0:T(8,128)S(1)}, f32[3,8,128]{2,1,0:T(8,128)}, u32[]{:S(2)}) copy-start(f32[3,8,128]{2,1,0:T(8,128)} %get-tuple-element.5) | copy-start | bytes 36868

commit v7 on v6

--- a/solution.py
+++ b/solution.py
@@ -20,7 +20,7 @@
 QUARTERS = 4
 PIECES = CHUNKS * QUARTERS
 
-ALONG, ACROSS, FROM_COLUMN, FROM_SECOND, THIRD, DIAGONAL, RESULT, RESULT_OUT = range(8)
+ALONG, ACROSS, FROM_COLUMN, FROM_SECOND, THIRD, DIAGONAL, RESULT, RESULT_OUT, RESULT_PUT = range(9)
 RIGHT_SLOTS = (0, 1, 2, 3, 8, 9, 10, 11)
 SLOTS = (
     ((0, 1, 0), (0, 1, 1), (1, 0, 2), (0, 2, 0), (1, 0, 5), (1, 0, 3), (1, 0, 6), (1, 0, 0), (0, 3, 0), (3, 0, 2), (0, 2, 1), (0, 1, 3), (1, 0, 4), (0, 3, 1), (1, 0, 7), (0, 1, 2), (1, 0, 1), (0, 3, 3), (2, 1, 0), (2, 2, 0), (0, 2, 3), (0, 3, 2), (2, 1, 1), (3, 0, 0), (2, 3, 0), (3, 1, 0), (2, 2, 1), (0, 2, 2), (0, 1, 4), (3, 0, 1), (2, 1, 3), (3, 2, 0), (2, 3, 1), (2, 2, 2), (2, 2, 3), (2, 1, 2), (4, 0, 0), (0, 2, 5), (0, 3, 4), (0, 2, 4), (0, 1, 5), (0, 1, 6), (0, 1, 7), (3, 3, 0), (2, 3, 3), (3, 1, 1), (3, 2, 1), (0, 2, 6), (2, 3, 2), (4, 0, 1), (3, 3, 1), (0, 3, 6), (3, 2, 2), (3, 1, 2), (0, 3, 5), (0, 2, 7), (0, 3, 7), (3, 2, 3), (3, 3, 2), (3, 0, 3), (5, 0, 0), (3, 3, 3), (4, 0, 3), (3, 1, 3), (3, 0, 4),),
@@ -29,7 +29,7 @@
     ((2, 2, 5), (5, 0, 3), (3, 2, 4), (2, 3, 4),),
     ((2, 1, 5), (3, 0, 5), (3, 1, 4),),
     ((2, 3, 5), (3, 2, 5), (2, 3, 6),),
-    ((2, 2, 7), (3, 3, 4), (2, 1, 7), (3, 1, 5),),
+    ((2, 2, 7), (3, 3, 4), (2, 1, 7), (3, 1, 5), (8, 0, 0),),
     ((3, 3, 5), (2, 3, 7), (3, 2, 6), (3, 1, 6), (3, 3, 6),),
     ((3, 0, 7), (3, 1, 7), (3, 2, 7), (4, 0, 5), (5, 0, 4), (4, 0, 4),),
     ((3, 3, 7), (5, 0, 5),),
@@ -58,12 +58,14 @@
         self.group_terms = 4 * CORES * terms_dev
         self.vec_size = bond * pair * bond
         self.lane = min(bond, 128)
+        self.wide = TILE_PARTS * self.slab
         self.lane_tiles = bond // self.lane
 
 
-def lanczos_kernel(d, psi, left, right, wexp, out, info, lv, rv, wv, kw, uv, ps, yst, zst, sig, part, vcur, vprev, tbuf, gbuf, scs, scr, nbuf,
+def lanczos_kernel(d, psi, left, right, pair_ops, flags, out, alphas, betas, lv, rv, rs, wv, kw, uv, ps, yst, zst, sig, part, vcur, vprev, tbuf, gbuf,
+                   scs, scr, nbuf,
                    loc_sem, psi_sem, d2d_sem, d2d_recv, rw_send, rw_recv, fw_send, fw_recv, l_send, l_recv, f_send, f_recv, u_send, u_recv,
-                   p_send, p_recv, s_send, s_recv, k_send, k_recv, n_send, n_recv, o_sem):
+                   p_send, p_recv, s_send, s_recv, k_send, k_recv, n_send, n_recv, o_sem, first_sem):
     me = lax.axis_index(AXIS_NAME)
     core = me % 2
     xpos = (me // 2) % 2
@@ -198,6 +200,10 @@
             turn_result(j - 1)
         elif kind == RESULT_OUT:
             hand_out(j - 1, 0, RESULT_EARLY)
+        elif kind == RESULT_PUT:
+            @pl.when(j > 1)
+            def _():
+                put_out(j - 2)
 
     for ch in range(CHUNKS):
         for h in range(2):
@@ -208,6 +214,8 @@
             remote(theirs, lv.at[ch, slot, core, :, :, pl.ds(h * d.half, d.half)], d2d_sem.at[ch, h], d2d_recv.at[ch, h], partner).start()
             pltpu.make_async_copy(mine, lv.at[ch, slot, core, :, :, pl.ds(h * d.half, d.half)], loc_sem.at[ch, h]).start()
 
+    all_right = pltpu.make_async_copy(right, rs, loc_sem.at[2, 0])
+    all_right.start()
     psi_rows = d.half * d.pair // 8
     psi_copies = [pltpu.make_async_copy(psi.at[pl.ds(pl.multiple_of(core * d.half * d.pair + n * psi_rows, psi_rows), psi_rows),
                                                pl.ds(c * d.lane, d.lane)],
@@ -216,18 +224,38 @@
     for copy in psi_copies:
         copy.start()
 
+    first_rows = d.out_rows * d.pair
+    first_copies = [pltpu.make_async_copy(psi.at[pl.ds(pl.multiple_of(me * first_rows, first_rows), first_rows), pl.ds(c * d.wide, d.wide)],
+                                          tbuf.at[LANCZOS_STEPS - 1, c], first_sem.at[c]) for c in range(d.bond // d.wide)]
+    for copy in first_copies:
+        copy.start()
+
+    spread = (lax.broadcasted_iota(jnp.int32, (d.pair, d.prod), 1) // d.sub == lax.broadcasted_iota(jnp.int32, (d.pair, d.prod), 0))
+    spread = spread.astype(jnp.float32).astype(jnp.bfloat16)
+    for t in range(d.terms_dev):
+        wv[slot, core, t] = jnp.dot(pair_ops[t], spread, preferred_element_type=jnp.float32).astype(jnp.bfloat16)
+    all_right.wait()
+    some_rows = d.bond // 8
+
+    def one_sided(i, carry):
+        at = pl.ds(pl.multiple_of(i * some_rows, some_rows), some_rows)
+        row = lax.broadcasted_iota(jnp.int32, (some_rows, d.bond), 0) + i * some_rows
+        one = jnp.where(row == lax.broadcasted_iota(jnp.int32, (some_rows, d.bond), 1), 1.0, 0.0)
+        for t in range(d.terms_dev):
+            rs[t, at, :] = jnp.where(flags[t] == 1, rs[t, at, :].astype(jnp.float32), one).astype(jnp.bfloat16)
+        return carry
+
+    lax.fori_loop(0, 8, one_sided, 0)
+
     def right_rows(s):
-        return right.at[:, pl.ds(pl.multiple_of(s * d.slab, d.slab), d.slab), :]
-
-    own_right = pltpu.make_async_copy(right_rows(slot), rv.at[slot, core], loc_sem.at[2, 0])
-    own_pair = pltpu.make_async_copy(wexp, wv.at[slot, core], loc_sem.at[2, 1])
-    own_right.start()
-    own_pair.start()
+        return rs.at[:, pl.ds(pl.multiple_of(s * d.slab, d.slab), d.slab), :]
+
+    rv[slot, core] = rs[:, pl.ds(pl.multiple_of(slot * d.slab, d.slab), d.slab), :]
     for n in range(1, CHIPS):
         chip = (me // 2 + n) % CHIPS
         to = chip_slot(chip // 4, chip // 2 % 2, chip % 2)
         remote(right_rows(to), rv.at[slot, core], rw_send.at[0], rw_recv.at[0], chip * 2 + core).start()
-        remote(wexp, wv.at[slot, core], rw_send.at[1], rw_recv.at[1], chip * 2 + core).start()
+        remote(wv.at[slot, core], wv.at[slot, core], rw_send.at[1], rw_recv.at[1], chip * 2 + core).start()
 
     for ch in range(CHUNKS):
         for h in range(2):
@@ -253,8 +281,14 @@
     to_partner.start()
     to_partner.wait()
     norm = jnp.sqrt((nbuf[0] + nbuf[1])[0:1, :] / d.vec_size)
-    info[2] = jnp.broadcast_to(norm, (8, 128))
     norm_one = norm[:, 0:1]
+    for copy in first_copies:
+        copy.wait()
+    tbuf[LANCZOS_STEPS - 1] = tbuf[LANCZOS_STEPS - 1] / norm_one[None]
+    first_out = [pltpu.make_async_copy(tbuf.at[LANCZOS_STEPS - 1, c], out.at[0, :, pl.ds(c * d.wide, d.wide)], first_sem.at[c])
+                 for c in range(d.bond // d.wide)]
+    for copy in first_out:
+        copy.start()
 
     def place(q):
         tiles = [(ps[c, pl.ds(q, d.half, stride=d.pair), :] / norm_one).T for c in range(d.lane_tiles)]
@@ -274,8 +308,6 @@
         return carry
 
     lax.fori_loop(0, d.pair // 4, start_vector, 0)
-    own_right.wait()
-    own_pair.wait()
     fifteen = rv.at[pl.ds(0, CHIPS - 1), 0]
     fifteen_w = wv.at[pl.ds(0, CHIPS - 1), 0]
     remote(fifteen, fifteen, rw_send.at[0], rw_recv.at[0], me).wait()
@@ -309,6 +341,8 @@
     l_event(5)
     l_event(6)
     vprev[...] = jnp.zeros_like(vprev)
+    for copy in first_out:
+        copy.wait()
 
     def right_product(grp, ch, qb):
         r_all = rv[pl.ds(grp * 4, 4)].reshape(d.group_terms * d.slab, d.bond)
@@ -338,24 +372,48 @@
         sig[...] += jnp.dot(zst[...], l_all, preferred_element_type=jnp.float32)
 
     def turn_result(j):
-        wide = TILE_PARTS * d.slab
         for n in range(d.pair // TILE_PARTS):
             rows = [vcur[(bh * d.pair + q) * d.sub:(bh * d.pair + q + 1) * d.sub, :]
                     for q in range(n * TILE_PARTS, (n + 1) * TILE_PARTS) for bh in range(2)]
-            tbuf[j, :, n * wide:(n + 1) * wide] = jnp.concatenate(rows, axis=0).T
+            tbuf[j, n] = jnp.concatenate(rows, axis=0).T
 
     def hand_out(j, first, last):
         for n in range(first, last):
             to = core * CHIPS + n
-            block = tbuf.at[j, n * d.out_rows:(n + 1) * d.out_rows, :]
+            block = tbuf.at[j, :, pl.ds(n * d.out_rows, d.out_rows), :]
 
             @pl.when(to != me)
             def _():
-                remote(block, gbuf.at[j, slot], k_send, k_recv, to).start()
+                remote(block, gbuf.at[j, slot], k_send.at[j], k_recv.at[j], to).start()
 
             @pl.when(to == me)
             def _():
                 gbuf[j, slot] = block[...]
+
+    sends_self = me // CHIPS == core
+    lanes = lax.broadcasted_iota(jnp.int32, (d.out_rows, d.wide), 1) // d.slab
+
+    def put_out(j):
+        @pl.when(sends_self)
+        def _():
+            some = gbuf.at[j, pl.ds(0, CHIPS - 1)]
+            remote(some, some, k_send.at[j], k_recv.at[j], me).wait()
+
+        @pl.when(jnp.logical_not(sends_self))
+        def _():
+            remote(gbuf.at[j], gbuf.at[j], k_send.at[j], k_recv.at[j], me).wait()
+
+        for ct in range(CHIPS // TILE_PARTS):
+            for qt in range(d.pair // TILE_PARTS):
+                src = [gbuf[j, ct * TILE_PARTS + c, qt] for c in range(TILE_PARTS)]
+                for q in range(TILE_PARTS):
+                    tile = jnp.zeros((d.out_rows, d.wide), jnp.float32)
+                    for c in range(TILE_PARTS):
+                        shift = (c - q) % TILE_PARTS * d.slab
+                        moved = pltpu.roll(src[c], shift, 1) if shift else src[c]
+                        tile = jnp.where(lanes == c, moved, tile)
+                    tbuf[j, ct, pl.ds(qt * TILE_PARTS + q, d.out_rows, stride=d.pair), :] = tile
+            pltpu.make_async_copy(tbuf.at[j, ct], out.at[1 + j, :, pl.ds(ct * d.wide, d.wide)], o_sem.at[j, ct]).start()
 
     def step(j, beta_prev):
         later = jnp.minimum(j, 1)
@@ -459,8 +517,6 @@
         off = alpha - told[:, 4:5]
         square = told[:, 2:3] - 2.0 * off * told[:, 3:4] + off * off * told[:, 1:2]
         beta = jnp.sqrt(jnp.sum(square, axis=0, keepdims=True) / d.vec_size)
-        info[0, pl.ds(j, 1), :] = jnp.broadcast_to(alpha, (1, 128))
-        info[1, pl.ds(j, 1), :] = jnp.broadcast_to(beta, (1, 128))
         vnew = (sig[:, :d.half] - (alpha - guess) * vcur[...]) / beta
         vprev[...] = vcur[...]
         vcur[...] = vnew
@@ -474,6 +530,8 @@
                     for q in range(d.pair):
                         uv[ch, q // 2, at, q % 2 * d.chunk:(q % 2 + 1) * d.chunk] = \
                             vb[(bh * d.pair + q) * d.sub:(bh * d.pair + q + 1) * d.sub, ch * d.chunk:(ch + 1) * d.chunk]
+        alphas[j] = alpha[0, 0]
+        betas[j] = beta[0, 0]
         return beta
 
 
@@ -490,58 +548,31 @@
         for h in range(2):
             theirs = left.at[:, pl.ds(0, d.chunk), pl.ds(0, d.half)]
             remote(theirs, lv.at[ch, slot, core, :, :, pl.ds(h * d.half, d.half)], d2d_sem.at[ch, h], d2d_recv.at[ch, h], partner).wait_send()
-
-    sends_self = me // CHIPS == core
-
-    @pl.when(sends_self)
-    def _():
-        some = gbuf.at[:, pl.ds(0, CHIPS - 1)]
-        remote(some, some, k_send, k_recv, me).wait()
-
-    @pl.when(jnp.logical_not(sends_self))
-    def _():
-        remote(gbuf, gbuf, k_send, k_recv, me).wait()
-
-    wide = TILE_PARTS * d.slab
-    lanes = lax.broadcasted_iota(jnp.int32, (d.out_rows, wide), 1) // d.slab
-
-    def put_out(j, carry):
-        for ct in range(CHIPS // TILE_PARTS):
-            for qt in range(d.pair // TILE_PARTS):
-                src = [gbuf[j, ct * TILE_PARTS + c, :, qt * wide:(qt + 1) * wide] for c in range(TILE_PARTS)]
-                for q in range(TILE_PARTS):
-                    tile = jnp.zeros((d.out_rows, wide), jnp.float32)
-                    for c in range(TILE_PARTS):
-                        shift = (c - q) % TILE_PARTS * d.slab
-                        moved = pltpu.roll(src[c], shift, 1) if shift else src[c]
-                        tile = jnp.where(lanes == c, moved, tile)
-                    at = (qt * TILE_PARTS + q) * d.out_rows
-                    tbuf[j, at:at + d.out_rows, ct * wide:(ct + 1) * wide] = tile
-        pltpu.make_async_copy(tbuf.at[j], out.at[j], o_sem).start()
-        return carry
-
-    lax.fori_loop(0, LANCZOS_STEPS, put_out, 0)
-    pltpu.make_async_copy(tbuf, out, o_sem).wait()
+    put_out(LANCZOS_STEPS - 2)
+    put_out(LANCZOS_STEPS - 1)
+    for j in range(LANCZOS_STEPS):
+        for c in range(d.bond // d.wide):
+            pltpu.make_async_copy(tbuf.at[j, c], out.at[1 + j, :, pl.ds(c * d.wide, d.wide)], o_sem.at[j, c]).wait()
 
 
 def solution(mesh):
     def device_body(wavefunction, left_loc, pair_loc, right_loc, flag_loc):
         bond, pair = wavefunction.shape[0], wavefunction.shape[1]
         d = Dims(bond, pair, left_loc.shape[0])
-        eye = jnp.eye(bond, dtype=jnp.bfloat16)
-        right_used = jnp.where((flag_loc == 1)[:, None, None], right_loc, eye)
-        pair_wide = jnp.repeat(pair_loc, d.sub, axis=2)
         bf16, f32 = jnp.bfloat16, jnp.float32
         dma = pltpu.SemaphoreType.DMA
         any_space = pl.BlockSpec(memory_space=pl.ANY)
-        rows_out, info = pl.pallas_call(
+        smem = pl.BlockSpec(memory_space=pltpu.SMEM)
+        scalars = jax.ShapeDtypeStruct((LANCZOS_STEPS,), f32)
+        krylov, alphas, betas = pl.pallas_call(
             functools.partial(lanczos_kernel, d),
-            out_shape=(jax.ShapeDtypeStruct((LANCZOS_STEPS, d.half, bond), f32), jax.ShapeDtypeStruct((3, 8, 128), f32)),
-            in_specs=[any_space] * 4,
-            out_specs=(any_space, pl.BlockSpec(memory_space=pltpu.VMEM)),
+            out_shape=(jax.ShapeDtypeStruct((LANCZOS_STEPS + 1, d.out_rows * pair, bond), f32), scalars, scalars),
+            in_specs=[any_space] * 3 + [pl.BlockSpec(memory_space=pltpu.VMEM), smem],
+            out_specs=(any_space, smem, smem),
             scratch_shapes=[
                 pltpu.VMEM((CHUNKS, CHIPS, CORES, d.terms_dev, d.chunk, bond), bf16),
                 pltpu.VMEM((CHIPS, CORES, d.terms_dev, d.slab, bond), bf16),
+                pltpu.VMEM((d.terms_dev, bond, bond), bf16),
                 pltpu.VMEM((CHIPS, CORES, d.terms_dev, pair, d.prod), bf16),
                 pltpu.VMEM((CHIPS, CORES, d.terms_dev, d.prod, d.prod), bf16),
                 pltpu.VMEM((CHUNKS, pair // 2, bond, 2 * d.chunk), bf16),
@@ -552,22 +583,19 @@
                 pltpu.VMEM((d.rows, d.half), f32),
                 pltpu.VMEM((d.rows, d.half), f32),
                 pltpu.VMEM((d.rows, d.half), f32),
-                pltpu.VMEM((LANCZOS_STEPS, d.half, bond), f32),
-                pltpu.VMEM((LANCZOS_STEPS, CHIPS, d.out_rows, bond), f32),
+                pltpu.VMEM((LANCZOS_STEPS, bond // d.wide, d.half, d.wide), f32),
+                pltpu.VMEM((LANCZOS_STEPS, CHIPS, bond // d.wide, d.out_rows, d.wide), f32),
                 pltpu.VMEM((1, 128), f32),
                 pltpu.VMEM((DEVS, 1, 128), f32),
                 pltpu.VMEM((2, 8, 128), f32),
                 dma((3, 2)), dma((8, d.lane_tiles)), dma((CHUNKS, 2)), dma((CHUNKS, 2)), dma((2,)), dma((2,)), dma((2,)), dma((2,)),
                 dma((4,)), dma((4, CHIPS)), dma, dma((CHIPS,)), dma((PIECES,)), dma((PIECES, CHIPS)),
-                dma, dma, dma, dma, dma, dma, dma, dma, dma,
+                dma, dma, dma, dma, dma((LANCZOS_STEPS,)), dma((LANCZOS_STEPS,)), dma, dma, dma((LANCZOS_STEPS, bond // d.wide)), dma((bond // d.wide,)),
             ],
             compiler_params=pltpu.CompilerParams(has_side_effects=True, vmem_limit_bytes=67043328),
             name='lanczos',
-        )(wavefunction.reshape(bond * pair, bond), left_loc, right_used, pair_wide)
-        row_start = lax.axis_index(AXIS_NAME) * d.out_rows
-        first = lax.dynamic_slice_in_dim(wavefunction, row_start, d.out_rows, axis=0) / info[2, 0, 0]
-        later = rows_out.reshape(LANCZOS_STEPS, pair, d.out_rows, bond).transpose(0, 2, 1, 3)
-        return jnp.concatenate([first[None], later]), info[0, :LANCZOS_STEPS, 0], info[1, :LANCZOS_STEPS, 0]
+        )(wavefunction.reshape(bond * pair, bond), left_loc, right_loc, pair_loc, flag_loc)
+        return krylov.reshape(LANCZOS_STEPS + 1, d.out_rows, pair, bond), alphas, betas
 
     return jax.shard_map(device_body, mesh=mesh, in_specs=(P(), P(AXIS_NAME), P(AXIS_NAME), P(AXIS_NAME), P(AXIS_NAME)),
                          out_specs=(P(None, AXIS_NAME), P(), P()), check_vma=False)

time: 473 us -> 470 us (level)
  other arithmetic: 7.07 us -> 0 us
  Pallas kernels: 458 us -> 463 us
    pallas_call x1, Pallas kernels: 458 us -> 463 us  [device_body(): pl.pallas_call(functools.partial(lanczos_kernel, d), out_shape=(jax.Shape...]
    unnamed x2 -> x7, local copies, waits for them, and re-layouts: 0.01 us -> 5.61 us
where the time goes in v7:
time: 470 us
  Pallas kernels  463 us (99%)
  local copies, waits for them, and re-layouts  5.61 us (1%)
    pallas_call x1, Pallas kernels, device_body(): pl.pallas_call(functools.partial(lanczos_kernel, d), out_shape=(jax.Shape...  463 us

profile of v7, /device:TPU:15, one launch (start us, length us, event | category | flops | bytes accessed | tf_op | source)
XLA Modules:
  0.0 469.8 jit_solution(6936555375093314070)
XLA Ops:
  0.6 463.5 %lanczos.1 = (f32[7,256,512]{2,1,0:T(8,128)}, f32[6]{0:T(128)}, f32[6]{0:T(128)}) custom-call(f32[8192,512]{1,0:T(8,128)} %bitcast.2, bf16[2,512,512]{2,1,0:T(8,128)(2,1)} %left.1, bf16[2,512,512]{2,1,0:T(8,128)(2,1)} %right.1, bf16[2,16,16]{2,1,0:T(8,128)(2,1)} %pair_ops.1, s32[2]{0:T(128)} %flags.1), custom_call_target="tpu_custom_call" | custom-call | tf_op jit(solution)/shard_map/lanczos/pallas_call | solution.py:567
  464.1 0.0 copy-start.1
  464.1 0.0 copy-start
  464.1 4.6 copy.11
  468.7 0.0 copy-done.1
  468.7 0.5 copy.12
  469.2 0.0 copy-done
  469.2 0.5 copy.13
Async XLA Ops:
  464.1 4.6 copy-start.1
  464.1 5.1 %copy-start = (f32[6]{0:T(128)S(1)}, f32[6]{0:T(128)}, u32[]{:S(2)}) copy-start(f32[6]{0:T(128)} %get-tuple-element.14) | copy-start | bytes 76

commit v8 on v7

--- a/solution.py
+++ b/solution.py
@@ -40,7 +40,7 @@
     (),
     (),
 )
-RESULT_EARLY = 9
+RESULT_EARLY, RESULT_LATE = (3, 1, 2), (0,)
 
 
 class Dims:
@@ -62,7 +62,7 @@
         self.lane_tiles = bond // self.lane
 
 
-def lanczos_kernel(d, psi, left, right, pair_ops, flags, out, alphas, betas, lv, rv, rs, wv, kw, uv, ps, yst, zst, sig, part, vcur, vprev, tbuf, gbuf,
+def lanczos_kernel(d, psi, left, right, pair_ops, flags, out, first, alphas, betas, lv, rv, rs, wv, kw, uv, ps, yst, zst, sig, part, vcur, vprev, tbuf, gbuf,
                    scs, scr, nbuf,
                    loc_sem, psi_sem, d2d_sem, d2d_recv, rw_send, rw_recv, fw_send, fw_recv, l_send, l_recv, f_send, f_recv, u_send, u_recv,
                    p_send, p_recv, s_send, s_recv, k_send, k_recv, n_send, n_recv, o_sem, first_sem):
@@ -197,9 +197,9 @@
         elif kind == DIAGONAL:
             g.last(True)
         elif kind == RESULT:
-            turn_result(j - 1)
+            turn_result(j - 1, vcur)
         elif kind == RESULT_OUT:
-            hand_out(j - 1, 0, RESULT_EARLY)
+            hand_out(j - 1, RESULT_EARLY)
         elif kind == RESULT_PUT:
             @pl.when(j > 1)
             def _():
@@ -230,33 +230,6 @@
     for copy in first_copies:
         copy.start()
 
-    spread = (lax.broadcasted_iota(jnp.int32, (d.pair, d.prod), 1) // d.sub == lax.broadcasted_iota(jnp.int32, (d.pair, d.prod), 0))
-    spread = spread.astype(jnp.float32).astype(jnp.bfloat16)
-    for t in range(d.terms_dev):
-        wv[slot, core, t] = jnp.dot(pair_ops[t], spread, preferred_element_type=jnp.float32).astype(jnp.bfloat16)
-    all_right.wait()
-    some_rows = d.bond // 8
-
-    def one_sided(i, carry):
-        at = pl.ds(pl.multiple_of(i * some_rows, some_rows), some_rows)
-        row = lax.broadcasted_iota(jnp.int32, (some_rows, d.bond), 0) + i * some_rows
-        one = jnp.where(row == lax.broadcasted_iota(jnp.int32, (some_rows, d.bond), 1), 1.0, 0.0)
-        for t in range(d.terms_dev):
-            rs[t, at, :] = jnp.where(flags[t] == 1, rs[t, at, :].astype(jnp.float32), one).astype(jnp.bfloat16)
-        return carry
-
-    lax.fori_loop(0, 8, one_sided, 0)
-
-    def right_rows(s):
-        return rs.at[:, pl.ds(pl.multiple_of(s * d.slab, d.slab), d.slab), :]
-
-    rv[slot, core] = rs[:, pl.ds(pl.multiple_of(slot * d.slab, d.slab), d.slab), :]
-    for n in range(1, CHIPS):
-        chip = (me // 2 + n) % CHIPS
-        to = chip_slot(chip // 4, chip // 2 % 2, chip % 2)
-        remote(right_rows(to), rv.at[slot, core], rw_send.at[0], rw_recv.at[0], chip * 2 + core).start()
-        remote(wv.at[slot, core], wv.at[slot, core], rw_send.at[1], rw_recv.at[1], chip * 2 + core).start()
-
     for ch in range(CHUNKS):
         for h in range(2):
             pltpu.make_async_copy(lv.at[ch, slot, core, :, :, pl.ds(h * d.half, d.half)], lv.at[ch, slot, core, :, :, pl.ds(h * d.half, d.half)], loc_sem.at[ch, h]).wait()
@@ -265,6 +238,33 @@
     l_along()
     for g in l_gathers:
         g.own_across()
+
+    spread = (lax.broadcasted_iota(jnp.int32, (d.pair, d.prod), 1) // d.sub == lax.broadcasted_iota(jnp.int32, (d.pair, d.prod), 0))
+    spread = spread.astype(jnp.float32).astype(jnp.bfloat16)
+    for t in range(d.terms_dev):
+        wv[slot, core, t] = jnp.dot(pair_ops[t], spread, preferred_element_type=jnp.float32).astype(jnp.bfloat16)
+    all_right.wait()
+    some_rows = d.bond // 8
+
+    def one_sided(i, carry):
+        at = pl.ds(pl.multiple_of(i * some_rows, some_rows), some_rows)
+        row = lax.broadcasted_iota(jnp.int32, (some_rows, d.bond), 0) + i * some_rows
+        one = jnp.where(row == lax.broadcasted_iota(jnp.int32, (some_rows, d.bond), 1), 1.0, 0.0)
+        for t in range(d.terms_dev):
+            rs[t, at, :] = jnp.where(flags[t] == 1, rs[t, at, :].astype(jnp.float32), one).astype(jnp.bfloat16)
+        return carry
+
+    lax.fori_loop(0, 8, one_sided, 0)
+
+    def right_rows(s):
+        return rs.at[:, pl.ds(pl.multiple_of(s * d.slab, d.slab), d.slab), :]
+
+    rv[slot, core] = rs[:, pl.ds(pl.multiple_of(slot * d.slab, d.slab), d.slab), :]
+    for n in range(1, CHIPS):
+        chip = (me // 2 + n) % CHIPS
+        to = chip_slot(chip // 4, chip // 2 % 2, chip % 2)
+        remote(right_rows(to), rv.at[slot, core], rw_send.at[0], rw_recv.at[0], chip * 2 + core).start()
+        remote(wv.at[slot, core], wv.at[slot, core], rw_send.at[1], rw_recv.at[1], chip * 2 + core).start()
 
     total = jnp.zeros((8, d.lane), jnp.float32)
     for n in range(8):
@@ -285,7 +285,7 @@
     for copy in first_copies:
         copy.wait()
     tbuf[LANCZOS_STEPS - 1] = tbuf[LANCZOS_STEPS - 1] / norm_one[None]
-    first_out = [pltpu.make_async_copy(tbuf.at[LANCZOS_STEPS - 1, c], out.at[0, :, pl.ds(c * d.wide, d.wide)], first_sem.at[c])
+    first_out = [pltpu.make_async_copy(tbuf.at[LANCZOS_STEPS - 1, c], first.at[:, pl.ds(c * d.wide, d.wide)], first_sem.at[c])
                  for c in range(d.bond // d.wide)]
     for copy in first_out:
         copy.start()
@@ -371,29 +371,31 @@
         l_all = lv[ch, pl.ds(grp * 4, 4)].reshape(d.group_terms * d.chunk, d.bond)
         sig[...] += jnp.dot(zst[...], l_all, preferred_element_type=jnp.float32)
 
-    def turn_result(j):
+    def turn_result(j, vector):
         for n in range(d.pair // TILE_PARTS):
-            rows = [vcur[(bh * d.pair + q) * d.sub:(bh * d.pair + q + 1) * d.sub, :]
+            rows = [vector[(bh * d.pair + q) * d.sub:(bh * d.pair + q + 1) * d.sub, :d.half]
                     for q in range(n * TILE_PARTS, (n + 1) * TILE_PARTS) for bh in range(2)]
             tbuf[j, n] = jnp.concatenate(rows, axis=0).T
 
-    def hand_out(j, first, last):
-        for n in range(first, last):
-            to = core * CHIPS + n
-            block = tbuf.at[j, :, pl.ds(n * d.out_rows, d.out_rows), :]
-
-            @pl.when(to != me)
-            def _():
-                remote(block, gbuf.at[j, slot], k_send.at[j], k_recv.at[j], to).start()
-
-            @pl.when(to == me)
-            def _():
-                gbuf[j, slot] = block[...]
+    def hand_out(j, planes):
+        for plane in planes:
+            y, x = (ypos + plane // 2 * (1 - 2 * ypos), xpos + plane % 2 * (1 - 2 * xpos))
+            for n in range(4):
+                to = device(core * 2 + (zpos + n // 2) % 2, y, x, n % 2)
+                block = tbuf.at[j, :, pl.ds(pl.multiple_of((to - core * CHIPS) * d.out_rows, d.out_rows), d.out_rows), :]
+
+                @pl.when(to != me)
+                def _():
+                    remote(block, gbuf.at[j, slot], k_send.at[j], k_recv.at[j], to).start()
+
+                @pl.when(to == me)
+                def _():
+                    gbuf[j, slot] = block[...]
 
     sends_self = me // CHIPS == core
     lanes = lax.broadcasted_iota(jnp.int32, (d.out_rows, d.wide), 1) // d.slab
 
-    def put_out(j):
+    def put_out(j, finish=None):
         @pl.when(sends_self)
         def _():
             some = gbuf.at[j, pl.ds(0, CHIPS - 1)]
@@ -406,6 +408,8 @@
         for ct in range(CHIPS // TILE_PARTS):
             for qt in range(d.pair // TILE_PARTS):
                 src = [gbuf[j, ct * TILE_PARTS + c, qt] for c in range(TILE_PARTS)]
+                if finish is not None:
+                    src = [finish(x, gbuf[j - 1, ct * TILE_PARTS + c, qt], ct * TILE_PARTS + c) for c, x in enumerate(src)]
                 for q in range(TILE_PARTS):
                     tile = jnp.zeros((d.out_rows, d.wide), jnp.float32)
                     for c in range(TILE_PARTS):
@@ -413,9 +417,10 @@
                         moved = pltpu.roll(src[c], shift, 1) if shift else src[c]
                         tile = jnp.where(lanes == c, moved, tile)
                     tbuf[j, ct, pl.ds(qt * TILE_PARTS + q, d.out_rows, stride=d.pair), :] = tile
-            pltpu.make_async_copy(tbuf.at[j, ct], out.at[1 + j, :, pl.ds(ct * d.wide, d.wide)], o_sem.at[j, ct]).start()
-
-    def step(j, beta_prev):
+            pltpu.make_async_copy(tbuf.at[j, ct], out.at[j, :, pl.ds(ct * d.wide, d.wide)], o_sem.at[j, ct]).start()
+
+    def step(j, carried):
+        beta_prev = carried[0]
         later = jnp.minimum(j, 1)
         own = xpos * 2 + ypos
         sig[...] = jnp.zeros_like(sig)
@@ -508,7 +513,12 @@
 
         @pl.when(j > 0)
         def _():
-            hand_out(j - 1, RESULT_EARLY, CHIPS)
+            hand_out(j - 1, RESULT_LATE)
+
+        @pl.when(j == LANCZOS_STEPS - 1)
+        def _():
+            turn_result(LANCZOS_STEPS - 1, sig)
+            hand_out(LANCZOS_STEPS - 1, (3, 1, 2, 0))
 
         heard = scr.at[pl.ds(0, DEVS - 1)]
         remote(heard, heard, s_send, s_recv, me).wait()
@@ -532,13 +542,12 @@
                             vb[(bh * d.pair + q) * d.sub:(bh * d.pair + q + 1) * d.sub, ch * d.chunk:(ch + 1) * d.chunk]
         alphas[j] = alpha[0, 0]
         betas[j] = beta[0, 0]
-        return beta
-
-
-    lax.fori_loop(0, LANCZOS_STEPS, step, jnp.zeros((1, 1), jnp.float32))
-
-    turn_result(LANCZOS_STEPS - 1)
-    hand_out(LANCZOS_STEPS - 1, 0, CHIPS)
+        return beta, alpha
+
+
+    zero = jnp.zeros((1, 1), jnp.float32)
+    last_beta, last_alpha = lax.fori_loop(0, LANCZOS_STEPS, step, (zero, zero))
+
     for n, part in enumerate((lv.at[0, pl.ds(0, 15), :, 0], lv.at[1, pl.ds(0, 15), :, 0, :, pl.ds(edge, d.bond - edge)],
                               lv.at[0, pl.ds(0, 15), :, 0, :, pl.ds(0, d.half)], lv.at[1, pl.ds(0, 15), :, 0, :, pl.ds(edge, d.half - edge)])):
         remote(part, part, l_send.at[n], l_recv.at[n, 0], me).wait_send()
@@ -549,10 +558,15 @@
             theirs = left.at[:, pl.ds(0, d.chunk), pl.ds(0, d.half)]
             remote(theirs, lv.at[ch, slot, core, :, :, pl.ds(h * d.half, d.half)], d2d_sem.at[ch, h], d2d_recv.at[ch, h], partner).wait_send()
     put_out(LANCZOS_STEPS - 2)
-    put_out(LANCZOS_STEPS - 1)
+
+    def finish(block, before, s):
+        owner = device(s % 4, s // 4 % 2, s // 8, me // CHIPS)
+        return (block - (last_alpha - scr[owner][:, 4:5]) * before) / last_beta
+
+    put_out(LANCZOS_STEPS - 1, finish)
     for j in range(LANCZOS_STEPS):
         for c in range(d.bond // d.wide):
-            pltpu.make_async_copy(tbuf.at[j, c], out.at[1 + j, :, pl.ds(c * d.wide, d.wide)], o_sem.at[j, c]).wait()
+            pltpu.make_async_copy(tbuf.at[j, c], out.at[j, :, pl.ds(c * d.wide, d.wide)], o_sem.at[j, c]).wait()
 
 
 def solution(mesh):
@@ -564,11 +578,12 @@
         any_space = pl.BlockSpec(memory_space=pl.ANY)
         smem = pl.BlockSpec(memory_space=pltpu.SMEM)
         scalars = jax.ShapeDtypeStruct((LANCZOS_STEPS,), f32)
-        krylov, alphas, betas = pl.pallas_call(
+        later, first, alphas, betas = pl.pallas_call(
             functools.partial(lanczos_kernel, d),
-            out_shape=(jax.ShapeDtypeStruct((LANCZOS_STEPS + 1, d.out_rows * pair, bond), f32), scalars, scalars),
+            out_shape=(jax.ShapeDtypeStruct((LANCZOS_STEPS, d.out_rows * pair, bond), f32),
+                       jax.ShapeDtypeStruct((d.out_rows * pair, bond), f32), scalars, scalars),
             in_specs=[any_space] * 3 + [pl.BlockSpec(memory_space=pltpu.VMEM), smem],
-            out_specs=(any_space, smem, smem),
+            out_specs=(any_space, any_space, smem, smem),
             scratch_shapes=[
                 pltpu.VMEM((CHUNKS, CHIPS, CORES, d.terms_dev, d.chunk, bond), bf16),
                 pltpu.VMEM((CHIPS, CORES, d.terms_dev, d.slab, bond), bf16),
@@ -595,6 +610,7 @@
             compiler_params=pltpu.CompilerParams(has_side_effects=True, vmem_limit_bytes=67043328),
             name='lanczos',
         )(wavefunction.reshape(bond * pair, bond), left_loc, right_loc, pair_loc, flag_loc)
+        krylov = jnp.concatenate([first[None], later])
         return krylov.reshape(LANCZOS_STEPS + 1, d.out_rows, pair, bond), alphas, betas
 
     return jax.shard_map(device_body, mesh=mesh, in_specs=(P(), P(AXIS_NAME), P(AXIS_NAME), P(AXIS_NAME), P(AXIS_NAME)),

time: 470 us -> 506 us (1.077)
  Pallas kernels: 463 us -> 497 us
    pallas_call x1, Pallas kernels: 463 us -> 497 us  [device_body(): pl.pallas_call(functools.partial(lanczos_kernel, d), out_shape=(jax.Shape...]
where the time goes in v8:
time: 506 us; the launch traced here: 503 us
  Pallas kernels  497 us (98%)
    pallas_call x1, Pallas kernels, device_body(): pl.pallas_call(functools.partial(lanczos_kernel, d), out_shape=(jax.Shape...  497 us

profile of v8, /device:TPU:15, one launch (start us, length us, event | category | flops | bytes accessed | tf_op | source)
XLA Modules:
  0.0 503.5 jit_solution(2589626634792322815)
XLA Ops:
  0.6 497.3 %lanczos.1 = (f32[6,256,512]{2,1,0:T(8,128)}, f32[256,512]{1,0:T(8,128)}, f32[6]{0:T(128)}, f32[6]{0:T(128)}) custom-call(f32[8192,512]{1,0:T(8,128)} %bitcast.3, bf16[2,512,512]{2,1,0:T(8,128)(2,1)} %left.1, bf16[2,512,512]{2,1,0:T(8,128)(2,1)} %right.1, bf16[2,16,16]{2,1,0:T(8,128)(2,1)} %pair_ops.1, s32[2]{0:T(128)} %flags.1), custom_call_target="tpu_custom_call" | custom-call | tf_op jit(solution)/shard_map/lanczos/pallas_call | solution.py:581
  497.9 0.0 copy-start.1
  497.9 0.0 copy-start
  497.9 4.5 pad_maximum_fusion
  502.5 0.0 copy-done.1
  502.5 0.5 copy.10
  503.0 0.0 copy-done
  503.0 0.5 copy.11
Async XLA Ops:
  497.9 4.6 copy-start.1
  497.9 5.1 %copy-start = (f32[6]{0:T(128)S(1)}, f32[6]{0:T(128)}, u32[]{:S(2)}) copy-start(f32[6]{0:T(128)} %get-tuple-element.16) | copy-start | bytes 76

commit v9 on v8

--- a/solution.py
+++ b/solution.py
@@ -40,7 +40,7 @@
     (),
     (),
 )
-RESULT_EARLY, RESULT_LATE = (3, 1, 2), (0,)
+RESULT_EARLY = 9
 
 
 class Dims:
@@ -199,11 +199,14 @@
         elif kind == RESULT:
             turn_result(j - 1, vcur)
         elif kind == RESULT_OUT:
-            hand_out(j - 1, RESULT_EARLY)
+            hand_out(j - 1, 0, RESULT_EARLY)
         elif kind == RESULT_PUT:
             @pl.when(j > 1)
             def _():
                 put_out(j - 2)
+
+    all_right = pltpu.make_async_copy(right, rs, loc_sem.at[2, 0])
+    all_right.start()
 
     for ch in range(CHUNKS):
         for h in range(2):
@@ -214,8 +217,6 @@
             remote(theirs, lv.at[ch, slot, core, :, :, pl.ds(h * d.half, d.half)], d2d_sem.at[ch, h], d2d_recv.at[ch, h], partner).start()
             pltpu.make_async_copy(mine, lv.at[ch, slot, core, :, :, pl.ds(h * d.half, d.half)], loc_sem.at[ch, h]).start()
 
-    all_right = pltpu.make_async_copy(right, rs, loc_sem.at[2, 0])
-    all_right.start()
     psi_rows = d.half * d.pair // 8
     psi_copies = [pltpu.make_async_copy(psi.at[pl.ds(pl.multiple_of(core * d.half * d.pair + n * psi_rows, psi_rows), psi_rows),
                                                pl.ds(c * d.lane, d.lane)],
@@ -229,6 +230,33 @@
                                           tbuf.at[LANCZOS_STEPS - 1, c], first_sem.at[c]) for c in range(d.bond // d.wide)]
     for copy in first_copies:
         copy.start()
+
+    spread = (lax.broadcasted_iota(jnp.int32, (d.pair, d.prod), 1) // d.sub == lax.broadcasted_iota(jnp.int32, (d.pair, d.prod), 0))
+    spread = spread.astype(jnp.float32).astype(jnp.bfloat16)
+    for t in range(d.terms_dev):
+        wv[slot, core, t] = jnp.dot(pair_ops[t], spread, preferred_element_type=jnp.float32).astype(jnp.bfloat16)
+    all_right.wait()
+    some_rows = d.bond // 8
+
+    def one_sided(i, carry):
+        at = pl.ds(pl.multiple_of(i * some_rows, some_rows), some_rows)
+        row = lax.broadcasted_iota(jnp.int32, (some_rows, d.bond), 0) + i * some_rows
+        one = jnp.where(row == lax.broadcasted_iota(jnp.int32, (some_rows, d.bond), 1), 1.0, 0.0)
+        for t in range(d.terms_dev):
+            rs[t, at, :] = jnp.where(flags[t] == 1, rs[t, at, :].astype(jnp.float32), one).astype(jnp.bfloat16)
+        return carry
+
+    lax.fori_loop(0, 8, one_sided, 0)
+
+    def right_rows(s):
+        return rs.at[:, pl.ds(pl.multiple_of(s * d.slab, d.slab), d.slab), :]
+
+    rv[slot, core] = rs[:, pl.ds(pl.multiple_of(slot * d.slab, d.slab), d.slab), :]
+    for n in range(1, CHIPS):
+        chip = (me // 2 + n) % CHIPS
+        to = chip_slot(chip // 4, chip // 2 % 2, chip % 2)
+        remote(right_rows(to), rv.at[slot, core], rw_send.at[0], rw_recv.at[0], chip * 2 + core).start()
+        remote(wv.at[slot, core], wv.at[slot, core], rw_send.at[1], rw_recv.at[1], chip * 2 + core).start()
 
     for ch in range(CHUNKS):
         for h in range(2):
@@ -238,33 +266,6 @@
     l_along()
     for g in l_gathers:
         g.own_across()
-
-    spread = (lax.broadcasted_iota(jnp.int32, (d.pair, d.prod), 1) // d.sub == lax.broadcasted_iota(jnp.int32, (d.pair, d.prod), 0))
-    spread = spread.astype(jnp.float32).astype(jnp.bfloat16)
-    for t in range(d.terms_dev):
-        wv[slot, core, t] = jnp.dot(pair_ops[t], spread, preferred_element_type=jnp.float32).astype(jnp.bfloat16)
-    all_right.wait()
-    some_rows = d.bond // 8
-
-    def one_sided(i, carry):
-        at = pl.ds(pl.multiple_of(i * some_rows, some_rows), some_rows)
-        row = lax.broadcasted_iota(jnp.int32, (some_rows, d.bond), 0) + i * some_rows
-        one = jnp.where(row == lax.broadcasted_iota(jnp.int32, (some_rows, d.bond), 1), 1.0, 0.0)
-        for t in range(d.terms_dev):
-            rs[t, at, :] = jnp.where(flags[t] == 1, rs[t, at, :].astype(jnp.float32), one).astype(jnp.bfloat16)
-        return carry
-
-    lax.fori_loop(0, 8, one_sided, 0)
-
-    def right_rows(s):
-        return rs.at[:, pl.ds(pl.multiple_of(s * d.slab, d.slab), d.slab), :]
-
-    rv[slot, core] = rs[:, pl.ds(pl.multiple_of(slot * d.slab, d.slab), d.slab), :]
-    for n in range(1, CHIPS):
-        chip = (me // 2 + n) % CHIPS
-        to = chip_slot(chip // 4, chip // 2 % 2, chip % 2)
-        remote(right_rows(to), rv.at[slot, core], rw_send.at[0], rw_recv.at[0], chip * 2 + core).start()
-        remote(wv.at[slot, core], wv.at[slot, core], rw_send.at[1], rw_recv.at[1], chip * 2 + core).start()
 
     total = jnp.zeros((8, d.lane), jnp.float32)
     for n in range(8):
@@ -377,20 +378,18 @@
                     for q in range(n * TILE_PARTS, (n + 1) * TILE_PARTS) for bh in range(2)]
             tbuf[j, n] = jnp.concatenate(rows, axis=0).T
 
-    def hand_out(j, planes):
-        for plane in planes:
-            y, x = (ypos + plane // 2 * (1 - 2 * ypos), xpos + plane % 2 * (1 - 2 * xpos))
-            for n in range(4):
-                to = device(core * 2 + (zpos + n // 2) % 2, y, x, n % 2)
-                block = tbuf.at[j, :, pl.ds(pl.multiple_of((to - core * CHIPS) * d.out_rows, d.out_rows), d.out_rows), :]
-
-                @pl.when(to != me)
-                def _():
-                    remote(block, gbuf.at[j, slot], k_send.at[j], k_recv.at[j], to).start()
-
-                @pl.when(to == me)
-                def _():
-                    gbuf[j, slot] = block[...]
+    def hand_out(j, begin, end):
+        for n in range(begin, end):
+            to = core * CHIPS + n
+            block = tbuf.at[j, :, pl.ds(n * d.out_rows, d.out_rows), :]
+
+            @pl.when(to != me)
+            def _():
+                remote(block, gbuf.at[j, slot], k_send.at[j], k_recv.at[j], to).start()
+
+            @pl.when(to == me)
+            def _():
+                gbuf[j, slot] = block[...]
 
     sends_self = me // CHIPS == core
     lanes = lax.broadcasted_iota(jnp.int32, (d.out_rows, d.wide), 1) // d.slab
@@ -513,12 +512,12 @@
 
         @pl.when(j > 0)
         def _():
-            hand_out(j - 1, RESULT_LATE)
+            hand_out(j - 1, RESULT_EARLY, CHIPS)
 
         @pl.when(j == LANCZOS_STEPS - 1)
         def _():
             turn_result(LANCZOS_STEPS - 1, sig)
-            hand_out(LANCZOS_STEPS - 1, (3, 1, 2, 0))
+            hand_out(LANCZOS_STEPS - 1, 0, CHIPS)
 
         heard = scr.at[pl.ds(0, DEVS - 1)]
         remote(heard, heard, s_send, s_recv, me).wait()

time: 506 us -> 466 us (0.921)
  Pallas kernels: 497 us -> 460 us
    pallas_call x1, Pallas kernels: 497 us -> 460 us  [device_body(): pl.pallas_call(functools.partial(lanczos_kernel, d), out_shape=(jax.Shape...]
where the time goes in v9:
time: 466 us
  Pallas kernels  460 us (99%)
    pallas_call x1, Pallas kernels, device_body(): pl.pallas_call(functools.partial(lanczos_kernel, d), out_shape=(jax.Shape...  460 us

profile of v9, /device:TPU:15, one launch (start us, length us, event | category | flops | bytes accessed | tf_op | source)
XLA Modules:
  0.0 466.1 jit_solution(5574121486649334548)
XLA Ops:
  0.6 459.8 %lanczos.1 = (f32[6,256,512]{2,1,0:T(8,128)}, f32[256,512]{1,0:T(8,128)}, f32[6]{0:T(128)}, f32[6]{0:T(128)}) custom-call(f32[8192,512]{1,0:T(8,128)} %bitcast.3, bf16[2,512,512]{2,1,0:T(8,128)(2,1)} %left.1, bf16[2,512,512]{2,1,0:T(8,128)(2,1)} %right.1, bf16[2,16,16]{2,1,0:T(8,128)(2,1)} %pair_ops.1, s32[2]{0:T(128)} %flags.1), custom_call_target="tpu_custom_call" | custom-call | tf_op jit(solution)/shard_map/lanczos/pallas_call | solution.py:580
  460.5 0.0 copy-start.1
  460.5 0.0 copy-start
  460.5 4.5 pad_maximum_fusion
  465.0 0.0 copy-done.1
  465.0 0.5 copy.10
  465.6 0.0 copy-done
  465.6 0.5 copy.11
Async XLA Ops:
  460.5 4.6 copy-start.1
  460.5 5.1 %copy-start = (f32[6]{0:T(128)S(1)}, f32[6]{0:T(128)}, u32[]{:S(2)}) copy-start(f32[6]{0:T(128)} %get-tuple-element.16) | copy-start | bytes 76

commit v10 on v9

--- a/solution.py
+++ b/solution.py
@@ -147,16 +147,12 @@
             g.event(n)
         l_swap(chip_slot(zs[i], ypos, xpos) if n % 2 else chip_slot(zs[i], y_two, x_two), core).start()
 
-    def l_last(diagonal):
-        for i in range(4):
-            which = chip_slot(zs[i], 1 - ypos, 1 - xpos) if diagonal else chip_slot(zs[i], y_three, x_three)
-            for g in l_gathers:
-                g.wait(which)
-            l_swap(which, core).start()
-
-    def l_fill(n, grp):
-        s = grp * 4 + n
-
+    def l_late(s):
+        for g in l_gathers:
+            g.wait(s)
+        l_swap(s, core).start()
+
+    def l_fill(s):
         @pl.when(s != slot)
         def _():
             l_swap(s, 1 - core).wait_recv()
@@ -165,7 +161,6 @@
                 lv[:, s, c, 1 - core, :, d.half:] = tile.reshape(CHUNKS, d.chunk, d.half)
                 for t in range(d.terms_dev):
                     lv[1, s, c, t, :, :edge] = lv[0, s, c, t, :, edge:d.half].T
-        return grp
 
     def l_along():
         for i in (1, 2, 3):
@@ -208,13 +203,18 @@
     all_right = pltpu.make_async_copy(right, rs, loc_sem.at[2, 0])
     all_right.start()
 
+    barrier = pltpu.get_barrier_semaphore()
+
+    def knock(n, carry):
+        pl.semaphore_signal(barrier, inc=1, device_id=((me + n) % DEVS,), device_id_type=MESH)
+        return carry
+
+    lax.fori_loop(1, DEVS, knock, 0)
+
     for ch in range(CHUNKS):
         for h in range(2):
             mine = left.at[:, pl.ds(pl.multiple_of(core * d.half + ch * d.chunk, d.chunk), d.chunk),
                            pl.ds(pl.multiple_of((core + h) % 2 * d.half, d.half), d.half)]
-            theirs = left.at[:, pl.ds(pl.multiple_of((1 - core) * d.half + ch * d.chunk, d.chunk), d.chunk),
-                             pl.ds(pl.multiple_of((1 - core + h) % 2 * d.half, d.half), d.half)]
-            remote(theirs, lv.at[ch, slot, core, :, :, pl.ds(h * d.half, d.half)], d2d_sem.at[ch, h], d2d_recv.at[ch, h], partner).start()
             pltpu.make_async_copy(mine, lv.at[ch, slot, core, :, :, pl.ds(h * d.half, d.half)], loc_sem.at[ch, h]).start()
 
     psi_rows = d.half * d.pair // 8
@@ -252,6 +252,13 @@
         return rs.at[:, pl.ds(pl.multiple_of(s * d.slab, d.slab), d.slab), :]
 
     rv[slot, core] = rs[:, pl.ds(pl.multiple_of(slot * d.slab, d.slab), d.slab), :]
+
+    pl.semaphore_wait(barrier, DEVS - 1)
+    for ch in range(CHUNKS):
+        for h in range(2):
+            theirs = left.at[:, pl.ds(pl.multiple_of((1 - core) * d.half + ch * d.chunk, d.chunk), d.chunk),
+                             pl.ds(pl.multiple_of((1 - core + h) % 2 * d.half, d.half), d.half)]
+            remote(theirs, lv.at[ch, slot, core, :, :, pl.ds(h * d.half, d.half)], d2d_sem.at[ch, h], d2d_recv.at[ch, h], partner).start()
     for n in range(1, CHIPS):
         chip = (me // 2 + n) % CHIPS
         to = chip_slot(chip // 4, chip // 2 % 2, chip % 2)
@@ -345,23 +352,61 @@
     for copy in first_out:
         copy.wait()
 
-    def right_product(grp, ch, qb):
+    def right_product(grp, ch, qb, to):
         r_all = rv[pl.ds(grp * 4, 4)].reshape(d.group_terms * d.slab, d.bond)
         y = jnp.dot(r_all, uv[ch, qb], preferred_element_type=jnp.float32).astype(jnp.bfloat16)
         y = y.reshape(d.group_terms, 2, d.sub, 2 * d.chunk)
         for q2 in range(2):
             for bh in range(2):
-                yst[pl.ds(grp * d.group_terms, d.group_terms), qb * 2 + q2, :, bh * d.chunk:(bh + 1) * d.chunk] = \
+                yst[pl.ds(to * d.group_terms, d.group_terms), qb * 2 + q2, :, bh * d.chunk:(bh + 1) * d.chunk] = \
                     y[:, bh, :, q2 * d.chunk:(q2 + 1) * d.chunk]
-
-    def right_of_group(grp, ch):
-        for qb in range(d.pair // 2):
-            right_product(grp, ch, qb)
 
     def right_of_piece(ch, part):
         for qb in range(2):
             for grp in range(GROUPS):
-                right_product(grp, ch, part * 2 + qb)
+                right_product(grp, ch, part * 2 + qb, grp)
+
+    def first_group(n, carry):
+        own, third = xpos * 2 + ypos, x_three * 2 + y_three
+        grp = jnp.where(n == 0, own, jnp.where(n == 1, x_two * 2 + y_two, jnp.where(n == 2, third, 3 - own)))
+        spare = (grp + 1) % GROUPS
+
+        def right_of_group(ch, carry):
+            to = grp + ch * (spare - grp)
+            for qb in range(d.pair // 2):
+                right_product(grp, ch, qb, to)
+            return carry
+
+        lax.fori_loop(0, CHUNKS, right_of_group, 0)
+
+        def one_block(i, carry):
+            z = jnp.where(i == 0, zs[0], jnp.where(i == 1, zs[1], jnp.where(i == 2, zs[2], zs[3])))
+            s = grp * 4 + z
+
+            @pl.when(n == 1)
+            def _():
+                l_late(third * 4 + z)
+
+            @pl.when(n == 3)
+            def _():
+                l_late(s)
+
+            l_fill(s)
+            block_terms = CORES * d.terms_dev
+            for ch in range(CHUNKS):
+                at = (grp + ch * (spare - grp)) * d.group_terms + z * block_terms
+                for k in range(block_terms):
+                    y = yst[at + k].reshape(d.prod, 2 * d.chunk)
+                    w = jnp.dot(kw[s, k // 2, k % 2], y, preferred_element_type=jnp.float32).astype(jnp.bfloat16)
+                    for bh in range(2):
+                        col = (ch * block_terms + k) * d.chunk
+                        zst[bh * d.prod:(bh + 1) * d.prod, col:col + d.chunk] = w[:, bh * d.chunk:(bh + 1) * d.chunk]
+            wide = CHUNKS * block_terms * d.chunk
+            sig[...] += jnp.dot(zst[:, :wide], lv[:, s].reshape(wide, d.bond), preferred_element_type=jnp.float32)
+            return carry
+
+        lax.fori_loop(0, 4, one_block, 0)
+        return carry
 
     def left_products(ch, grp):
         for k in range(d.group_terms):
@@ -420,64 +465,40 @@
 
     def step(j, carried):
         beta_prev = carried[0]
-        later = jnp.minimum(j, 1)
-        own = xpos * 2 + ypos
         sig[...] = jnp.zeros_like(sig)
 
         def slot_step(t, carry):
-            n = t // 4
-            first_grp = jnp.where(n == 0, own, jnp.where(n == 1, x_two * 2 + y_two, jnp.where(n == 2, x_three * 2 + y_three, 3 - own)))
-            first_ch = t // 2 % 2
             done_right = sum((t > r).astype(jnp.int32) for r in RIGHT_SLOTS)
             done_left = t - done_right
-            now_right = sum((t == r).astype(jnp.int32) for r in RIGHT_SLOTS)
-            is_right = (1 - later) * (1 - t % 2) + later * now_right
-
-            @pl.when(j == 0)
-            def _():
-                @pl.when(t == 5)
+            is_right = sum((t == r).astype(jnp.int32) for r in RIGHT_SLOTS)
+            for four in range(0, len(SLOTS), 4):
+                @pl.when((t >= four) & (t < four + 4))
                 def _():
-                    l_last(False)
-
-                @pl.when(t == 13)
-                def _():
-                    l_last(True)
-
-                @pl.when(t % 4 == 1)
-                def _():
-                    lax.fori_loop(0, 4, l_fill, first_grp)
-
-            @pl.when(j > 0)
-            def _():
-                for four in range(0, len(SLOTS), 4):
-                    @pl.when((t >= four) & (t < four + 4))
-                    def _():
-                        for at in range(four, four + 4):
-                            if not SLOTS[at]:
-                                continue
-
-                            @pl.when(t == at)
-                            def _():
-                                for kind, i, p in SLOTS[at]:
-                                    act(kind, i, p, j)
-
-            @pl.when((is_right == 1) & (j == 0))
-            def _():
-                right_of_group(first_grp, first_ch)
-
-            @pl.when((is_right == 1) & (j > 0))
+                    for at in range(four, four + 4):
+                        if not SLOTS[at]:
+                            continue
+
+                        @pl.when(t == at)
+                        def _():
+                            for kind, i, p in SLOTS[at]:
+                                act(kind, i, p, j)
+
+            @pl.when(is_right == 1)
             def _():
                 right_of_piece(done_right // QUARTERS, done_right % QUARTERS)
 
             @pl.when(is_right == 0)
             def _():
-                left_products((1 - later) * first_ch + later * (done_left // GROUPS), (1 - later) * first_grp + later * (done_left % GROUPS))
+                left_products(done_left // GROUPS, done_left % GROUPS)
             return carry
 
-        lax.fori_loop(0, len(SLOTS), slot_step, 0)
+        @pl.when(j == 0)
+        def _():
+            lax.fori_loop(0, GROUPS, first_group, 0)
 
         @pl.when(j > 0)
         def _():
+            lax.fori_loop(0, len(SLOTS), slot_step, 0)
             for p in range(PIECES):
                 sent = uv.at[p // QUARTERS, pl.ds(0, 2), pl.ds(0, 15 * d.slab), :]
                 remote(sent, sent, u_send.at[p], u_recv.at[p, 0], me).wait_send()
@@ -606,7 +627,7 @@
                 dma((4,)), dma((4, CHIPS)), dma, dma((CHIPS,)), dma((PIECES,)), dma((PIECES, CHIPS)),
                 dma, dma, dma, dma, dma((LANCZOS_STEPS,)), dma((LANCZOS_STEPS,)), dma, dma, dma((LANCZOS_STEPS, bond // d.wide)), dma((bond // d.wide,)),
             ],
-            compiler_params=pltpu.CompilerParams(has_side_effects=True, vmem_limit_bytes=67043328),
+            compiler_params=pltpu.CompilerParams(has_side_effects=True, collective_id=0, vmem_limit_bytes=67043328),
             name='lanczos',
         )(wavefunction.reshape(bond * pair, bond), left_loc, right_loc, pair_loc, flag_loc)
         krylov = jnp.concatenate([first[None], later])

time: 466 us -> 473 us (1.015)
  Pallas kernels: 460 us -> 466 us
    pallas_call x1, Pallas kernels: 460 us -> 466 us  [device_body(): pl.pallas_call(functools.partial(lanczos_kernel, d), out_shape=(jax.Shape...]
where the time goes in v10:
time: 473 us
  Pallas kernels  466 us (99%)
    pallas_call x1, Pallas kernels, device_body(): pl.pallas_call(functools.partial(lanczos_kernel, d), out_shape=(jax.Shape...  466 us

profile of v10, /device:TPU:15, one launch (start us, length us, event | category | flops | bytes accessed | tf_op | source)
XLA Modules:
  0.0 472.7 jit_solution(15979898426935834780)
XLA Ops:
  0.6 466.5 %lanczos.1 = (f32[6,256,512]{2,1,0:T(8,128)}, f32[256,512]{1,0:T(8,128)}, f32[6]{0:T(128)}, f32[6]{0:T(128)}) custom-call(f32[8192,512]{1,0:T(8,128)} %bitcast.3, bf16[2,512,512]{2,1,0:T(8,128)(2,1)} %left.1, bf16[2,512,512]{2,1,0:T(8,128)(2,1)} %right.1, bf16[2,16,16]{2,1,0:T(8,128)(2,1)} %pair_ops.1, s32[2]{0:T(128)} %flags.1), custom_call_target="tpu_custom_call" | custom-call | tf_op jit(solution)/shard_map/lanczos/pallas_call | solution.py:601
  467.1 0.0 copy-start.1
  467.1 0.0 copy-start
  467.1 4.5 pad_maximum_fusion
  471.7 0.0 copy-done.1
  471.7 0.5 copy.10
  472.2 0.0 copy-done
  472.2 0.5 copy.11
Async XLA Ops:
  467.1 4.6 copy-start.1
  467.1 5.1 %copy-start = (f32[6]{0:T(128)S(1)}, f32[6]{0:T(128)}, u32[]{:S(2)}) copy-start(f32[6]{0:T(128)} %get-tuple-element.16) | copy-start | bytes 76

commit v11 on v9

--- a/solution.py
+++ b/solution.py
@@ -208,13 +208,18 @@
     all_right = pltpu.make_async_copy(right, rs, loc_sem.at[2, 0])
     all_right.start()
 
+    barrier = pltpu.get_barrier_semaphore()
+
+    def knock(n, carry):
+        pl.semaphore_signal(barrier, inc=1, device_id=((me + n) % DEVS,), device_id_type=MESH)
+        return carry
+
+    lax.fori_loop(1, DEVS, knock, 0)
+
     for ch in range(CHUNKS):
         for h in range(2):
             mine = left.at[:, pl.ds(pl.multiple_of(core * d.half + ch * d.chunk, d.chunk), d.chunk),
                            pl.ds(pl.multiple_of((core + h) % 2 * d.half, d.half), d.half)]
-            theirs = left.at[:, pl.ds(pl.multiple_of((1 - core) * d.half + ch * d.chunk, d.chunk), d.chunk),
-                             pl.ds(pl.multiple_of((1 - core + h) % 2 * d.half, d.half), d.half)]
-            remote(theirs, lv.at[ch, slot, core, :, :, pl.ds(h * d.half, d.half)], d2d_sem.at[ch, h], d2d_recv.at[ch, h], partner).start()
             pltpu.make_async_copy(mine, lv.at[ch, slot, core, :, :, pl.ds(h * d.half, d.half)], loc_sem.at[ch, h]).start()
 
     psi_rows = d.half * d.pair // 8
@@ -252,6 +257,13 @@
         return rs.at[:, pl.ds(pl.multiple_of(s * d.slab, d.slab), d.slab), :]
 
     rv[slot, core] = rs[:, pl.ds(pl.multiple_of(slot * d.slab, d.slab), d.slab), :]
+
+    pl.semaphore_wait(barrier, DEVS - 1)
+    for ch in range(CHUNKS):
+        for h in range(2):
+            theirs = left.at[:, pl.ds(pl.multiple_of((1 - core) * d.half + ch * d.chunk, d.chunk), d.chunk),
+                             pl.ds(pl.multiple_of((1 - core + h) % 2 * d.half, d.half), d.half)]
+            remote(theirs, lv.at[ch, slot, core, :, :, pl.ds(h * d.half, d.half)], d2d_sem.at[ch, h], d2d_recv.at[ch, h], partner).start()
     for n in range(1, CHIPS):
         chip = (me // 2 + n) % CHIPS
         to = chip_slot(chip // 4, chip // 2 % 2, chip % 2)
@@ -606,7 +618,7 @@
                 dma((4,)), dma((4, CHIPS)), dma, dma((CHIPS,)), dma((PIECES,)), dma((PIECES, CHIPS)),
                 dma, dma, dma, dma, dma((LANCZOS_STEPS,)), dma((LANCZOS_STEPS,)), dma, dma, dma((LANCZOS_STEPS, bond // d.wide)), dma((bond // d.wide,)),
             ],
-            compiler_params=pltpu.CompilerParams(has_side_effects=True, vmem_limit_bytes=67043328),
+            compiler_params=pltpu.CompilerParams(has_side_effects=True, collective_id=0, vmem_limit_bytes=67043328),
             name='lanczos',
         )(wavefunction.reshape(bond * pair, bond), left_loc, right_loc, pair_loc, flag_loc)
         krylov = jnp.concatenate([first[None], later])

time: 466 us -> 462 us (level)
  Pallas kernels: 460 us -> 455 us
where the time goes in v11:
time: 462 us
  Pallas kernels  455 us (98%)
    pallas_call x1, Pallas kernels, device_body(): pl.pallas_call(functools.partial(lanczos_kernel, d), out_shape=(jax.Shape...  455 us

profile of v11, /device:TPU:15, one launch (start us, length us, event | category | flops | bytes accessed | tf_op | source)
XLA Modules:
  0.0 461.6 jit_solution(5720344184930511914)
XLA Ops:
  0.6 455.4 %lanczos.1 = (f32[6,256,512]{2,1,0:T(8,128)}, f32[256,512]{1,0:T(8,128)}, f32[6]{0:T(128)}, f32[6]{0:T(128)}) custom-call(f32[8192,512]{1,0:T(8,128)} %bitcast.3, bf16[2,512,512]{2,1,0:T(8,128)(2,1)} %left.1, bf16[2,512,512]{2,1,0:T(8,128)(2,1)} %right.1, bf16[2,16,16]{2,1,0:T(8,128)(2,1)} %pair_ops.1, s32[2]{0:T(128)} %flags.1), custom_call_target="tpu_custom_call" | custom-call | tf_op jit(solution)/shard_map/lanczos/pallas_call | solution.py:592
  456.0 0.0 copy-start.1
  456.0 0.0 copy-start
  456.0 4.5 pad_maximum_fusion
  460.6 0.0 copy-done.1
  460.6 0.5 copy.10
  461.1 0.0 copy-done
  461.1 0.5 copy.11
Async XLA Ops:
  456.0 4.6 copy-start.1
  456.0 5.1 %copy-start = (f32[6]{0:T(128)S(1)}, f32[6]{0:T(128)}, u32[]{:S(2)}) copy-start(f32[6]{0:T(128)} %get-tuple-element.16) | copy-start | bytes 76

commit v12 on v10

--- a/solution.py
+++ b/solution.py
@@ -147,10 +147,12 @@
             g.event(n)
         l_swap(chip_slot(zs[i], ypos, xpos) if n % 2 else chip_slot(zs[i], y_two, x_two), core).start()
 
-    def l_late(s):
-        for g in l_gathers:
-            g.wait(s)
-        l_swap(s, core).start()
+    def l_last(diagonal):
+        for i in range(4):
+            which = chip_slot(zs[i], 1 - ypos, 1 - xpos) if diagonal else chip_slot(zs[i], y_three, x_three)
+            for g in l_gathers:
+                g.wait(which)
+            l_swap(which, core).start()
 
     def l_fill(s):
         @pl.when(s != slot)
@@ -345,9 +347,6 @@
         return carry
 
     lax.fori_loop(0, CHIPS, spread_pair, 0)
-    l_event(4)
-    l_event(5)
-    l_event(6)
     vprev[...] = jnp.zeros_like(vprev)
     for copy in first_out:
         copy.wait()
@@ -366,56 +365,58 @@
             for grp in range(GROUPS):
                 right_product(grp, ch, part * 2 + qb, grp)
 
-    def first_group(n, carry):
-        own, third = xpos * 2 + ypos, x_three * 2 + y_three
-        grp = jnp.where(n == 0, own, jnp.where(n == 1, x_two * 2 + y_two, jnp.where(n == 2, third, 3 - own)))
-        spare = (grp + 1) % GROUPS
-
-        def right_of_group(ch, carry):
-            to = grp + ch * (spare - grp)
-            for qb in range(d.pair // 2):
-                right_product(grp, ch, qb, to)
-            return carry
-
-        lax.fori_loop(0, CHUNKS, right_of_group, 0)
-
-        def one_block(i, carry):
-            z = jnp.where(i == 0, zs[0], jnp.where(i == 1, zs[1], jnp.where(i == 2, zs[2], zs[3])))
-            s = grp * 4 + z
-
-            @pl.when(n == 1)
-            def _():
-                l_late(third * 4 + z)
-
-            @pl.when(n == 3)
-            def _():
-                l_late(s)
-
-            l_fill(s)
-            block_terms = CORES * d.terms_dev
-            for ch in range(CHUNKS):
-                at = (grp + ch * (spare - grp)) * d.group_terms + z * block_terms
-                for k in range(block_terms):
-                    y = yst[at + k].reshape(d.prod, 2 * d.chunk)
-                    w = jnp.dot(kw[s, k // 2, k % 2], y, preferred_element_type=jnp.float32).astype(jnp.bfloat16)
-                    for bh in range(2):
-                        col = (ch * block_terms + k) * d.chunk
-                        zst[bh * d.prod:(bh + 1) * d.prod, col:col + d.chunk] = w[:, bh * d.chunk:(bh + 1) * d.chunk]
-            wide = CHUNKS * block_terms * d.chunk
-            sig[...] += jnp.dot(zst[:, :wide], lv[:, s].reshape(wide, d.bond), preferred_element_type=jnp.float32)
-            return carry
-
-        lax.fori_loop(0, 4, one_block, 0)
-        return carry
-
-    def left_products(ch, grp):
+    def right_of_group(grp, ch, to):
+        for qb in range(d.pair // 2):
+            right_product(grp, ch, qb, to)
+
+    def left_products(ch, grp, at=None):
         for k in range(d.group_terms):
             w = kw[grp * 4 + k // 4, k // 2 % 2, k % 2]
-            z = jnp.dot(w, yst[grp * d.group_terms + k].reshape(d.prod, 2 * d.chunk), preferred_element_type=jnp.float32).astype(jnp.bfloat16)
+            z = jnp.dot(w, yst[(grp if at is None else at) * d.group_terms + k].reshape(d.prod, 2 * d.chunk), preferred_element_type=jnp.float32).astype(jnp.bfloat16)
             for bh in range(2):
                 zst[bh * d.prod:(bh + 1) * d.prod, k * d.chunk:(k + 1) * d.chunk] = z[:, bh * d.chunk:(bh + 1) * d.chunk]
         l_all = lv[ch, pl.ds(grp * 4, 4)].reshape(d.group_terms * d.chunk, d.bond)
         sig[...] += jnp.dot(zst[...], l_all, preferred_element_type=jnp.float32)
+
+    def first_right(grp, carry):
+        right_of_group(grp, 0, grp)
+
+        @pl.when(grp == 1)
+        def _():
+            l_event(4)
+        return carry
+
+    def first_group(n, carry):
+        own, third = xpos * 2 + ypos, x_three * 2 + y_three
+        grp = jnp.where(n == 0, own, jnp.where(n == 1, x_two * 2 + y_two, jnp.where(n == 2, third, 3 - own)))
+        spare = jnp.where(n == 3, own, grp)
+
+        @pl.when(n == 1)
+        def _():
+            l_event(6)
+            l_last(False)
+
+        @pl.when(n == 3)
+        def _():
+            right_of_group(grp, 1, spare)
+            l_last(True)
+
+        def fill(z, carry):
+            l_fill(grp * 4 + z)
+            return carry
+
+        lax.fori_loop(0, 4, fill, 0)
+
+        def chunk_products(ch, carry):
+            left_products(ch, grp, (1 - ch) * grp + ch * spare)
+
+            @pl.when((ch == 0) & (n < 3))
+            def _():
+                right_of_group(grp, 1, spare)
+            return carry
+
+        lax.fori_loop(0, CHUNKS, chunk_products, 0)
+        return carry
 
     def turn_result(j, vector):
         for n in range(d.pair // TILE_PARTS):
@@ -494,6 +495,8 @@
 
         @pl.when(j == 0)
         def _():
+            lax.fori_loop(0, GROUPS, first_right, 0)
+            l_event(5)
             lax.fori_loop(0, GROUPS, first_group, 0)
 
         @pl.when(j > 0)

time: 473 us -> 449 us (0.949)
  Pallas kernels: 466 us -> 442 us
    pallas_call x1, Pallas kernels: 466 us -> 442 us  [device_body(): pl.pallas_call(functools.partial(lanczos_kernel, d), out_shape=(jax.Shape...]
where the time goes in v12:
time: 449 us
  Pallas kernels  442 us (98%)
  other arithmetic  4.53 us (1%)
    pallas_call x1, Pallas kernels, device_body(): pl.pallas_call(functools.partial(lanczos_kernel, d), out_shape=(jax.Shape...  442 us

profile of v12, /device:TPU:15, one launch (start us, length us, event | category | flops | bytes accessed | tf_op | source)
XLA Modules:
  0.0 448.7 jit_solution(6120873865028809381)
XLA Ops:
  0.6 442.4 %lanczos.1 = (f32[6,256,512]{2,1,0:T(8,128)}, f32[256,512]{1,0:T(8,128)}, f32[6]{0:T(128)}, f32[6]{0:T(128)}) custom-call(f32[8192,512]{1,0:T(8,128)} %bitcast.3, bf16[2,512,512]{2,1,0:T(8,128)(2,1)} %left.1, bf16[2,512,512]{2,1,0:T(8,128)(2,1)} %right.1, bf16[2,16,16]{2,1,0:T(8,128)(2,1)} %pair_ops.1, s32[2]{0:T(128)} %flags.1), custom_call_target="tpu_custom_call" | custom-call | tf_op jit(solution)/shard_map/lanczos/pallas_call | solution.py:604
  443.1 0.0 copy-start.1
  443.1 0.0 copy-start
  443.1 4.5 %pad_maximum_fusion = f32[7,16,16,512]{3,2,1,0:T(8,128)} fusion(f32[6,16,16,512]{3,2,1,0:T(8,128)} %bitcast.4, f32[1,16,16,512]{3,2,1,0:T(8,128)} %bitcast.5), kind=kLoop, calls=%fused_computation | loop fusion | flops 917504 | bytes 7340032 | tf_op jit(solution)/shard_map/concatenate | solution.py:636
  447.6 0.0 copy-done.1
  447.6 0.5 copy.10
  448.2 0.0 copy-done
  448.2 0.5 copy.11
Async XLA Ops:
  443.1 4.6 %copy-start.1 = (f32[6]{0:T(128)S(1)}, f32[6]{0:T(128)}, u32[]{:S(2)}) copy-start(f32[6]{0:T(128)} %get-tuple-element.15) | copy-start | bytes 76
  443.1 5.1 %copy-start = (f32[6]{0:T(128)S(1)}, f32[6]{0:T(128)}, u32[]{:S(2)}) copy-start(f32[6]{0:T(128)} %get-tuple-element.16) | copy-start | bytes 76

commit v13 on v12

--- a/solution.py
+++ b/solution.py
@@ -80,7 +80,6 @@
 
     partner = device(zpos, ypos, xpos, 1 - core)
     slot = chip_slot(zpos, ypos, xpos)
-    zs = (zpos, zpos + 1 - 2 * (zpos % 2), (zpos + 2) % 4, 3 - zpos)
     inner = (zpos + 1) // 2 % 2
     zn = (zpos, (1 - inner) * (zpos + 1 - zpos // 3 * 2) + inner * (zpos - 1), (1 - inner) * ((zpos + 2) % 4) + inner * (zpos + 1),
           (1 - inner) * (3 - zpos) + inner * ((zpos + 2) % 4))
@@ -106,7 +105,7 @@
 
         def own_along(self):
             for i in (1, 2, 3):
-                self.send(slot, device(zs[i], ypos, xpos, core))
+                self.send(slot, device(zn[i], ypos, xpos, core))
 
         def own_across(self):
             self.send(slot, three)
@@ -115,18 +114,18 @@
         def event(self, n):
             i = (n + 1) // 2
             if n % 2:
-                which = chip_slot(zs[i], ypos, xpos)
+                which = chip_slot(zn[i], ypos, xpos)
                 self.wait(which)
                 self.send(which, three)
                 self.send(which, two)
             else:
-                which = chip_slot(zs[i], y_two, x_two)
+                which = chip_slot(zn[i], y_two, x_two)
                 self.wait(which)
                 self.send(which, three)
 
         def last(self, diagonal):
             for i in range(4):
-                self.wait(chip_slot(zs[i], 1 - ypos, 1 - xpos) if diagonal else chip_slot(zs[i], y_three, x_three))
+                self.wait(chip_slot(zn[i], 1 - ypos, 1 - xpos) if diagonal else chip_slot(zn[i], y_three, x_three))
 
     edge = d.chunk
     l_parts = (
@@ -145,11 +144,11 @@
         i = (n + 1) // 2
         for g in l_gathers:
             g.event(n)
-        l_swap(chip_slot(zs[i], ypos, xpos) if n % 2 else chip_slot(zs[i], y_two, x_two), core).start()
+        l_swap(chip_slot(zn[i], ypos, xpos) if n % 2 else chip_slot(zn[i], y_two, x_two), core).start()
 
     def l_last(diagonal):
         for i in range(4):
-            which = chip_slot(zs[i], 1 - ypos, 1 - xpos) if diagonal else chip_slot(zs[i], y_three, x_three)
+            which = chip_slot(zn[i], 1 - ypos, 1 - xpos) if diagonal else chip_slot(zn[i], y_three, x_three)
             for g in l_gathers:
                 g.wait(which)
             l_swap(which, core).start()
@@ -167,7 +166,7 @@
     def l_along():
         for i in (1, 2, 3):
             for g in l_gathers:
-                g.send(slot, device(zs[i], ypos, xpos, core))
+                g.send(slot, device(zn[i], ypos, xpos, core))
 
     def u_block(p):
         return lambda s: uv.at[p // QUARTERS, pl.ds(p % QUARTERS * 2, 2), pl.ds(pl.multiple_of(s * d.slab, d.slab), d.slab), :]
@@ -262,10 +261,10 @@
                              pl.ds(pl.multiple_of((1 - core + h) % 2 * d.half, d.half), d.half)]
             remote(theirs, lv.at[ch, slot, core, :, :, pl.ds(h * d.half, d.half)], d2d_sem.at[ch, h], d2d_recv.at[ch, h], partner).start()
     for n in range(1, CHIPS):
-        chip = (me // 2 + n) % CHIPS
-        to = chip_slot(chip // 4, chip // 2 % 2, chip % 2)
-        remote(right_rows(to), rv.at[slot, core], rw_send.at[0], rw_recv.at[0], chip * 2 + core).start()
-        remote(wv.at[slot, core], wv.at[slot, core], rw_send.at[1], rw_recv.at[1], chip * 2 + core).start()
+        z, y, x = zn[n // 4], ypos + n % 4 // 2 * (1 - 2 * ypos), xpos + n % 2 * (1 - 2 * xpos)
+        to = device(z, y, x, core)
+        remote(right_rows(chip_slot(z, y, x)), rv.at[slot, core], rw_send.at[0], rw_recv.at[0], to).start()
+        remote(wv.at[slot, core], wv.at[slot, core], rw_send.at[1], rw_recv.at[1], to).start()
 
     for ch in range(CHUNKS):
         for h in range(2):
@@ -318,6 +317,11 @@
         return carry
 
     lax.fori_loop(0, d.pair // 4, start_vector, 0)
+    l_event(0)
+    l_event(1)
+    lax.fori_loop(d.pair // 4, d.pair // 2, start_vector, 0)
+    l_event(3)
+    l_event(2)
     fifteen = rv.at[pl.ds(0, CHIPS - 1), 0]
     fifteen_w = wv.at[pl.ds(0, CHIPS - 1), 0]
     remote(fifteen, fifteen, rw_send.at[0], rw_recv.at[0], me).wait()
@@ -326,11 +330,6 @@
     fw_pair = remote(wv.at[:, core], wv.at[:, core], fw_send.at[1], fw_recv.at[1], partner)
     fw_right.start()
     fw_pair.start()
-    l_event(0)
-    l_event(1)
-    lax.fori_loop(d.pair // 4, d.pair // 2, start_vector, 0)
-    l_event(2)
-    l_event(3)
     fw_right.wait()
     fw_pair.wait()
     lane = lax.broadcasted_iota(jnp.int32, (d.sub, d.prod), 1)
@@ -383,7 +382,7 @@
 
         @pl.when(grp == 1)
         def _():
-            l_event(4)
+            l_event(5)
         return carry
 
     def first_group(n, carry):
@@ -496,7 +495,7 @@
         @pl.when(j == 0)
         def _():
             lax.fori_loop(0, GROUPS, first_right, 0)
-            l_event(5)
+            l_event(4)
             lax.fori_loop(0, GROUPS, first_group, 0)
 
         @pl.when(j > 0)

time: 449 us -> 467 us (1.040)
  Pallas kernels: 442 us -> 460 us
    pallas_call x1, Pallas kernels: 442 us -> 460 us  [device_body(): pl.pallas_call(functools.partial(lanczos_kernel, d), out_shape=(jax.Shape...]
where the time goes in v13:
time: 467 us
  Pallas kernels  460 us (99%)
    pallas_call x1, Pallas kernels, device_body(): pl.pallas_call(functools.partial(lanczos_kernel, d), out_shape=(jax.Shape...  460 us

profile of v13, /device:TPU:15, one launch (start us, length us, event | category | flops | bytes accessed | tf_op | source)
XLA Modules:
  0.0 466.6 jit_solution(13025434007221939609)
XLA Ops:
  0.6 460.3 %lanczos.1 = (f32[6,256,512]{2,1,0:T(8,128)}, f32[256,512]{1,0:T(8,128)}, f32[6]{0:T(128)}, f32[6]{0:T(128)}) custom-call(f32[8192,512]{1,0:T(8,128)} %bitcast.3, bf16[2,512,512]{2,1,0:T(8,128)(2,1)} %left.1, bf16[2,512,512]{2,1,0:T(8,128)(2,1)} %right.1, bf16[2,16,16]{2,1,0:T(8,128)(2,1)} %pair_ops.1, s32[2]{0:T(128)} %flags.1), custom_call_target="tpu_custom_call" | custom-call | tf_op jit(solution)/shard_map/lanczos/pallas_call | solution.py:603
  461.0 0.0 copy-start.1
  461.0 0.0 copy-start
  461.0 4.5 pad_maximum_fusion
  465.5 0.0 copy-done.1
  465.5 0.5 copy.10
  466.0 0.0 copy-done
  466.0 0.5 copy.11
Async XLA Ops:
  461.0 4.6 copy-start.1
  461.0 5.1 %copy-start = (f32[6]{0:T(128)S(1)}, f32[6]{0:T(128)}, u32[]{:S(2)}) copy-start(f32[6]{0:T(128)} %get-tuple-element.16) | copy-start | bytes 76

commit v14 on v13

--- a/solution.py
+++ b/solution.py
@@ -261,10 +261,10 @@
                              pl.ds(pl.multiple_of((1 - core + h) % 2 * d.half, d.half), d.half)]
             remote(theirs, lv.at[ch, slot, core, :, :, pl.ds(h * d.half, d.half)], d2d_sem.at[ch, h], d2d_recv.at[ch, h], partner).start()
     for n in range(1, CHIPS):
-        z, y, x = zn[n // 4], ypos + n % 4 // 2 * (1 - 2 * ypos), xpos + n % 2 * (1 - 2 * xpos)
-        to = device(z, y, x, core)
-        remote(right_rows(chip_slot(z, y, x)), rv.at[slot, core], rw_send.at[0], rw_recv.at[0], to).start()
-        remote(wv.at[slot, core], wv.at[slot, core], rw_send.at[1], rw_recv.at[1], to).start()
+        chip = (me // 2 + n) % CHIPS
+        to = chip_slot(chip // 4, chip // 2 % 2, chip % 2)
+        remote(right_rows(to), rv.at[slot, core], rw_send.at[0], rw_recv.at[0], chip * 2 + core).start()
+        remote(wv.at[slot, core], wv.at[slot, core], rw_send.at[1], rw_recv.at[1], chip * 2 + core).start()
 
     for ch in range(CHUNKS):
         for h in range(2):
@@ -317,11 +317,6 @@
         return carry
 
     lax.fori_loop(0, d.pair // 4, start_vector, 0)
-    l_event(0)
-    l_event(1)
-    lax.fori_loop(d.pair // 4, d.pair // 2, start_vector, 0)
-    l_event(3)
-    l_event(2)
     fifteen = rv.at[pl.ds(0, CHIPS - 1), 0]
     fifteen_w = wv.at[pl.ds(0, CHIPS - 1), 0]
     remote(fifteen, fifteen, rw_send.at[0], rw_recv.at[0], me).wait()
@@ -330,6 +325,11 @@
     fw_pair = remote(wv.at[:, core], wv.at[:, core], fw_send.at[1], fw_recv.at[1], partner)
     fw_right.start()
     fw_pair.start()
+    l_event(0)
+    l_event(1)
+    lax.fori_loop(d.pair // 4, d.pair // 2, start_vector, 0)
+    l_event(3)
+    l_event(2)
     fw_right.wait()
     fw_pair.wait()
     lane = lax.broadcasted_iota(jnp.int32, (d.sub, d.prod), 1)

time: 467 us -> 467 us (level)
  no operation moved by 1% of the time
where the time goes in v14:
time: 467 us
  Pallas kernels  461 us (99%)
    pallas_call x1, Pallas kernels, device_body(): pl.pallas_call(functools.partial(lanczos_kernel, d), out_shape=(jax.Shape...  461 us

profile of v14, /device:TPU:15, one launch (start us, length us, event | category | flops | bytes accessed | tf_op | source)
XLA Modules:
  0.0 466.8 jit_solution(14156845179525632786)
XLA Ops:
  0.6 460.6 %lanczos.1 = (f32[6,256,512]{2,1,0:T(8,128)}, f32[256,512]{1,0:T(8,128)}, f32[6]{0:T(128)}, f32[6]{0:T(128)}) custom-call(f32[8192,512]{1,0:T(8,128)} %bitcast.3, bf16[2,512,512]{2,1,0:T(8,128)(2,1)} %left.1, bf16[2,512,512]{2,1,0:T(8,128)(2,1)} %right.1, bf16[2,16,16]{2,1,0:T(8,128)(2,1)} %pair_ops.1, s32[2]{0:T(128)} %flags.1), custom_call_target="tpu_custom_call" | custom-call | tf_op jit(solution)/shard_map/lanczos/pallas_call | solution.py:603
  461.2 0.0 copy-start.1
  461.3 0.0 copy-start
  461.3 4.5 pad_maximum_fusion
  465.8 0.0 copy-done.1
  465.8 0.5 copy.10
  466.3 0.0 copy-done
  466.3 0.5 copy.11
Async XLA Ops:
  461.2 4.6 copy-start.1
  461.3 5.1 %copy-start = (f32[6]{0:T(128)S(1)}, f32[6]{0:T(128)}, u32[]{:S(2)}) copy-start(f32[6]{0:T(128)} %get-tuple-element.16) | copy-start | bytes 76

commit v15 on v12

--- a/solution.py
+++ b/solution.py
@@ -40,7 +40,7 @@
     (),
     (),
 )
-RESULT_EARLY = 9
+RESULT_EARLY = 5
 
 
 class Dims:

time: 449 us -> 475 us (1.058)
  Pallas kernels: 442 us -> 468 us
    pallas_call x1, Pallas kernels: 442 us -> 468 us  [device_body(): pl.pallas_call(functools.partial(lanczos_kernel, d), out_shape=(jax.Shape...]
where the time goes in v15:
time: 475 us
  Pallas kernels  468 us (99%)
    pallas_call x1, Pallas kernels, device_body(): pl.pallas_call(functools.partial(lanczos_kernel, d), out_shape=(jax.Shape...  468 us

profile of v15, /device:TPU:15, one launch (start us, length us, event | category | flops | bytes accessed | tf_op | source)
XLA Modules:
  0.0 474.7 jit_solution(4625165889486274961)
XLA Ops:
  0.6 468.5 %lanczos.1 = (f32[6,256,512]{2,1,0:T(8,128)}, f32[256,512]{1,0:T(8,128)}, f32[6]{0:T(128)}, f32[6]{0:T(128)}) custom-call(f32[8192,512]{1,0:T(8,128)} %bitcast.3, bf16[2,512,512]{2,1,0:T(8,128)(2,1)} %left.1, bf16[2,512,512]{2,1,0:T(8,128)(2,1)} %right.1, bf16[2,16,16]{2,1,0:T(8,128)(2,1)} %pair_ops.1, s32[2]{0:T(128)} %flags.1), custom_call_target="tpu_custom_call" | custom-call | tf_op jit(solution)/shard_map/lanczos/pallas_call | solution.py:604
  469.1 0.0 copy-start.1
  469.1 0.0 copy-start
  469.1 4.5 pad_maximum_fusion
  473.7 0.0 copy-done.1
  473.7 0.5 copy.10
  474.2 0.0 copy-done
  474.2 0.5 copy.11
Async XLA Ops:
  469.1 4.6 copy-start.1
  469.1 5.1 %copy-start = (f32[6]{0:T(128)S(1)}, f32[6]{0:T(128)}, u32[]{:S(2)}) copy-start(f32[6]{0:T(128)} %get-tuple-element.16) | copy-start | bytes 76

commit v16 on v15

--- a/solution.py
+++ b/solution.py
@@ -40,7 +40,7 @@
     (),
     (),
 )
-RESULT_EARLY = 5
+RESULT_EARLY = 12
 
 
 class Dims:

time: 475 us -> 446 us (0.939)
  Pallas kernels: 468 us -> 440 us
    pallas_call x1, Pallas kernels: 468 us -> 440 us  [device_body(): pl.pallas_call(functools.partial(lanczos_kernel, d), out_shape=(jax.Shape...]
where the time goes in v16:
time: 446 us
  Pallas kernels  440 us (99%)
  other arithmetic  4.53 us (1%)
    pallas_call x1, Pallas kernels, device_body(): pl.pallas_call(functools.partial(lanczos_kernel, d), out_shape=(jax.Shape...  440 us

profile of v16, /device:TPU:15, one launch (start us, length us, event | category | flops | bytes accessed | tf_op | source)
XLA Modules:
  0.0 446.2 jit_solution(17475163334682158736)
XLA Ops:
  0.6 439.9 %lanczos.1 = (f32[6,256,512]{2,1,0:T(8,128)}, f32[256,512]{1,0:T(8,128)}, f32[6]{0:T(128)}, f32[6]{0:T(128)}) custom-call(f32[8192,512]{1,0:T(8,128)} %bitcast.3, bf16[2,512,512]{2,1,0:T(8,128)(2,1)} %left.1, bf16[2,512,512]{2,1,0:T(8,128)(2,1)} %right.1, bf16[2,16,16]{2,1,0:T(8,128)(2,1)} %pair_ops.1, s32[2]{0:T(128)} %flags.1), custom_call_target="tpu_custom_call" | custom-call | tf_op jit(solution)/shard_map/lanczos/pallas_call | solution.py:604
  440.6 0.0 copy-start.1
  440.6 0.0 copy-start
  440.6 4.5 %pad_maximum_fusion = f32[7,16,16,512]{3,2,1,0:T(8,128)} fusion(f32[6,16,16,512]{3,2,1,0:T(8,128)} %bitcast.4, f32[1,16,16,512]{3,2,1,0:T(8,128)} %bitcast.5), kind=kLoop, calls=%fused_computation | loop fusion | flops 917504 | bytes 7340032 | tf_op jit(solution)/shard_map/concatenate | solution.py:636
  445.1 0.0 copy-done.1
  445.1 0.5 copy.10
  445.6 0.0 copy-done
  445.6 0.5 copy.11
Async XLA Ops:
  440.6 4.6 %copy-start.1 = (f32[6]{0:T(128)S(1)}, f32[6]{0:T(128)}, u32[]{:S(2)}) copy-start(f32[6]{0:T(128)} %get-tuple-element.15) | copy-start | bytes 76
  440.6 5.1 %copy-start = (f32[6]{0:T(128)S(1)}, f32[6]{0:T(128)}, u32[]{:S(2)}) copy-start(f32[6]{0:T(128)} %get-tuple-element.16) | copy-start | bytes 76

commit v17 on v16

--- a/solution.py
+++ b/solution.py
@@ -233,10 +233,12 @@
     for copy in first_copies:
         copy.start()
 
-    spread = (lax.broadcasted_iota(jnp.int32, (d.pair, d.prod), 1) // d.sub == lax.broadcasted_iota(jnp.int32, (d.pair, d.prod), 0))
-    spread = spread.astype(jnp.float32).astype(jnp.bfloat16)
+    side_by_side = jnp.zeros((d.pair, 128), jnp.float32)
     for t in range(d.terms_dev):
-        wv[slot, core, t] = jnp.dot(pair_ops[t], spread, preferred_element_type=jnp.float32).astype(jnp.bfloat16)
+        place_of = lax.broadcasted_iota(jnp.int32, (d.pair, 128), 1) == lax.broadcasted_iota(jnp.int32, (d.pair, 128), 0) + t * d.pair
+        place_of = jnp.where(place_of, 1.0, 0.0).astype(jnp.bfloat16)
+        side_by_side += jnp.dot(pair_ops[t], place_of, preferred_element_type=jnp.float32)
+    wv[slot, core] = side_by_side.astype(jnp.bfloat16)
     all_right.wait()
     some_rows = d.bond // 8
 
@@ -337,10 +339,16 @@
     row = lax.broadcasted_iota(jnp.int32, (d.sub, d.prod), 0)
     diagonal = lane % d.sub == row
 
+    for t in range(d.terms_dev):
+        at_row = lax.broadcasted_iota(jnp.int32, (128, d.prod), 0)
+        wide = jnp.where(at_row == lax.broadcasted_iota(jnp.int32, (128, d.prod), 1) // d.sub + t * d.pair, 1.0, 0.0).astype(jnp.bfloat16)
+        spread = jnp.dot(wv[...].reshape(CHIPS * CORES * d.pair, 128), wide, preferred_element_type=jnp.float32)
+        zst[:, t * d.prod:(t + 1) * d.prod] = spread.astype(jnp.bfloat16)
+
     def spread_pair(s, carry):
         for c in range(2):
             for t in range(d.terms_dev):
-                w = wv[s, c, t].astype(jnp.float32)
+                w = zst[pl.ds(pl.multiple_of((s * CORES + c) * d.pair, d.pair), d.pair), t * d.prod:(t + 1) * d.prod].astype(jnp.float32)
                 for q in range(d.pair):
                     full = jnp.where(diagonal, jnp.broadcast_to(w[q:q + 1, :], (d.sub, d.prod)), 0.0)
                     kw[s, c, t, q * d.sub:(q + 1) * d.sub, :] = full.astype(jnp.bfloat16)
@@ -611,7 +619,7 @@
                 pltpu.VMEM((CHUNKS, CHIPS, CORES, d.terms_dev, d.chunk, bond), bf16),
                 pltpu.VMEM((CHIPS, CORES, d.terms_dev, d.slab, bond), bf16),
                 pltpu.VMEM((d.terms_dev, bond, bond), bf16),
-                pltpu.VMEM((CHIPS, CORES, d.terms_dev, pair, d.prod), bf16),
+                pltpu.VMEM((CHIPS, CORES, pair, 128), bf16),
                 pltpu.VMEM((CHIPS, CORES, d.terms_dev, d.prod, d.prod), bf16),
                 pltpu.VMEM((CHUNKS, pair // 2, bond, 2 * d.chunk), bf16),
                 pltpu.VMEM((d.lane_tiles, d.half * pair, d.lane), f32),

time: 446 us -> 440 us (0.987)
  Pallas kernels: 440 us -> 434 us
    pallas_call x1, Pallas kernels: 440 us -> 434 us  [device_body(): pl.pallas_call(functools.partial(lanczos_kernel, d), out_shape=(jax.Shape...]
where the time goes in v17:
time: 440 us
  Pallas kernels  434 us (99%)
  other arithmetic  4.53 us (1%)
    pallas_call x1, Pallas kernels, device_body(): pl.pallas_call(functools.partial(lanczos_kernel, d), out_shape=(jax.Shape...  434 us

profile of v17, /device:TPU:15, one launch (start us, length us, event | category | flops | bytes accessed | tf_op | source)
XLA Modules:
  0.0 440.0 jit_solution(5348667377982074850)
XLA Ops:
  0.6 433.8 %lanczos.1 = (f32[6,256,512]{2,1,0:T(8,128)}, f32[256,512]{1,0:T(8,128)}, f32[6]{0:T(128)}, f32[6]{0:T(128)}) custom-call(f32[8192,512]{1,0:T(8,128)} %bitcast.3, bf16[2,512,512]{2,1,0:T(8,128)(2,1)} %left.1, bf16[2,512,512]{2,1,0:T(8,128)(2,1)} %right.1, bf16[2,16,16]{2,1,0:T(8,128)(2,1)} %pair_ops.1, s32[2]{0:T(128)} %flags.1), custom_call_target="tpu_custom_call" | custom-call | tf_op jit(solution)/shard_map/lanczos/pallas_call | solution.py:612
  434.4 0.0 copy-start.1
  434.5 0.0 copy-start
  434.5 4.5 %pad_maximum_fusion = f32[7,16,16,512]{3,2,1,0:T(8,128)} fusion(f32[6,16,16,512]{3,2,1,0:T(8,128)} %bitcast.4, f32[1,16,16,512]{3,2,1,0:T(8,128)} %bitcast.5), kind=kLoop, calls=%fused_computation | loop fusion | flops 917504 | bytes 7340032 | tf_op jit(solution)/shard_map/concatenate | solution.py:644
  439.0 0.0 copy-done.1
  439.0 0.5 copy.10
  439.5 0.0 copy-done
  439.5 0.5 copy.11
Async XLA Ops:
  434.4 4.6 %copy-start.1 = (f32[6]{0:T(128)S(1)}, f32[6]{0:T(128)}, u32[]{:S(2)}) copy-start(f32[6]{0:T(128)} %get-tuple-element.15) | copy-start | bytes 76
  434.5 5.1 %copy-start = (f32[6]{0:T(128)S(1)}, f32[6]{0:T(128)}, u32[]{:S(2)}) copy-start(f32[6]{0:T(128)} %get-tuple-element.16) | copy-start | bytes 76

commit v18 on v17

--- a/solution.py
+++ b/solution.py
@@ -35,10 +35,6 @@
     ((3, 3, 7), (5, 0, 5),),
     ((4, 0, 6), (5, 0, 6),),
     ((4, 0, 7), (5, 0, 7), (7, 0, 0),),
-    (),
-    (),
-    (),
-    (),
 )
 RESULT_EARLY = 12
 
@@ -343,12 +339,12 @@
         at_row = lax.broadcasted_iota(jnp.int32, (128, d.prod), 0)
         wide = jnp.where(at_row == lax.broadcasted_iota(jnp.int32, (128, d.prod), 1) // d.sub + t * d.pair, 1.0, 0.0).astype(jnp.bfloat16)
         spread = jnp.dot(wv[...].reshape(CHIPS * CORES * d.pair, 128), wide, preferred_element_type=jnp.float32)
-        zst[:, t * d.prod:(t + 1) * d.prod] = spread.astype(jnp.bfloat16)
+        zst[0, :, t * d.prod:(t + 1) * d.prod] = spread.astype(jnp.bfloat16)
 
     def spread_pair(s, carry):
         for c in range(2):
             for t in range(d.terms_dev):
-                w = zst[pl.ds(pl.multiple_of((s * CORES + c) * d.pair, d.pair), d.pair), t * d.prod:(t + 1) * d.prod].astype(jnp.float32)
+                w = zst[0, pl.ds(pl.multiple_of((s * CORES + c) * d.pair, d.pair), d.pair), t * d.prod:(t + 1) * d.prod].astype(jnp.float32)
                 for q in range(d.pair):
                     full = jnp.where(diagonal, jnp.broadcast_to(w[q:q + 1, :], (d.sub, d.prod)), 0.0)
                     kw[s, c, t, q * d.sub:(q + 1) * d.sub, :] = full.astype(jnp.bfloat16)
@@ -377,14 +373,31 @@
         for qb in range(d.pair // 2):
             right_product(grp, ch, qb, to)
 
-    def left_products(ch, grp, at=None):
+    def pair_products(grp, at, side):
         for k in range(d.group_terms):
             w = kw[grp * 4 + k // 4, k // 2 % 2, k % 2]
-            z = jnp.dot(w, yst[(grp if at is None else at) * d.group_terms + k].reshape(d.prod, 2 * d.chunk), preferred_element_type=jnp.float32).astype(jnp.bfloat16)
+            z = jnp.dot(w, yst[at * d.group_terms + k].reshape(d.prod, 2 * d.chunk), preferred_element_type=jnp.float32).astype(jnp.bfloat16)
             for bh in range(2):
-                zst[bh * d.prod:(bh + 1) * d.prod, k * d.chunk:(k + 1) * d.chunk] = z[:, bh * d.chunk:(bh + 1) * d.chunk]
+                zst[side, bh * d.prod:(bh + 1) * d.prod, k * d.chunk:(k + 1) * d.chunk] = z[:, bh * d.chunk:(bh + 1) * d.chunk]
+
+    def sum_left(ch, grp, side):
         l_all = lv[ch, pl.ds(grp * 4, 4)].reshape(d.group_terms * d.chunk, d.bond)
-        sig[...] += jnp.dot(zst[...], l_all, preferred_element_type=jnp.float32)
+        sig[...] += jnp.dot(zst[side], l_all, preferred_element_type=jnp.float32)
+
+    def left_products(ch, grp, at=None):
+        pair_products(grp, grp if at is None else at, 0)
+        sum_left(ch, grp, 0)
+
+    def last_products():
+        pair_products(0, 0, 0)
+
+        def both(grp, carry):
+            sum_left(CHUNKS - 1, grp - 1, (grp - 1) % 2)
+            pair_products(grp, grp, grp % 2)
+            return carry
+
+        lax.fori_loop(1, GROUPS, both, 0)
+        sum_left(CHUNKS - 1, GROUPS - 1, (GROUPS - 1) % 2)
 
     def first_right(grp, carry):
         right_of_group(grp, 0, grp)
@@ -483,7 +496,7 @@
             for four in range(0, len(SLOTS), 4):
                 @pl.when((t >= four) & (t < four + 4))
                 def _():
-                    for at in range(four, four + 4):
+                    for at in range(four, min(four + 4, len(SLOTS))):
                         if not SLOTS[at]:
                             continue
 
@@ -496,9 +509,10 @@
             def _():
                 right_of_piece(done_right // QUARTERS, done_right % QUARTERS)
 
-            @pl.when(is_right == 0)
+            @pl.when((is_right == 0) & (done_left < GROUPS))
             def _():
-                left_products(done_left // GROUPS, done_left % GROUPS)
+                left_products(0, done_left)
+
             return carry
 
         @pl.when(j == 0)
@@ -510,6 +524,7 @@
         @pl.when(j > 0)
         def _():
             lax.fori_loop(0, len(SLOTS), slot_step, 0)
+            last_products()
             for p in range(PIECES):
                 sent = uv.at[p // QUARTERS, pl.ds(0, 2), pl.ds(0, 15 * d.slab), :]
                 remote(sent, sent, u_send.at[p], u_recv.at[p, 0], me).wait_send()
@@ -598,6 +613,16 @@
     for j in range(LANCZOS_STEPS):
         for c in range(d.bond // d.wide):
             pltpu.make_async_copy(tbuf.at[j, c], out.at[j, :, pl.ds(c * d.wide, d.wide)], o_sem.at[j, c]).wait()
+
+
+def join_kernel(first, later, out):
+    @pl.when(pl.program_id(0) == 0)
+    def _():
+        out[0] = first[...]
+
+    @pl.when(pl.program_id(0) > 0)
+    def _():
+        out[...] = later[...]
 
 
 def solution(mesh):
@@ -624,7 +649,7 @@
                 pltpu.VMEM((CHUNKS, pair // 2, bond, 2 * d.chunk), bf16),
                 pltpu.VMEM((d.lane_tiles, d.half * pair, d.lane), f32),
                 pltpu.VMEM((CHIPS * CORES * d.terms_dev, pair, d.sub, 2 * d.chunk), bf16),
-                pltpu.VMEM((d.rows, d.group_terms * d.chunk), bf16),
+                pltpu.VMEM((2, d.rows, d.group_terms * d.chunk), bf16),
                 pltpu.VMEM((d.rows, bond), f32),
                 pltpu.VMEM((d.rows, d.half), f32),
                 pltpu.VMEM((d.rows, d.half), f32),
@@ -641,7 +666,16 @@
             compiler_params=pltpu.CompilerParams(has_side_effects=True, collective_id=0, vmem_limit_bytes=67043328),
             name='lanczos',
         )(wavefunction.reshape(bond * pair, bond), left_loc, right_loc, pair_loc, flag_loc)
-        krylov = jnp.concatenate([first[None], later])
+        block = (1, d.out_rows * pair, bond)
+        krylov = pl.pallas_call(
+            join_kernel,
+            out_shape=jax.ShapeDtypeStruct((LANCZOS_STEPS + 1,) + block[1:], f32),
+            grid=(LANCZOS_STEPS + 1,),
+            in_specs=[pl.BlockSpec(block[1:], lambda i: (0, 0)), pl.BlockSpec(block, lambda i: (jnp.maximum(i - 1, 0), 0, 0))],
+            out_specs=pl.BlockSpec(block, lambda i: (i, 0, 0)),
+            compiler_params=pltpu.CompilerParams(vmem_limit_bytes=8 * 1024 * 1024),
+            name='join',
+        )(first, later)
         return krylov.reshape(LANCZOS_STEPS + 1, d.out_rows, pair, bond), alphas, betas
 
     return jax.shard_map(device_body, mesh=mesh, in_specs=(P(), P(AXIS_NAME), P(AXIS_NAME), P(AXIS_NAME), P(AXIS_NAME)),

time: 440 us -> 442 us (level)
  other arithmetic: 4.53 us -> 0 us
    concatenate x1 -> x0, other arithmetic: 4.53 us -> none  [device_body(): krylov = jnp.concatenate([first[None], later])]
where the time goes in v18:
time: 442 us
  Pallas kernels  437 us (99%)
    pallas_call x1, Pallas kernels, device_body(): pl.pallas_call(functools.partial(lanczos_kernel, d), out_shape=(jax.Shape...  434 us

profile of v18, /device:TPU:15, one launch (start us, length us, event | category | flops | bytes accessed | tf_op | source)
XLA Modules:
  0.0 441.8 jit_solution(3876753292748326583)
XLA Ops:
  0.6 433.8 %lanczos.1 = (f32[6,256,512]{2,1,0:T(8,128)}, f32[256,512]{1,0:T(8,128)}, f32[6]{0:T(128)}, f32[6]{0:T(128)}) custom-call(f32[8192,512]{1,0:T(8,128)} %bitcast.2, bf16[2,512,512]{2,1,0:T(8,128)(2,1)} %left.1, bf16[2,512,512]{2,1,0:T(8,128)(2,1)} %right.1, bf16[2,16,16]{2,1,0:T(8,128)(2,1)} %pair_ops.1, s32[2]{0:T(128)} %flags.1), custom_call_target="tpu_custom_call" | custom-call | tf_op jit(solution)/shard_map/lanczos/pallas_call | solution.py:637
  434.5 0.0 copy-start
  434.5 1.9 copy-done
  436.4 0.0 copy-start.1
  436.4 1.0 copy-done.1
  437.4 0.0 copy-start.3
  437.4 0.0 copy-start.2
  437.4 3.3 join.1
  440.7 0.0 copy-done.3
  440.7 0.5 copy.10
  441.2 0.0 copy-done.2
  441.2 0.5 copy.11
Async XLA Ops:
  434.5 1.9 copy-start
  436.4 1.0 copy-start.1
  437.4 3.3 copy-start.3
  437.4 3.8 copy-start.2

commit v19 on v17

--- a/solution.py
+++ b/solution.py
@@ -31,16 +31,16 @@
     ((2, 3, 5), (3, 2, 5), (2, 3, 6),),
     ((2, 2, 7), (3, 3, 4), (2, 1, 7), (3, 1, 5), (8, 0, 0),),
     ((3, 3, 5), (2, 3, 7), (3, 2, 6), (3, 1, 6), (3, 3, 6),),
-    ((3, 0, 7), (3, 1, 7), (3, 2, 7), (4, 0, 5), (5, 0, 4), (4, 0, 4),),
+    ((3, 0, 7), (3, 1, 7), (3, 2, 7), (4, 0, 5), (5, 0, 4), (4, 0, 4), (7, 0, 0),),
     ((3, 3, 7), (5, 0, 5),),
     ((4, 0, 6), (5, 0, 6),),
-    ((4, 0, 7), (5, 0, 7), (7, 0, 0),),
+    ((4, 0, 7), (5, 0, 7), (7, 1, 0),),
     (),
     (),
     (),
     (),
 )
-RESULT_EARLY = 12
+RESULT_PARTS = ((0, 4), (4, 12), (12, 16))
 
 
 class Dims:
@@ -196,7 +196,7 @@
         elif kind == RESULT:
             turn_result(j - 1, vcur)
         elif kind == RESULT_OUT:
-            hand_out(j - 1, 0, RESULT_EARLY)
+            hand_out(j - 1, *RESULT_PARTS[i])
         elif kind == RESULT_PUT:
             @pl.when(j > 1)
             def _():
@@ -544,7 +544,7 @@
 
         @pl.when(j > 0)
         def _():
-            hand_out(j - 1, RESULT_EARLY, CHIPS)
+            hand_out(j - 1, *RESULT_PARTS[2])
 
         @pl.when(j == LANCZOS_STEPS - 1)
         def _():

time: 440 us -> 451 us (1.025)
  Pallas kernels: 434 us -> 445 us
    pallas_call x1, Pallas kernels: 434 us -> 445 us  [device_body(): pl.pallas_call(functools.partial(lanczos_kernel, d), out_shape=(jax.Shape...]
where the time goes in v19:
time: 451 us
  Pallas kernels  445 us (99%)
  other arithmetic  4.53 us (1%)
    pallas_call x1, Pallas kernels, device_body(): pl.pallas_call(functools.partial(lanczos_kernel, d), out_shape=(jax.Shape...  445 us

profile of v19, /device:TPU:15, one launch (start us, length us, event | category | flops | bytes accessed | tf_op | source)
XLA Modules:
  0.0 450.9 jit_solution(3412331195666686256)
XLA Ops:
  0.6 444.7 %lanczos.1 = (f32[6,256,512]{2,1,0:T(8,128)}, f32[256,512]{1,0:T(8,128)}, f32[6]{0:T(128)}, f32[6]{0:T(128)}) custom-call(f32[8192,512]{1,0:T(8,128)} %bitcast.3, bf16[2,512,512]{2,1,0:T(8,128)(2,1)} %left.1, bf16[2,512,512]{2,1,0:T(8,128)(2,1)} %right.1, bf16[2,16,16]{2,1,0:T(8,128)(2,1)} %pair_ops.1, s32[2]{0:T(128)} %flags.1), custom_call_target="tpu_custom_call" | custom-call | tf_op jit(solution)/shard_map/lanczos/pallas_call | solution.py:612
  445.3 0.0 copy-start.1
  445.3 0.0 copy-start
  445.3 4.5 %pad_maximum_fusion = f32[7,16,16,512]{3,2,1,0:T(8,128)} fusion(f32[6,16,16,512]{3,2,1,0:T(8,128)} %bitcast.4, f32[1,16,16,512]{3,2,1,0:T(8,128)} %bitcast.5), kind=kLoop, calls=%fused_computation | loop fusion | flops 917504 | bytes 7340032 | tf_op jit(solution)/shard_map/concatenate | solution.py:644
  449.8 0.0 copy-done.1
  449.8 0.5 copy.10
  450.4 0.0 copy-done
  450.4 0.5 copy.11
Async XLA Ops:
  445.3 4.6 %copy-start.1 = (f32[6]{0:T(128)S(1)}, f32[6]{0:T(128)}, u32[]{:S(2)}) copy-start(f32[6]{0:T(128)} %get-tuple-element.15) | copy-start | bytes 76
  445.3 5.1 %copy-start = (f32[6]{0:T(128)S(1)}, f32[6]{0:T(128)}, u32[]{:S(2)}) copy-start(f32[6]{0:T(128)} %get-tuple-element.16) | copy-start | bytes 76

commit v20 on v17

--- a/solution.py
+++ b/solution.py
@@ -34,8 +34,8 @@
     ((3, 0, 7), (3, 1, 7), (3, 2, 7), (4, 0, 5), (5, 0, 4), (4, 0, 4),),
     ((3, 3, 7), (5, 0, 5),),
     ((4, 0, 6), (5, 0, 6),),
-    ((4, 0, 7), (5, 0, 7), (7, 0, 0),),
-    (),
+    ((4, 0, 7), (5, 0, 7),),
+    ((7, 0, 0),),
     (),
     (),
     (),

time: 440 us -> 437 us (level)
  no operation moved by 1% of the time
where the time goes in v20:
time: 437 us
  Pallas kernels  431 us (99%)
  other arithmetic  4.53 us (1%)
    pallas_call x1, Pallas kernels, device_body(): pl.pallas_call(functools.partial(lanczos_kernel, d), out_shape=(jax.Shape...  431 us

profile of v20, /device:TPU:15, one launch (start us, length us, event | category | flops | bytes accessed | tf_op | source)
XLA Modules:
  0.0 437.0 jit_solution(7956321473548529865)
XLA Ops:
  0.6 430.8 %lanczos.1 = (f32[6,256,512]{2,1,0:T(8,128)}, f32[256,512]{1,0:T(8,128)}, f32[6]{0:T(128)}, f32[6]{0:T(128)}) custom-call(f32[8192,512]{1,0:T(8,128)} %bitcast.3, bf16[2,512,512]{2,1,0:T(8,128)(2,1)} %left.1, bf16[2,512,512]{2,1,0:T(8,128)(2,1)} %right.1, bf16[2,16,16]{2,1,0:T(8,128)(2,1)} %pair_ops.1, s32[2]{0:T(128)} %flags.1), custom_call_target="tpu_custom_call" | custom-call | tf_op jit(solution)/shard_map/lanczos/pallas_call | solution.py:612
  431.4 0.0 copy-start.1
  431.4 0.0 copy-start
  431.4 4.5 %pad_maximum_fusion = f32[7,16,16,512]{3,2,1,0:T(8,128)} fusion(f32[6,16,16,512]{3,2,1,0:T(8,128)} %bitcast.4, f32[1,16,16,512]{3,2,1,0:T(8,128)} %bitcast.5), kind=kLoop, calls=%fused_computation | loop fusion | flops 917504 | bytes 7340032 | tf_op jit(solution)/shard_map/concatenate | solution.py:644
  436.0 0.0 copy-done.1
  436.0 0.5 copy.10
  436.5 0.0 copy-done
  436.5 0.5 copy.11
Async XLA Ops:
  431.4 4.6 %copy-start.1 = (f32[6]{0:T(128)S(1)}, f32[6]{0:T(128)}, u32[]{:S(2)}) copy-start(f32[6]{0:T(128)} %get-tuple-element.15) | copy-start | bytes 76
  431.4 5.1 %copy-start = (f32[6]{0:T(128)S(1)}, f32[6]{0:T(128)}, u32[]{:S(2)}) copy-start(f32[6]{0:T(128)} %get-tuple-element.16) | copy-start | bytes 76
